TPU v7x, 512 devices: a whole 4x8x8 slice. The times are simulated.
512 devices in a mesh: elem: 128 (over z, y, core), bucket: 4 (over x).
Axes of the slice: x: 4, y: 8, z: 8, core: 2. Of those that a mesh axis runs over, the one named last changes fastest.
Arguments:
- node_data: float32 [24, 1572864], P(None, 'elem'), may hold values from -6 to 6
- eroded: int32 [65536], P('elem'), may hold values from 0 to 2047, as said below
- bucket_map: int32 [1572864], P('elem'), may hold values from 0 to 1023, as said below
- seg_point: float32 [1024, 3, 512], P('elem', None, 'bucket'), may hold values from -3 to 3
- seg_angle: float32 [1024, 2, 512], P('elem', None, 'bucket'), may hold values from -3.140625 to 3.140625
Outputs:
- face_force: float32 [3, 393216], P(None, 'elem')
Inputs may be any that keep to these rules, and one draw needn't show every extreme that they name: `eroded`: the 512 entries of one index of elem are distinct local element numbers. `bucket_map`: among the faces of the elements listed in eroded, those of one index of elem name one bucket at most 5 times; in every draw some bucket is named exactly 5 times by every index of elem.
All inputs are finite; a program needn't handle non-finite values.
Results may differ from a plain program's by a relative error of at most 0.00012.
Values sent between devices are 32-bit elements; how exact they have to be, the bound alone decides.
No kernel may reach another device: no remote copies, remote signals or barrier semaphores. Data moves between devices by JAX's collectives and lax.ppermute only.
A program may use at most 64 MiB of HBM per device.

v0:
```python
import jax
import jax.numpy as jnp
from jax import lax
from jax.sharding import PartitionSpec as P

STIFFNESS = 20.0
DAMPING = 0.5


def in_one_piece(arrays, axis, dim, along):
    widths = [a.shape[along] for a in arrays]
    both = jnp.concatenate(arrays, axis=along)
    result = lax.all_gather(both, axis, axis=dim, tiled=True)
    return tuple(jnp.split(result, [sum(widths[:k]) for k in range(1, len(widths))], axis=along))


def in_one_piece_2(arrays, axis, split_dim, concat_dim, along):
    ends, at = ([], 0)
    for a in arrays[:-1]:
        at += a.shape[along]
        ends.append(at)
    both = jnp.concatenate(arrays, axis=along)
    return tuple(
        jnp.split(
            lax.all_to_all(both, axis, split_axis=split_dim, concat_axis=concat_dim, tiled=True),
            ends,
            axis=along,
        )
    )


def from_everyone(value, axis):
    copies = jnp.broadcast_to(value, (lax.axis_size(axis), *value.shape))
    return lax.all_to_all(copies, axis, split_axis=0, concat_axis=0, tiled=True)


def of_everyone(value, axis):
    return from_everyone(value, axis).sum(axis=0)


def face_geometry(payload):
    corner = payload[0:12].reshape(4, 3, -1)
    motion = payload[12:24].reshape(4, 3, -1)
    centroid = 0.25 * (corner[0] + corner[1] + corner[2] + corner[3])
    first_edge = corner[2] - corner[0]
    second_edge = corner[3] - corner[1]
    area_x = 0.5 * (first_edge[1] * second_edge[2] - first_edge[2] * second_edge[1])
    area_y = 0.5 * (first_edge[2] * second_edge[0] - first_edge[0] * second_edge[2])
    area_z = 0.5 * (first_edge[0] * second_edge[1] - first_edge[1] * second_edge[0])
    velocity = 0.25 * (motion[0] + motion[1] + motion[2] + motion[3])
    return jnp.concatenate([centroid, jnp.stack([area_x, area_y, area_z]), velocity], axis=0)


def unit_normal(angles):
    return jnp.stack(
        [
            jnp.cos(angles[:, 0]) * jnp.sin(angles[:, 1]),
            jnp.sin(angles[:, 0]) * jnp.sin(angles[:, 1]),
            jnp.cos(angles[:, 1]),
        ],
        axis=1,
    )


def penalty_terms(geometry, point, normal, stiff):
    offset = geometry[0:3, :, None] - point
    dist_sq = offset[0] * offset[0] + offset[1] * offset[1] + offset[2] * offset[2]
    gap_value = offset[0] * normal[0] + offset[1] * normal[1] + offset[2] * normal[2]
    closing = (
        geometry[6][:, None] * normal[0]
        + geometry[7][:, None] * normal[1]
        + geometry[8][:, None] * normal[2]
    )
    projected = jnp.abs(
        geometry[3][:, None] * normal[0]
        + geometry[4][:, None] * normal[1]
        + geometry[5][:, None] * normal[2]
    )
    depth_in = jnp.maximum(-gap_value, 0.0)
    weight = jnp.exp(-0.5 * dist_sq)
    return weight * depth_in * (stiff - DAMPING * closing) * projected


def local(node_data, eroded, bucket_map, seg_point, seg_angle):
    elem_count = lax.axis_size("elem")
    group_count = lax.axis_size("bucket")
    local_buckets = seg_point.shape[0]
    bucket_total = local_buckets * elem_count
    erode_count = eroded.shape[0]
    extract_count = 6 * erode_count
    slot_count = max(2, (10 * erode_count + bucket_total - 1) // bucket_total)
    sides = jnp.arange(6, dtype=jnp.int32)
    face_index = (6 * eroded[:, None] + sides[None, :]).reshape(extract_count)
    face_rows = jnp.take(node_data, face_index, axis=1)
    face_bucket = jnp.take(bucket_map, face_index)
    bucket_iota = jnp.arange(bucket_total, dtype=jnp.int32)

    def rank_block(carried, block_ids):
        onehot = (block_ids[:, None] == bucket_iota[None, :]).astype(jnp.int32)
        earlier = jnp.cumsum(onehot, axis=0) - onehot + carried[None, :]
        return (carried + jnp.sum(onehot, axis=0), jnp.sum(onehot * earlier, axis=1))

    local_counts, ranks = lax.scan(
        rank_block,
        jnp.zeros((bucket_total,), jnp.int32),
        face_bucket.reshape(extract_count // 128, 128),
    )
    ranks = ranks.reshape(extract_count)
    handled = ranks % group_count == lax.axis_index("bucket")
    slot_width = (slot_count + group_count - 1) // group_count
    width = bucket_total * slot_width
    target = face_bucket * slot_width + ranks // group_count
    send_index = jnp.where(handled, target, width)
    seg_point, seg_angle = in_one_piece((seg_point, seg_angle), "bucket", 2, 1)
    payload = face_geometry(face_rows)
    outgoing = (
        jnp.zeros((payload.shape[0], width), jnp.float32)
        .at[:, send_index]
        .set(payload, mode="drop")
    )
    present = jnp.zeros((1, width), jnp.float32).at[:, send_index].set(1.0, mode="drop")
    incoming, present_in = in_one_piece_2((outgoing, present), "elem", 1, 1, 0)
    bucket_counts = jnp.sum(present_in.reshape(elem_count, local_buckets, slot_width), axis=(0, 2))
    bucket_counts = of_everyone(bucket_counts, "bucket")
    row_count = incoming.shape[0]
    grouped = (
        incoming.reshape(row_count, elem_count, local_buckets, slot_width)
        .transpose(2, 0, 1, 3)
        .reshape(local_buckets, row_count, elem_count * slot_width)
    )
    stiffness = STIFFNESS * lax.rsqrt(jnp.maximum(bucket_counts, 1.0))
    normals = unit_normal(seg_angle)

    def bucket_force(items):
        faces_in, points, normal, stiff = items
        traction = penalty_terms(faces_in, points[:, None, :], normal[:, None, :], stiff)
        return jnp.einsum("sg,cg->cs", traction, normal, precision=lax.Precision.HIGHEST)

    partial_force = lax.map(bucket_force, (grouped, seg_point, normals, stiffness))
    partial_force = (
        partial_force.reshape(local_buckets, 3, elem_count, slot_width)
        .transpose(1, 2, 0, 3)
        .reshape(3, width)
    )
    returned = lax.all_to_all(partial_force, "elem", split_axis=1, concat_axis=1, tiled=True)
    picked = jnp.take(returned, target, axis=1)
    return of_everyone(jnp.where(handled[None, :], picked, 0.0), "bucket")


def solution(mesh):
    in_specs = (
        P(None, "elem"),
        P("elem"),
        P("elem"),
        P("elem", None, "bucket"),
        P("elem", None, "bucket"),
    )
    out_specs = P(None, "elem")
    return jax.shard_map(local, mesh=mesh, in_specs=in_specs, out_specs=out_specs, check_vma=False)
```

profile of v0, /device:TPU:1, one launch (start us, length us, event | category | flops | bytes accessed | tf_op | source)
XLA Modules:
  0.0 195.2 jit_solution(9392164284306216652)
XLA Ops:
  0.0 0.7 broadcast_multiply_fusion
  1.4 17.4 %gather_fusion = s32[3072]{0:T(1024)S(1)} fusion(s32[12288]{0:T(1024)S(1)} %copy-done, s32[3072]{0:T(1024)S(1)} %broadcast_clamp_fusion.1), kind=kCustom, calls=%fused_computation | custom fusion | bytes 36864 | tf_op jit(solution)/shard_map/jit(_take)/gather | solution.py:95
  18.9 23.5 %while.26 = (s32[]{:T(128)}, s32[1024]{0:T(1024)S(1)}, s32[24,128]{1,0:T(8,128)S(1)}, s32[24,128]{1,0:T(8,128)S(1)}) while((s32[]{:T(128)}, s32[1024]{0:T(1024)S(1)}, s32[24,128]{1,0:T(8,128)S(1)}, s32[24,128]{1,0:T(8,128)S(1)}) %tuple.79), condition=%wide.region_4.5_spmd.clone.clone, body=%wide.region_0.4_spmd.clone.sunk.clone | while | flops 17827712 | bytes 2129484 | solution.py:103
  42.4 4.0 %copy.101 = f32[24,12288]{0,1:T(8,128)} copy(f32[24,12288]{1,0:T(8,128)S(1)} %copy-done.1) | data formatting | bytes 2359296 | tf_op args[0]
  46.3 10.9 %gather_fusion.1 = f32[3072,24]{1,0:T(8,128)S(1)} fusion(f32[24,12288]{0,1:T(8,128)} %copy.101, s32[3072]{0:T(1024)S(1)} %broadcast_clamp_fusion.1), kind=kCustom, calls=%fused_computation.1 | custom fusion | bytes 602112 | tf_op jit(solution)/shard_map/jit(_take)/gather | solution.py:94
  58.9 8.4 %scatter_custom_fusion = f32[9,2048]{0,1:T(8,128)S(1)} fusion(s32[3072]{0:T(1024)S(1)} %bitcast.161, f32[3072,9]{1,0:T(8,128)S(1)} %copy.103, f32[]{:T(128)} %constant.125.clone.1), kind=kCustom, calls=%fused_computation.79 | custom fusion | bytes 73732 | tf_op jit(solution)/shard_map/scatter | solution.py:119
  67.6 11.8 %scatter_custom_fusion.1 = f32[2048]{0:T(1024)S(1)} fusion(s32[3072]{0:T(1024)S(1)} %bitcast.162, f32[3072]{0:T(1024)S(1)} %broadcast.570, f32[]{:T(128)} %constant.125.clone.1), kind=kCustom, calls=%fused_computation.132 | custom fusion | bytes 8196 | tf_op jit(solution)/shard_map/scatter | solution.py:121
  80.1 1.1 reshape.759
  81.2 18.4 %all-to-all-start = ((f32[128,1,160]{2,1,0:T(1,128)}), f32[128,1,160]{2,1,0:T(1,128)S(1)}, u32[]{:S(2)}, u32[]{:S(2)}) async-start(f32[128,1,160]{2,1,0:T(1,128)} %reshape.759), calls=%async_computation | async-start | bytes 262144 | tf_op jit(solution)/shard_map/all_to_all | solution.py:25
  99.6 10.2 %all_gather.3 = f32[8,5,512]{2,0,1:T(8,128)S(1)} all-gather(f32[8,5,128]{2,0,1:T(8,128)S(1)} %pad_maximum_fusion.2), channel_id=1, replica_groups=mesh['elem'=128,'bucket'=4] {'bucket'}, dimensions={2}, use_global_device_ids=true | all-gather | bytes 102400 | tf_op jit(solution)/shard_map/all_gather | solution.py:13
  110.0 2.3 %all-to-all-done = f32[128,1,160]{2,1,0:T(1,128)S(1)} async-done(((f32[128,1,160]{2,1,0:T(1,128)}), f32[128,1,160]{2,1,0:T(1,128)S(1)}, u32[]{:S(2)}, u32[]{:S(2)}) %all-to-all-start) | async-done | bytes 81952 | tf_op jit(solution)/shard_map/all_to_all | solution.py:25
  112.8 1.0 reduce.3
  115.8 4.0 %all-to-all-start.1 = ((f32[4,1,8]{2,1,0:T(1,128)}), f32[4,1,8]{2,1,0:T(1,128)S(1)}, u32[]{:S(2)}, u32[]{:S(2)}) async-start(f32[4,1,8]{2,1,0:T(1,128)} %broadcast_in_dim.100), calls=%async_computation.1 | async-start | bytes 4096 | tf_op jit(solution)/shard_map/all_to_all | solution.py:34
  120.2 3.7 %all-to-all-done.1 = f32[4,1,8]{2,1,0:T(1,128)S(1)} async-done(((f32[4,1,8]{2,1,0:T(1,128)}), f32[4,1,8]{2,1,0:T(1,128)S(1)}, u32[]{:S(2)}, u32[]{:S(2)}) %all-to-all-start.1) | async-done | bytes 160 | tf_op jit(solution)/shard_map/all_to_all | solution.py:34
  123.9 20.6 %while.25 = (s32[]{:T(128)}, f32[8,3,256]{2,1,0:T(4,128)S(1)}, f32[8,3,512]{2,0,1:T(8,128)S(1)}, f32[8,9,256]{2,1,0:T(8,128)S(1)}, f32[8,3,512]{2,0,1:T(8,128)S(1)}, /*index=5*/f32[8]{0:T(128)S(1)}) while((s32[]{:T(128)}, f32[8,3,256]{2,1,0:T(4,128)S(1)}, f32[8,3,512]{2,0,1:T(8,128)S(1)}, f32[8,9,256]{2,1,0:T(8,128)S(1)}, ...), condition=%wide.region_11.12_spmd.clone, body=%wide.region_10.11_spmd.sunk.clone | while | flops 8912904 | bytes 3257541 | solution.py:139
  124.8 1.7 fusion.88
  127.4 1.7 fusion.88
  129.4 0.6 dynamic_slice.30
  130.0 1.7 fusion.88
  132.6 1.7 fusion.88
  135.1 1.7 fusion.88
  137.7 1.7 fusion.88
  140.3 1.7 fusion.88
  142.8 1.7 fusion.88
  144.8 0.9 copy.114
  145.7 14.3 %all-to-all-start.2 = ((f32[3,128,16]{2,0,1:T(4,128)}), f32[3,128,16]{2,0,1:T(4,128)S(1)}, u32[]{:S(2)}, u32[]{:S(2)}) async-start(f32[3,128,16]{2,0,1:T(4,128)} %copy.114), calls=%async_computation.2 | async-start | bytes 524288 | tf_op jit(solution)/shard_map/all_to_all | solution.py:145
  160.0 15.2 %all-to-all-done.2 = f32[3,128,16]{2,0,1:T(4,128)S(1)} async-done(((f32[3,128,16]{2,0,1:T(4,128)}), f32[3,128,16]{2,0,1:T(4,128)S(1)}, u32[]{:S(2)}, u32[]{:S(2)}) %all-to-all-start.2) | async-done | bytes 24608 | tf_op jit(solution)/shard_map/all_to_all | solution.py:145
  175.2 0.8 copy.115
  176.0 8.1 %gather_fusion.2 = f32[3072,3]{1,0:T(8,128)S(1)} fusion(f32[3,2048]{0,1:T(8,128)S(1)} %bitcast.139, s32[3072]{0:T(1024)S(1)} %broadcast_clamp_fusion), kind=kCustom, calls=%fused_computation.2 | custom fusion | bytes 86016 | tf_op jit(solution)/shard_map/jit(_take)/gather | solution.py:146
  184.2 2.1 %select_bitcast_fusion = f32[3,3072]{0,1:T(8,128)S(1)} fusion(f32[3072,3]{1,0:T(8,128)S(1)} %gather_fusion.2, pred[3072]{0:T(1024)(128)(4,1)S(1)} %get-tuple-element.172, pred[3072]{0:T(1024)(128)(4,1)S(1)} %get-tuple-element.147), kind=kLoop, calls=%fused_computation.78 | loop fusion | flops 18432 | bytes 79872 | tf_op jit(solution)/shard_map/jit(_where)/select_n | solution.py:147
  186.8 7.8 %all_to_all.32 = f32[4,3,3072]{2,1,0:T(4,128)S(1)} all-to-all(f32[4,3,3072]{2,1,0:T(4,128)S(1)} %broadcast_in_dim.103), channel_id=1, replica_groups=mesh['elem'=128,'bucket'=4] {'bucket'}, dimensions={0} | all-to-all | bytes 294912 | tf_op jit(solution)/shard_map/all_to_all | solution.py:34
  194.5 0.7 reduce_sum.56
  (300 shorter events, 35.9 us)
Async XLA Ops:
  0.0 1.4 copy-start
  18.9 23.5 %copy-start.1 = (f32[24,12288]{1,0:T(8,128)S(1)}, f32[24,12288]{1,0:T(8,128)}, u32[]{:S(2)}) copy-start(f32[24,12288]{1,0:T(8,128)} %param.9) | copy-start | bytes 3538948
  79.6 19.9 %copy-start.3 = (f32[8,2,128]{2,1,0:T(2,128)S(1)}, f32[8,2,128]{2,1,0:T(2,128)}, u32[]{:S(2)}) copy-start(f32[8,2,128]{2,1,0:T(2,128)} %param.13) | copy-start | bytes 24580
  79.6 20.0 %copy-start.2 = (f32[8,3,128]{2,0,1:T(8,128)S(1)}, f32[8,3,128]{2,0,1:T(8,128)}, u32[]{:S(2)}) copy-start(f32[8,3,128]{2,0,1:T(8,128)} %param.12) | copy-start | bytes 36868
  81.2 31.1 %all-to-all-start = ((f32[128,1,160]{2,1,0:T(1,128)}), f32[128,1,160]{2,1,0:T(1,128)S(1)}, u32[]{:S(2)}, u32[]{:S(2)}) async-start(f32[128,1,160]{2,1,0:T(1,128)} %reshape.759), calls=%async_computation | async-start | bytes 262144 | tf_op jit(solution)/shard_map/all_to_all | solution.py:25
  115.8 8.1 %all-to-all-start.1 = ((f32[4,1,8]{2,1,0:T(1,128)}), f32[4,1,8]{2,1,0:T(1,128)S(1)}, u32[]{:S(2)}, u32[]{:S(2)}) async-start(f32[4,1,8]{2,1,0:T(1,128)} %broadcast_in_dim.100), calls=%async_computation.1 | async-start | bytes 4096 | tf_op jit(solution)/shard_map/all_to_all | solution.py:34
  145.7 29.5 %all-to-all-start.2 = ((f32[3,128,16]{2,0,1:T(4,128)}), f32[3,128,16]{2,0,1:T(4,128)S(1)}, u32[]{:S(2)}, u32[]{:S(2)}) async-start(f32[3,128,16]{2,0,1:T(4,128)} %copy.114), calls=%async_computation.2 | async-start | bytes 524288 | tf_op jit(solution)/shard_map/all_to_all | solution.py:145
where the time goes:
time: 196 us; the launch traced here: 195 us
  local copies, waits for them, and re-layouts  76 us (39%)
  starting transfers between devices  36.7 us (19%)
  other arithmetic  28.2 us (14%)
  waiting for transfers between devices  21.1 us (11%)
  blocking collectives  18 us (9%)
  matrix products  13.3 us (7%)
    all_to_all x1, starting transfers between devices, in_one_piece_2(): lax.all_to_all(both, axis, split_axis=split_dim, concat_axis=concat_dim,...  18.4 us
    gather x1, local copies, waits for them, and re-layouts, local(): face_bucket = jnp.take(bucket_map, face_index)  17.4 us
    all_to_all x1, waiting for transfers between devices, local(): lax.all_to_all(partial_force, 'elem', split_axis=1, concat_axis=1, tiled=...  15.2 us
    all_to_all x1, starting transfers between devices, local(): lax.all_to_all(partial_force, 'elem', split_axis=1, concat_axis=1, tiled=...  14.3 us
    dot_general x8, matrix products, bucket_force(): jnp.einsum('sg,cg->cs', traction, normal, precision=lax.Precision.HIGHEST)  13.3 us
    scatter x1, local copies, waits for them, and re-layouts, local(): jnp.zeros((1, width), jnp.float32).at[:, send_index].set(1.0, mode='drop')  11.8 us
    another operation x24, other arithmetic, rank_block(): earlier = jnp.cumsum(onehot, axis=0) - onehot + carried[None, :]  11.7 us
    gather x2, local copies, waits for them, and re-layouts, local(): face_rows = jnp.take(node_data, face_index, axis=1)  11.3 us
  transfers between devices with their start and end apart: 3, of which 3 were waited for; matrix products, arithmetic and copies ran while one was open for 0% of the time, Pallas kernels for 0%

commit v1 on v0

v1 whole, which is shorter than its diff:
```python
import jax
import jax.numpy as jnp
from jax import lax
from jax.experimental import pallas as pl
from jax.experimental.pallas import tpu as pltpu
from jax.sharding import PartitionSpec as P

STIFFNESS = 20.0
DAMPING = 0.5
SLOTS = 5
LANES = 128
F32 = jnp.float32
BF16 = jnp.bfloat16
NT = (((1,), (1,)), ((), ()))


def one_hot(row, size):
    numbers = lax.broadcasted_iota(jnp.int32, (size, row.shape[1]), 0)
    return jnp.where(numbers == row, 1.0, 0.0).astype(BF16)


def pack_kernel(eroded_ref, map_ref, node_hbm, out_ref, code_ref, node_ref, row_ref, lo_hot, col_ref,
                rank_ref, slot_ref, left_ref, right_ref, sum_ref, geo_ref, sem):
    copy = pltpu.make_async_copy(node_hbm, node_ref, sem)
    copy.start()
    group = lax.axis_index("bucket")
    blocks = map_ref.shape[0]
    count = row_ref.shape[1]
    rows4 = eroded_ref.shape[0]
    span = count // rows4

    eroded = eroded_ref[...]
    lane = lax.broadcasted_iota(jnp.int32, (LANES, span), 1)
    six = 6 * lax.broadcasted_iota(jnp.int32, (LANES, span), 0)
    spread = jnp.where((lane >= six) & (lane < six + 6), 1.0, 0.0).astype(BF16)
    high = jnp.dot((eroded >> 3).astype(F32).astype(BF16), spread, preferred_element_type=F32)
    low = jnp.dot((eroded & 7).astype(F32).astype(BF16), spread, preferred_element_type=F32)
    number = lax.broadcasted_iota(jnp.int32, (rows4, span), 1)
    faces4 = 6 * (high * 8.0 + low).astype(jnp.int32) + number % 6
    for a in range(rows4):
        row_ref[0:1, a * span:(a + 1) * span] = faces4[a:a + 1, :]

    buckets = map_ref[...]
    digits = jnp.concatenate([(buckets >> 3).astype(F32), (buckets & 7).astype(F32)], axis=0).astype(BF16)
    step = 512
    for c in range(count // step):
        face = row_ref[0:1, c * step:(c + 1) * step]
        hot = one_hot(face & (LANES - 1), LANES)
        lo_hot[:, c * step:(c + 1) * step] = hot
        both = jnp.dot(digits, hot, preferred_element_type=F32)
        value = both[:blocks] * 8.0 + both[blocks:]
        numbers = lax.broadcasted_iota(jnp.int32, (blocks, step), 0)
        rank_ref[0:1, c * step:(c + 1) * step] = jnp.sum(
            jnp.where(numbers == (face >> 7), value, 0.0), axis=0, keepdims=True)

    tiles = count // LANES
    for t in range(tiles):
        mine = rank_ref[0:1, t * LANES:(t + 1) * LANES]
        col_ref[t * LANES:(t + 1) * LANES, :] = jnp.broadcast_to(mine, (LANES, LANES)).T
    earlier = (lax.broadcasted_iota(jnp.int32, (LANES, LANES), 0)
               < lax.broadcasted_iota(jnp.int32, (LANES, LANES), 1))
    for t in range(tiles):
        mine = rank_ref[0:1, t * LANES:(t + 1) * LANES]

        def same(block, total, mine=mine):
            other = col_ref[pl.ds(pl.multiple_of(block * LANES, LANES), LANES), :]
            hit = jnp.where(other == mine, 1.0, 0.0)
            return total + jnp.sum(hit.reshape(LANES // 8, 8, LANES), axis=0)

        total = lax.fori_loop(0, t, same, jnp.zeros((8, LANES), F32))
        other = col_ref[t * LANES:(t + 1) * LANES, :]
        hit = jnp.where((other == mine) & earlier, 1.0, 0.0)
        total = total + jnp.sum(hit.reshape(LANES // 8, 8, LANES), axis=0)
        rank_ref[1:2, t * LANES:(t + 1) * LANES] = jnp.sum(total, axis=0, keepdims=True)

    bucket = rank_ref[0:1, :].astype(jnp.int32)
    rank = rank_ref[1:2, :]
    owner = bucket >> 3
    inner = bucket & 7
    code_ref[0:1, :] = owner
    code_ref[1:2, :] = inner * SLOTS + rank.astype(jnp.int32)
    column = jnp.where((inner >> 1) == group, (inner & 1) * LANES + owner + 1, 0).astype(F32)
    placed = jnp.zeros((2 * blocks, LANES), F32)
    for c in range(count // step):
        at = slice(c * step, (c + 1) * step)
        face = row_ref[0:1, at]
        numbers = lax.broadcasted_iota(jnp.int32, (blocks, step), 0)
        mine = numbers == (face >> 7)
        left = jnp.concatenate(
            [jnp.where(mine, column[:, at], 0.0), jnp.where(mine, rank[:, at], 0.0)], axis=0).astype(BF16)
        placed = placed + lax.dot_general(left, lo_hot[:, at], NT, preferred_element_type=F32)
    slot_ref[...] = placed

    copy.wait()
    left_ref[5 * 48:, :] = jnp.ones((16, left_ref.shape[1]), BF16)
    sum_ref[...] = jnp.zeros(sum_ref.shape, F32)
    per = left_ref.shape[1] // LANES

    def pack(chunk, carry):
        for t in range(per):
            block = chunk * per + t
            lanes = pl.ds(pl.multiple_of(block * LANES, LANES), LANES)
            at = slice(t * LANES, (t + 1) * LANES)
            col = slot_ref[pl.ds(block, 1), :]
            order = slot_ref[pl.ds(blocks + block, 1), :]
            numbers = lax.broadcasted_iota(jnp.int32, (256, LANES), 0).astype(F32) + 1.0
            right_ref[:, at] = jnp.where(numbers == col, 1.0, 0.0).astype(BF16)
            node = node_ref[:, lanes]
            first = node.astype(BF16).astype(F32)
            pieces = jnp.concatenate([first, node - first], axis=0)
            for k in range(SLOTS):
                left_ref[k * 48:(k + 1) * 48, at] = jnp.where(order == float(k), pieces, 0.0).astype(BF16)
        sum_ref[...] += lax.dot_general(left_ref[...], right_ref[...], NT, preferred_element_type=F32)
        return carry

    lax.fori_loop(0, blocks // per, pack, 0)

    col_ref[0:LANES, :] = jnp.zeros((LANES, LANES), F32)
    for par in range(2):
        at = slice(par * LANES, (par + 1) * LANES)
        for k in range(SLOTS):
            geo_ref[k * 24:(k + 1) * 24, :] = (
                sum_ref[k * 48:k * 48 + 24, at] + sum_ref[k * 48 + 24:k * 48 + 48, at])
        row = [geo_ref[pl.ds(r, SLOTS, stride=24), :] for r in range(24)]
        corner = [row[3 * m:3 * m + 3] for m in range(4)]
        motion = [row[12 + 3 * m:15 + 3 * m] for m in range(4)]
        centroid = [0.25 * (corner[0][i] + corner[1][i] + corner[2][i] + corner[3][i]) for i in range(3)]
        one = [corner[2][i] - corner[0][i] for i in range(3)]
        two = [corner[3][i] - corner[1][i] for i in range(3)]
        area = [
            0.5 * (one[1] * two[2] - one[2] * two[1]),
            0.5 * (one[2] * two[0] - one[0] * two[2]),
            0.5 * (one[0] * two[1] - one[1] * two[0]),
        ]
        velocity = [0.25 * (motion[0][i] + motion[1][i] + motion[2][i] + motion[3][i]) for i in range(3)]
        for q, value in enumerate(centroid + area + velocity):
            start = par * 64 + q * SLOTS
            col_ref[start:start + SLOTS, :] = value
        col_ref[par * 64 + 45:par * 64 + 46, :] = sum_ref[240:241, at]
    out_ref[...] = col_ref[0:LANES, :].T


def force_kernel(face_ref, seg_ref, out_ref, row_ref, wide_ref):
    row_ref[...] = face_ref[...].T
    groups = seg_ref.shape[0] // 2
    for g in range(2 * groups):
        columns = seg_ref[g].T
        for q in range(6):
            wide_ref[g % 2, q, (g // 2) * LANES:(g // 2 + 1) * LANES, :] = jnp.broadcast_to(
                columns[:, q:q + 1], (LANES, LANES))
    out_ref[...] = jnp.zeros(out_ref.shape, F32)
    chunk = 64
    for par in range(2):
        count = jnp.sum(row_ref[par * 64 + 45:par * 64 + 46, :], axis=1, keepdims=True)
        stiff = jnp.broadcast_to(STIFFNESS * lax.rsqrt(jnp.maximum(count, 1.0)), (1, LANES))
        for k in range(SLOTS):
            geo = [row_ref[par * 64 + q * SLOTS + k:par * 64 + q * SLOTS + k + 1, :] for q in range(9)]

            def pairs(step, total, par=par, geo=geo, stiff=stiff):
                at = pl.ds(pl.multiple_of(step * chunk, chunk), chunk)
                seg = [wide_ref[par, q, at, :] for q in range(6)]
                normal = seg[3:6]
                off = [geo[i] - seg[i] for i in range(3)]
                dist_sq = off[0] * off[0] + off[1] * off[1] + off[2] * off[2]
                gap = off[0] * normal[0] + off[1] * normal[1] + off[2] * normal[2]
                closing = geo[6] * normal[0] + geo[7] * normal[1] + geo[8] * normal[2]
                projected = jnp.abs(geo[3] * normal[0] + geo[4] * normal[1] + geo[5] * normal[2])
                weight = jnp.exp(-0.5 * dist_sq)
                traction = weight * jnp.maximum(-gap, 0.0) * (stiff - DAMPING * closing) * projected
                return tuple(
                    total[i] + jnp.sum((traction * normal[i]).reshape(chunk // 8, 8, LANES), axis=0)
                    for i in range(3))

            zero = jnp.zeros((8, LANES), F32)
            total = lax.fori_loop(0, wide_ref.shape[2] // chunk, pairs, (zero, zero, zero))
            for i in range(3):
                force = jnp.sum(total[i], axis=0, keepdims=True)
                for x in range(out_ref.shape[0]):
                    out_ref[x, i * 10 + par * SLOTS + k:i * 10 + par * SLOTS + k + 1, :] = force


def pick_kernel(force_ref, code_ref, out_ref, row_ref):
    turned = force_ref[...].T
    for x in range(4):
        for i in range(3):
            row_ref[i * 40 + x * 10:i * 40 + x * 10 + 10, :] = turned[x * 32 + i * 10:x * 32 + i * 10 + 10, :]
    value = row_ref[...]
    first = value.astype(BF16)
    second = (value - first.astype(F32)).astype(BF16)
    left = jnp.concatenate([first.astype(F32), second.astype(F32)], axis=0).astype(BF16)
    rows = value.shape[0]
    step = 512
    for c in range(out_ref.shape[1] // step):
        at = slice(c * step, (c + 1) * step)
        hot = one_hot(code_ref[0:1, at], LANES)
        both = jnp.dot(left, hot, preferred_element_type=F32)
        found = both[:rows] + both[rows:]
        mine = lax.broadcasted_iota(jnp.int32, (40, step), 0) == code_ref[1:2, at]
        for i in range(3):
            out_ref[i:i + 1, at] = jnp.sum(
                jnp.where(mine, found[i * 40:(i + 1) * 40], 0.0), axis=0, keepdims=True)


def local(node_data, eroded, bucket_map, seg_point, seg_angle):
    owners = lax.axis_size("elem")
    groups = lax.axis_size("bucket")
    faces = node_data.shape[1]
    blocks = faces // LANES
    uncovered = 6 * eroded.shape[0]
    vmem = pl.BlockSpec(memory_space=pltpu.VMEM)

    azimuth, polar = seg_angle[:, 0], seg_angle[:, 1]
    normal = jnp.stack(
        [jnp.cos(azimuth) * jnp.sin(polar), jnp.sin(azimuth) * jnp.sin(polar), jnp.cos(polar)], axis=1)
    segs = jnp.concatenate([seg_point, normal, jnp.zeros_like(seg_angle)], axis=1)
    segs = lax.all_to_all(segs, "bucket", 0, 0, tiled=True)

    packed, code = pl.pallas_call(
        pack_kernel,
        out_shape=(
            jax.ShapeDtypeStruct((owners, LANES), F32),
            jax.ShapeDtypeStruct((2, uncovered), jnp.int32),
        ),
        in_specs=[vmem, vmem, pl.BlockSpec(memory_space=pl.ANY)],
        out_specs=(vmem, vmem),
        scratch_shapes=[
            pltpu.VMEM((24, faces), F32),
            pltpu.VMEM((1, uncovered), jnp.int32),
            pltpu.VMEM((LANES, uncovered), BF16),
            pltpu.VMEM((uncovered, LANES), F32),
            pltpu.VMEM((2, uncovered), F32),
            pltpu.VMEM((2 * blocks, LANES), F32),
            pltpu.VMEM((256, 8 * LANES), BF16),
            pltpu.VMEM((256, 8 * LANES), BF16),
            pltpu.VMEM((256, 256), F32),
            pltpu.VMEM((120, LANES), F32),
            pltpu.SemaphoreType.DMA,
        ],
        name="pack",
    )(eroded.reshape(-1, LANES), bucket_map.reshape(blocks, LANES), node_data)

    arrived = lax.all_to_all(packed.reshape(owners, 1, LANES), "elem", 0, 0, tiled=True)

    force = pl.pallas_call(
        force_kernel,
        out_shape=jax.ShapeDtypeStruct((groups, 32, LANES), F32),
        in_specs=[vmem, vmem],
        out_specs=vmem,
        scratch_shapes=[
            pltpu.VMEM((LANES, LANES), F32),
            pltpu.VMEM((2, 6, groups * LANES, LANES), F32),
        ],
        name="force",
    )(arrived.reshape(owners, LANES), segs)

    shared = lax.all_to_all(force, "bucket", 0, 0, tiled=True)
    outgoing = shared.reshape(groups * 32, owners).T
    returned = lax.all_to_all(outgoing.reshape(owners, 1, LANES), "elem", 0, 0, tiled=True)

    return pl.pallas_call(
        pick_kernel,
        out_shape=jax.ShapeDtypeStruct((3, uncovered), F32),
        in_specs=[vmem, vmem],
        out_specs=vmem,
        scratch_shapes=[pltpu.VMEM((120, LANES), F32)],
        name="pick",
    )(returned.reshape(owners, LANES), code)


def solution(mesh):
    in_specs = (
        P(None, "elem"),
        P("elem"),
        P("elem"),
        P("elem", None, "bucket"),
        P("elem", None, "bucket"),
    )
    out_specs = P(None, "elem")
    return jax.shard_map(local, mesh=mesh, in_specs=in_specs, out_specs=out_specs, check_vma=False)
```

time: 196 us -> 90.2 us (0.46)
  local copies, waits for them, and re-layouts: 76 us -> 1.46 us
  blocking collectives: 18 us -> 57.7 us
  starting transfers between devices: 36.7 us -> 4.83 us
  other arithmetic: 28.2 us -> 1.01 us
  Pallas kernels: 0 us -> 24.6 us
  waiting for transfers between devices: 21.1 us -> 0.01 us
  matrix products: 13.3 us -> 0 us
    all_to_all x1 -> x3, blocking collectives: 7.76 us -> 57.7 us  [the longest x1 29.5 us: local(): lax.all_to_all(packed.reshape(owners, 1, LANES), 'elem', 0, 0, tiled=True)]
    gather x4 -> x0, local copies, waits for them, and re-layouts: 36.9 us -> none  [the longest x1 17.4 us: local(): face_bucket = jnp.take(bucket_map, face_index)]
    all_to_all x3 -> x1, starting transfers between devices: 36.7 us -> 4.83 us  [local(): segs = lax.all_to_all(segs, 'bucket', 0, 0, tiled=True)]
    pallas_call x0 -> x3, Pallas kernels: none -> 24.6 us  [the longest x1 15.5 us: local(): pl.pallas_call(pack_kernel, out_shape=(jax.ShapeDtypeStruct((owners, LANE...]
    all_to_all x3 -> x1, waiting for transfers between devices: 21.1 us -> 0.01 us  [local(): segs = lax.all_to_all(segs, 'bucket', 0, 0, tiled=True)]
    scatter x3 -> x0, local copies, waits for them, and re-layouts: 20.5 us -> none  [the longest x1 11.8 us: local(): jnp.zeros((1, width), jnp.float32).at[:, send_index].set(1.0, mode='drop')]
    dot_general x8 -> x0, matrix products: 13.3 us -> none  [bucket_force(): jnp.einsum('sg,cg->cs', traction, normal, precision=lax.Precision.HIGHEST)]
    another operation x25 -> x0, other arithmetic: 11.7 us -> none  [the longest x24 11.7 us: rank_block(): earlier = jnp.cumsum(onehot, axis=0) - onehot + carried[None, :]]
  transfers between devices with their start and end apart: 3 -> 1, of which waited for: 3 -> 0; matrix products, arithmetic and copies ran while one was open for 0% -> 0% of each run, Pallas kernels for 0% -> 17%
where the time goes in v1:
time: 90.2 us; the launch traced here: 89.6 us
  blocking collectives  57.7 us (64%)
  Pallas kernels  24.6 us (27%)
  starting transfers between devices  4.83 us (5%)
  local copies, waits for them, and re-layouts  1.46 us (2%)
  other arithmetic  1.01 us (1%)
    all_to_all x1, blocking collectives, local(): lax.all_to_all(packed.reshape(owners, 1, LANES), 'elem', 0, 0, tiled=True)  29.5 us
    all_to_all x1, blocking collectives, local(): lax.all_to_all(outgoing.reshape(owners, 1, LANES), 'elem', 0, 0, tiled=True)  19.1 us
    pallas_call x1, Pallas kernels, local(): pl.pallas_call(pack_kernel, out_shape=(jax.ShapeDtypeStruct((owners, LANE...  15.5 us
    all_to_all x1, blocking collectives, local(): shared = lax.all_to_all(force, 'bucket', 0, 0, tiled=True)  8.99 us
    pallas_call x1, Pallas kernels, local(): pl.pallas_call(force_kernel, out_shape=jax.ShapeDtypeStruct((groups, 32,...  7 us
    all_to_all x1, starting transfers between devices, local(): segs = lax.all_to_all(segs, 'bucket', 0, 0, tiled=True)  4.83 us
    pallas_call x1, Pallas kernels, local(): pl.pallas_call(pick_kernel, out_shape=jax.ShapeDtypeStruct((3, uncovered)...  2.1 us
  transfers between devices with their start and end apart: 1, of which 0 were waited for; matrix products, arithmetic and copies ran while one was open for 0% of the time, Pallas kernels for 17%

profile of v1, /device:TPU:1, one launch (start us, length us, event | category | flops | bytes accessed | tf_op | source)
XLA Modules:
  0.0 89.6 jit_solution(11926698218291130671)
XLA Ops:
  0.0 0.7 copy.14
  0.7 1.0 %slice_cosine_fusion = (f32[8,1,128]{2,1,0:T(1,128)S(1)}, f32[8,1,128]{2,1,0:T(1,128)S(1)}, f32[8,1,128]{2,1,0:T(1,128)S(1)}) fusion(f32[8,2,128]{2,1,0:T(2,128)} %param.9), kind=kLoop, calls=%fused_computation.2 | loop fusion | flops 2048 | bytes 20480 | tf_op jit(solution)/shard_map/cos | solution.py:214
  1.7 0.7 concatenate.3
  2.4 4.8 %all-to-all-start.1 = ((f32[8,8,128]{2,1,0:T(8,128)}), f32[8,8,128]{2,1,0:T(8,128)S(1)}, u32[]{:S(2)}, u32[]{:S(2)}) async-start(f32[8,8,128]{2,1,0:T(8,128)} %concatenate.3), calls=%async_computation.1 | async-start | bytes 65536 | tf_op jit(solution)/shard_map/all_to_all | solution.py:216
  7.2 15.5 %pack.1 = (f32[128,128]{1,0:T(8,128)}, s32[2,3072]{1,0:T(2,128)}) custom-call(s32[4,128]{1,0:T(4,128)} %bitcast.17, s32[96,128]{1,0:T(8,128)} %bitcast.16, f32[24,12288]{1,0:T(8,128)} %node_hbm.1), custom_call_target="tpu_custom_call" | custom-call | tf_op jit(solution)/shard_map/pack/pallas_call | solution.py:218
  22.8 0.0 all-to-all-done.1.seg_ref
  22.8 0.0 copy-start
  22.8 29.5 %all_to_all.20 = f32[128,1,128]{2,1,0:T(1,128)} all-to-all(f32[128,1,128]{2,1,0:T(1,128)} %bitcast.15), channel_id=1, replica_groups=mesh['elem'=128,'bucket'=4] {'elem'}, dimensions={0} | all-to-all | bytes 131072 | tf_op jit(solution)/shard_map/all_to_all | solution.py:242
  52.3 0.0 copy-done
  52.3 7.0 %force.1 = f32[4,32,128]{2,1,0:T(8,128)} custom-call(f32[128,128]{1,0:T(8,128)} %bitcast.13, f32[8,8,128]{2,1,0:T(8,128)} %copy-done), custom_call_target="tpu_custom_call" | custom-call | tf_op jit(solution)/shard_map/force/pallas_call | solution.py:244
  59.3 9.0 %all_to_all.21 = f32[4,32,128]{2,1,0:T(8,128)S(1)} all-to-all(f32[4,32,128]{2,1,0:T(8,128)} %force.1), channel_id=1, replica_groups=mesh['elem'=128,'bucket'=4] {'bucket'}, dimensions={0} | all-to-all | bytes 131072 | tf_op jit(solution)/shard_map/all_to_all | solution.py:256
  68.3 0.1 copy.15
  68.4 19.1 %all_to_all.22 = f32[128,1,128]{2,1,0:T(1,128)} all-to-all(f32[128,1,128]{2,1,0:T(1,128)S(1)} %copy.15), channel_id=1, replica_groups=mesh['elem'=128,'bucket'=4] {'elem'}, dimensions={0} | all-to-all | bytes 131072 | tf_op jit(solution)/shard_map/all_to_all | solution.py:258
  87.5 2.1 %pick.1 = f32[3,3072]{1,0:T(4,128)} custom-call(f32[128,128]{1,0:T(8,128)} %bitcast.12, s32[2,3072]{1,0:T(2,128)} %get-tuple-element.8.code_ref), custom_call_target="tpu_custom_call" | custom-call | tf_op jit(solution)/shard_map/pick/pallas_call | solution.py:260
  (1 shorter events, 0.0 us)
Async XLA Ops:
  2.4 20.4 %all-to-all-start.1 = ((f32[8,8,128]{2,1,0:T(8,128)}), f32[8,8,128]{2,1,0:T(8,128)S(1)}, u32[]{:S(2)}, u32[]{:S(2)}) async-start(f32[8,8,128]{2,1,0:T(8,128)} %concatenate.3), calls=%async_computation.1 | async-start | bytes 65536 | tf_op jit(solution)/shard_map/all_to_all | solution.py:216
  22.8 29.5 %copy-start = (f32[8,8,128]{2,1,0:T(8,128)}, f32[8,8,128]{2,1,0:T(8,128)S(1)}, u32[]{:S(2)}) copy-start(f32[8,8,128]{2,1,0:T(8,128)S(1)} %all-to-all-done.1.seg_ref) | copy-start | bytes 98308

commit v2 on v1

--- a/solution.py
+++ b/solution.py
@@ -19,13 +19,26 @@
     return jnp.where(numbers == row, 1.0, 0.0).astype(BF16)
 
 
-def pack_kernel(eroded_ref, map_ref, node_hbm, out_ref, code_ref, node_ref, row_ref, lo_hot, col_ref,
-                rank_ref, slot_ref, left_ref, right_ref, sum_ref, geo_ref, sem):
+def segment_kernel(point_ref, angle_ref, seg_ref):
+    azimuth, polar = angle_ref[:, 0, :], angle_ref[:, 1, :]
+    ring = jnp.sin(polar)
+    for i in range(3):
+        seg_ref[:, i, :] = point_ref[i]
+    seg_ref[:, 3, :] = jnp.cos(azimuth) * ring
+    seg_ref[:, 4, :] = jnp.sin(azimuth) * ring
+    seg_ref[:, 5, :] = jnp.cos(polar)
+    seg_ref[:, 6, :] = jnp.zeros_like(ring)
+    seg_ref[:, 7, :] = jnp.zeros_like(ring)
+
+
+def pack_kernel(eroded_ref, map_ref, node_hbm, out_ref, code_ref, node_ref, row_ref, col_ref, rank_ref, owner_hot,
+                geo_ref, sem):
     copy = pltpu.make_async_copy(node_hbm, node_ref, sem)
     copy.start()
     group = lax.axis_index("bucket")
     blocks = map_ref.shape[0]
     count = row_ref.shape[1]
+    tiles = count // LANES
     rows4 = eroded_ref.shape[0]
     span = count // rows4
 
@@ -41,87 +54,58 @@
         row_ref[0:1, a * span:(a + 1) * span] = faces4[a:a + 1, :]
 
     buckets = map_ref[...]
-    digits = jnp.concatenate([(buckets >> 3).astype(F32), (buckets & 7).astype(F32)], axis=0).astype(BF16)
+    digits = jnp.concatenate([(buckets & 1016).astype(F32), (buckets & 7).astype(F32)], axis=1).astype(BF16)
     step = 512
     for c in range(count // step):
-        face = row_ref[0:1, c * step:(c + 1) * step]
+        at = slice(c * step, (c + 1) * step)
+        face = row_ref[0:1, at]
         hot = one_hot(face & (LANES - 1), LANES)
-        lo_hot[:, c * step:(c + 1) * step] = hot
-        both = jnp.dot(digits, hot, preferred_element_type=F32)
-        value = both[:blocks] * 8.0 + both[blocks:]
+        value = jnp.dot(digits, jnp.concatenate([hot, hot], axis=0), preferred_element_type=F32)
         numbers = lax.broadcasted_iota(jnp.int32, (blocks, step), 0)
-        rank_ref[0:1, c * step:(c + 1) * step] = jnp.sum(
-            jnp.where(numbers == (face >> 7), value, 0.0), axis=0, keepdims=True)
-
-    tiles = count // LANES
-    for t in range(tiles):
-        mine = rank_ref[0:1, t * LANES:(t + 1) * LANES]
-        col_ref[t * LANES:(t + 1) * LANES, :] = jnp.broadcast_to(mine, (LANES, LANES)).T
+        rank_ref[0:1, at] = jnp.sum(jnp.where(numbers == (face >> 7), value, 0.0), axis=0, keepdims=True)
+
     earlier = (lax.broadcasted_iota(jnp.int32, (LANES, LANES), 0)
                < lax.broadcasted_iota(jnp.int32, (LANES, LANES), 1))
+    counts, picks = [], []
     for t in range(tiles):
-        mine = rank_ref[0:1, t * LANES:(t + 1) * LANES]
-
-        def same(block, total, mine=mine):
-            other = col_ref[pl.ds(pl.multiple_of(block * LANES, LANES), LANES), :]
-            hit = jnp.where(other == mine, 1.0, 0.0)
-            return total + jnp.sum(hit.reshape(LANES // 8, 8, LANES), axis=0)
-
-        total = lax.fori_loop(0, t, same, jnp.zeros((8, LANES), F32))
-        other = col_ref[t * LANES:(t + 1) * LANES, :]
+        at = slice(t * LANES, (t + 1) * LANES)
+        mine = rank_ref[0:1, at]
+        other = jnp.broadcast_to(mine, (LANES, LANES)).T
         hit = jnp.where((other == mine) & earlier, 1.0, 0.0)
-        total = total + jnp.sum(hit.reshape(LANES // 8, 8, LANES), axis=0)
-        rank_ref[1:2, t * LANES:(t + 1) * LANES] = jnp.sum(total, axis=0, keepdims=True)
+        rank_ref[1:2, at] = jnp.sum(hit, axis=0, keepdims=True)
+        bucket = mine.astype(jnp.int32)
+        hot = one_hot(bucket >> 3, LANES)
+        owner_hot[:, at] = hot
+        picks.append(lax.broadcasted_iota(jnp.int32, (16, LANES), 0) == (bucket & 7))
+        inner = jnp.where(picks[t], 1.0, 0.0).astype(BF16)
+        counts.append(lax.dot_general(inner, hot, NT, preferred_element_type=F32))
+    before = jnp.zeros((16, LANES), F32)
+    for t in range(tiles):
+        at = slice(t * LANES, (t + 1) * LANES)
+        if t:
+            before = before + counts[t - 1]
+            seen = jnp.dot(before.astype(BF16), owner_hot[:, at], preferred_element_type=F32)
+            rank_ref[1:2, at] += jnp.sum(jnp.where(picks[t], seen, 0.0), axis=0, keepdims=True)
 
     bucket = rank_ref[0:1, :].astype(jnp.int32)
-    rank = rank_ref[1:2, :]
+    rank = rank_ref[1:2, :].astype(jnp.int32)
     owner = bucket >> 3
     inner = bucket & 7
     code_ref[0:1, :] = owner
-    code_ref[1:2, :] = inner * SLOTS + rank.astype(jnp.int32)
-    column = jnp.where((inner >> 1) == group, (inner & 1) * LANES + owner + 1, 0).astype(F32)
-    placed = jnp.zeros((2 * blocks, LANES), F32)
+    code_ref[1:2, :] = inner * SLOTS + rank
+    column = jnp.where((inner >> 1) == group, (inner & 1) * LANES + owner, -1)
+    source = jnp.zeros((16, 256), F32)
     for c in range(count // step):
         at = slice(c * step, (c + 1) * step)
         face = row_ref[0:1, at]
-        numbers = lax.broadcasted_iota(jnp.int32, (blocks, step), 0)
-        mine = numbers == (face >> 7)
-        left = jnp.concatenate(
-            [jnp.where(mine, column[:, at], 0.0), jnp.where(mine, rank[:, at], 0.0)], axis=0).astype(BF16)
-        placed = placed + lax.dot_general(left, lo_hot[:, at], NT, preferred_element_type=F32)
-    slot_ref[...] = placed
+        numbers = lax.broadcasted_iota(jnp.int32, (16, step), 0)
+        parts = jnp.where(numbers < 8, (face >> 7) + 1, face & (LANES - 1))
+        left = jnp.where((numbers & 7) == rank[:, at], parts, 0).astype(F32).astype(BF16)
+        source = source + lax.dot_general(left, one_hot(column[:, at], 256), NT, preferred_element_type=F32)
 
     copy.wait()
-    left_ref[5 * 48:, :] = jnp.ones((16, left_ref.shape[1]), BF16)
-    sum_ref[...] = jnp.zeros(sum_ref.shape, F32)
-    per = left_ref.shape[1] // LANES
-
-    def pack(chunk, carry):
-        for t in range(per):
-            block = chunk * per + t
-            lanes = pl.ds(pl.multiple_of(block * LANES, LANES), LANES)
-            at = slice(t * LANES, (t + 1) * LANES)
-            col = slot_ref[pl.ds(block, 1), :]
-            order = slot_ref[pl.ds(blocks + block, 1), :]
-            numbers = lax.broadcasted_iota(jnp.int32, (256, LANES), 0).astype(F32) + 1.0
-            right_ref[:, at] = jnp.where(numbers == col, 1.0, 0.0).astype(BF16)
-            node = node_ref[:, lanes]
-            first = node.astype(BF16).astype(F32)
-            pieces = jnp.concatenate([first, node - first], axis=0)
-            for k in range(SLOTS):
-                left_ref[k * 48:(k + 1) * 48, at] = jnp.where(order == float(k), pieces, 0.0).astype(BF16)
-        sum_ref[...] += lax.dot_general(left_ref[...], right_ref[...], NT, preferred_element_type=F32)
-        return carry
-
-    lax.fori_loop(0, blocks // per, pack, 0)
-
-    col_ref[0:LANES, :] = jnp.zeros((LANES, LANES), F32)
-    for par in range(2):
-        at = slice(par * LANES, (par + 1) * LANES)
-        for k in range(SLOTS):
-            geo_ref[k * 24:(k + 1) * 24, :] = (
-                sum_ref[k * 48:k * 48 + 24, at] + sum_ref[k * 48 + 24:k * 48 + 48, at])
-        row = [geo_ref[pl.ds(r, SLOTS, stride=24), :] for r in range(24)]
+    for g in range(blocks // 16):
+        row = [node_ref[pl.ds((r // 8) * blocks * 8 + r % 8 + g * 128, 16, stride=8), :] for r in range(24)]
         corner = [row[3 * m:3 * m + 3] for m in range(4)]
         motion = [row[12 + 3 * m:15 + 3 * m] for m in range(4)]
         centroid = [0.25 * (corner[0][i] + corner[1][i] + corner[2][i] + corner[3][i]) for i in range(3)]
@@ -134,10 +118,29 @@
         ]
         velocity = [0.25 * (motion[0][i] + motion[1][i] + motion[2][i] + motion[3][i]) for i in range(3)]
         for q, value in enumerate(centroid + area + velocity):
-            start = par * 64 + q * SLOTS
-            col_ref[start:start + SLOTS, :] = value
-        col_ref[par * 64 + 45:par * 64 + 46, :] = sum_ref[240:241, at]
-    out_ref[...] = col_ref[0:LANES, :].T
+            at = slice(q * blocks + g * 16, q * blocks + g * 16 + 16)
+            first = value.astype(BF16)
+            geo_ref[at, :LANES] = first
+            geo_ref[at, LANES:] = (value - first.astype(F32)).astype(BF16)
+
+    col_ref[...] = jnp.zeros(col_ref.shape, F32)
+    geometry = geo_ref[...]
+    filled = jnp.zeros((1, 256), F32)
+    for k in range(SLOTS):
+        high = source[k:k + 1, :].astype(jnp.int32) - 1
+        low = source[8 + k:9 + k, :].astype(jnp.int32)
+        filled = filled + jnp.where(high >= 0, 1.0, 0.0)
+        hot = one_hot(low, LANES)
+        found = jnp.dot(geometry, jnp.concatenate([hot, hot], axis=0), preferred_element_type=F32)
+        mine = lax.broadcasted_iota(jnp.int32, (blocks, 256), 0) == high
+        for q in range(9):
+            value = jnp.sum(jnp.where(mine, found[q * blocks:(q + 1) * blocks], 0.0), axis=0, keepdims=True)
+            for par in range(2):
+                start = par * 64 + q * SLOTS + k
+                col_ref[start:start + 1, :] = value[:, par * LANES:(par + 1) * LANES]
+    for par in range(2):
+        col_ref[par * 64 + 45:par * 64 + 46, :] = filled[:, par * LANES:(par + 1) * LANES]
+    out_ref[...] = col_ref[...].T
 
 
 def force_kernel(face_ref, seg_ref, out_ref, row_ref, wide_ref):
@@ -209,12 +212,16 @@
     uncovered = 6 * eroded.shape[0]
     vmem = pl.BlockSpec(memory_space=pltpu.VMEM)
 
-    azimuth, polar = seg_angle[:, 0], seg_angle[:, 1]
-    normal = jnp.stack(
-        [jnp.cos(azimuth) * jnp.sin(polar), jnp.sin(azimuth) * jnp.sin(polar), jnp.cos(polar)], axis=1)
-    segs = jnp.concatenate([seg_point, normal, jnp.zeros_like(seg_angle)], axis=1)
+    segs = pl.pallas_call(
+        segment_kernel,
+        out_shape=jax.ShapeDtypeStruct((seg_point.shape[0], 8, seg_point.shape[2]), F32),
+        in_specs=[vmem, vmem],
+        out_specs=vmem,
+        name="segments",
+    )(seg_point.transpose(1, 0, 2), seg_angle)
     segs = lax.all_to_all(segs, "bucket", 0, 0, tiled=True)
 
+    node_tiles = node_data.reshape(3, 8, blocks, LANES).transpose(0, 2, 1, 3).reshape(24 * blocks, LANES)
     packed, code = pl.pallas_call(
         pack_kernel,
         out_shape=(
@@ -224,20 +231,16 @@
         in_specs=[vmem, vmem, pl.BlockSpec(memory_space=pl.ANY)],
         out_specs=(vmem, vmem),
         scratch_shapes=[
-            pltpu.VMEM((24, faces), F32),
+            pltpu.VMEM((24 * blocks, LANES), F32),
             pltpu.VMEM((1, uncovered), jnp.int32),
+            pltpu.VMEM((LANES, LANES), F32),
+            pltpu.VMEM((2, uncovered), F32),
             pltpu.VMEM((LANES, uncovered), BF16),
-            pltpu.VMEM((uncovered, LANES), F32),
-            pltpu.VMEM((2, uncovered), F32),
-            pltpu.VMEM((2 * blocks, LANES), F32),
-            pltpu.VMEM((256, 8 * LANES), BF16),
-            pltpu.VMEM((256, 8 * LANES), BF16),
-            pltpu.VMEM((256, 256), F32),
-            pltpu.VMEM((120, LANES), F32),
+            pltpu.VMEM((9 * blocks, 2 * LANES), BF16),
             pltpu.SemaphoreType.DMA,
         ],
         name="pack",
-    )(eroded.reshape(-1, LANES), bucket_map.reshape(blocks, LANES), node_data)
+    )(eroded.reshape(-1, LANES), bucket_map.reshape(blocks, LANES), node_tiles)
 
     arrived = lax.all_to_all(packed.reshape(owners, 1, LANES), "elem", 0, 0, tiled=True)
 

time: 90.2 us -> 78.7 us (0.87)
  Pallas kernels: 24.6 us -> 15.9 us
  local copies, waits for them, and re-layouts: 1.46 us -> 0.09 us
  other arithmetic: 1.01 us -> 0 us
    pallas_call x1, Pallas kernels: 15.5 us -> 5.22 us  [local(): pl.pallas_call(pack_kernel, out_shape=(jax.ShapeDtypeStruct((owners, LANE...]
    pallas_call x0 -> x1, Pallas kernels: none -> 1.57 us  [local(): pl.pallas_call(segment_kernel, out_shape=jax.ShapeDtypeStruct((seg_point....]
    cos x1 -> x0, other arithmetic: 1.01 us -> none  [local(): jnp.cos(polar)]
  transfers between devices with their start and end apart: 1 -> 1, of which waited for: 0 -> 0; matrix products, arithmetic and copies ran while one was open for 0% -> 0% of each run, Pallas kernels for 17% -> 7%
where the time goes in v2:
time: 78.7 us; the launch traced here: 78.1 us
  blocking collectives  57.3 us (73%)
  Pallas kernels  15.9 us (20%)
  starting transfers between devices  4.83 us (6%)
    all_to_all x1, blocking collectives, local(): lax.all_to_all(packed.reshape(owners, 1, LANES), 'elem', 0, 0, tiled=True)  29.9 us
    all_to_all x1, blocking collectives, local(): lax.all_to_all(outgoing.reshape(owners, 1, LANES), 'elem', 0, 0, tiled=True)  18.6 us
    all_to_all x1, blocking collectives, local(): shared = lax.all_to_all(force, 'bucket', 0, 0, tiled=True)  8.8 us
    pallas_call x1, Pallas kernels, local(): pl.pallas_call(force_kernel, out_shape=jax.ShapeDtypeStruct((groups, 32,...  6.99 us
    pallas_call x1, Pallas kernels, local(): pl.pallas_call(pack_kernel, out_shape=(jax.ShapeDtypeStruct((owners, LANE...  5.22 us
    all_to_all x1, starting transfers between devices, local(): segs = lax.all_to_all(segs, 'bucket', 0, 0, tiled=True)  4.83 us
    pallas_call x1, Pallas kernels, local(): pl.pallas_call(pick_kernel, out_shape=jax.ShapeDtypeStruct((3, uncovered)...  2.1 us
  transfers between devices with their start and end apart: 1, of which 0 were waited for; matrix products, arithmetic and copies ran while one was open for 0% of the time, Pallas kernels for 7%

profile of v2, /device:TPU:1, one launch (start us, length us, event | category | flops | bytes accessed | tf_op | source)
XLA Modules:
  0.0 78.1 jit_solution(19266585954275023)
XLA Ops:
  0.0 1.6 %segments.1 = f32[8,8,128]{2,1,0:T(8,128)} custom-call(f32[3,8,128]{2,1,0:T(8,128)} %bitcast.24, f32[8,2,128]{2,1,0:T(2,128)} %angle_ref.1), custom_call_target="tpu_custom_call" | custom-call | tf_op jit(solution)/shard_map/segments/pallas_call | solution.py:215
  1.6 4.8 %all-to-all-start.1 = ((f32[8,8,128]{2,1,0:T(8,128)}), f32[8,8,128]{2,1,0:T(8,128)S(1)}, u32[]{:S(2)}, u32[]{:S(2)}) async-start(f32[8,8,128]{2,1,0:T(8,128)} %segments.1), calls=%async_computation.1 | async-start | bytes 65536 | tf_op jit(solution)/shard_map/all_to_all | solution.py:222
  6.4 5.2 %pack.1 = (f32[128,128]{1,0:T(8,128)}, s32[2,3072]{1,0:T(2,128)}) custom-call(s32[4,128]{1,0:T(4,128)} %bitcast.25, s32[96,128]{1,0:T(8,128)} %bitcast.23, f32[2304,128]{1,0:T(8,128)} %bitcast.18), custom_call_target="tpu_custom_call" | custom-call | tf_op jit(solution)/shard_map/pack/pallas_call | solution.py:225
  11.6 0.0 all-to-all-done.1.seg_ref
  11.6 0.0 copy-start
  11.7 29.9 %all_to_all.20 = f32[128,1,128]{2,1,0:T(1,128)} all-to-all(f32[128,1,128]{2,1,0:T(1,128)} %bitcast.22), channel_id=1, replica_groups=mesh['elem'=128,'bucket'=4] {'elem'}, dimensions={0} | all-to-all | bytes 131072 | tf_op jit(solution)/shard_map/all_to_all | solution.py:245
  41.5 0.0 copy-done
  41.5 7.0 %force.1 = f32[4,32,128]{2,1,0:T(8,128)} custom-call(f32[128,128]{1,0:T(8,128)} %bitcast.20, f32[8,8,128]{2,1,0:T(8,128)} %copy-done), custom_call_target="tpu_custom_call" | custom-call | tf_op jit(solution)/shard_map/force/pallas_call | solution.py:247
  48.5 8.8 %all_to_all.21 = f32[4,32,128]{2,1,0:T(8,128)S(1)} all-to-all(f32[4,32,128]{2,1,0:T(8,128)} %force.1), channel_id=1, replica_groups=mesh['elem'=128,'bucket'=4] {'bucket'}, dimensions={0} | all-to-all | bytes 131072 | tf_op jit(solution)/shard_map/all_to_all | solution.py:259
  57.3 0.1 copy.9
  57.4 18.6 %all_to_all.22 = f32[128,1,128]{2,1,0:T(1,128)} all-to-all(f32[128,1,128]{2,1,0:T(1,128)S(1)} %copy.9), channel_id=1, replica_groups=mesh['elem'=128,'bucket'=4] {'elem'}, dimensions={0} | all-to-all | bytes 131072 | tf_op jit(solution)/shard_map/all_to_all | solution.py:261
  76.0 2.1 %pick.1 = f32[3,3072]{1,0:T(4,128)} custom-call(f32[128,128]{1,0:T(8,128)} %bitcast.19, s32[2,3072]{1,0:T(2,128)} %get-tuple-element.8.code_ref), custom_call_target="tpu_custom_call" | custom-call | tf_op jit(solution)/shard_map/pick/pallas_call | solution.py:263
Async XLA Ops:
  1.6 10.1 %all-to-all-start.1 = ((f32[8,8,128]{2,1,0:T(8,128)}), f32[8,8,128]{2,1,0:T(8,128)S(1)}, u32[]{:S(2)}, u32[]{:S(2)}) async-start(f32[8,8,128]{2,1,0:T(8,128)} %segments.1), calls=%async_computation.1 | async-start | bytes 65536 | tf_op jit(solution)/shard_map/all_to_all | solution.py:222
  11.6 29.9 %copy-start = (f32[8,8,128]{2,1,0:T(8,128)}, f32[8,8,128]{2,1,0:T(8,128)S(1)}, u32[]{:S(2)}) copy-start(f32[8,8,128]{2,1,0:T(8,128)S(1)} %all-to-all-done.1.seg_ref) | copy-start | bytes 98308

commit v3 on v2

--- a/solution.py
+++ b/solution.py
@@ -19,16 +19,52 @@
     return jnp.where(numbers == row, 1.0, 0.0).astype(BF16)
 
 
-def segment_kernel(point_ref, angle_ref, seg_ref):
-    azimuth, polar = angle_ref[:, 0, :], angle_ref[:, 1, :]
+def pieces(value):
+    first = value.astype(BF16).astype(F32)
+    rest = value - first
+    second = rest.astype(BF16).astype(F32)
+    return first, second, rest - second
+
+
+def coefficient_kernel(seg_ref, left_ref, normal_ref, rows_ref):
+    rows_ref[...] = jnp.zeros(rows_ref.shape, F32)
+    log2e = 1.4426950408889634
+    order = (0, 0, 0, 1, 1, 2)
+    azimuth, polar = seg_ref[:, 3, :], seg_ref[:, 4, :]
     ring = jnp.sin(polar)
+    normal = [jnp.cos(azimuth) * ring, jnp.sin(azimuth) * ring, jnp.cos(polar)]
+    point = [seg_ref[:, i, :] for i in range(3)]
+    along = point[0] * normal[0] + point[1] * normal[1] + point[2] * normal[2]
+    square = point[0] * point[0] + point[1] * point[1] + point[2] * point[2]
+    terms = (
+        (0, [log2e * value for value in point]),
+        (0, [-value for value in normal]),
+        (6, [-DAMPING * value for value in normal]),
+        (3, normal),
+    )
+    split = [(start, [pieces(value) for value in values]) for start, values in terms]
+    constant = [pieces((-0.5 * log2e) * square), pieces(along)]
+    for term in range(4):
+        at = term * LANES
+        start, values = split[term]
+        for group, piece in enumerate(order):
+            for i in range(3):
+                rows_ref[:, at + group * 16 + start + i, :] = values[i][piece]
+        if term < 2:
+            for piece in range(3):
+                rows_ref[:, at + 96 + 6 + piece, :] = constant[term][piece]
+    for piece in range(3):
+        rows_ref[:, 96 + piece, :] = jnp.full_like(ring, -1.0)
+        rows_ref[:, 2 * LANES + 96 + 3 + piece, :] = jnp.full_like(ring, 1.0)
     for i in range(3):
-        seg_ref[:, i, :] = point_ref[i]
-    seg_ref[:, 3, :] = jnp.cos(azimuth) * ring
-    seg_ref[:, 4, :] = jnp.sin(azimuth) * ring
-    seg_ref[:, 5, :] = jnp.cos(polar)
-    seg_ref[:, 6, :] = jnp.zeros_like(ring)
-    seg_ref[:, 7, :] = jnp.zeros_like(ring)
+        normal_ref[:, i, :] = normal[i]
+    for i in range(3, 8):
+        normal_ref[:, i, :] = jnp.zeros_like(ring)
+    for g in range(seg_ref.shape[0]):
+        for term in range(4):
+            turned = rows_ref[g, term * LANES:(term + 1) * LANES, :].T.astype(BF16)
+            for half in range(2):
+                left_ref[g % 2, (g // 2) * 2 + half, term * 64:(term + 1) * 64, :] = turned[half * 64:(half + 1) * 64]
 
 
 def pack_kernel(eroded_ref, map_ref, node_hbm, out_ref, code_ref, node_ref, row_ref, col_ref, rank_ref, owner_hot,
@@ -136,50 +172,64 @@
         for q in range(9):
             value = jnp.sum(jnp.where(mine, found[q * blocks:(q + 1) * blocks], 0.0), axis=0, keepdims=True)
             for par in range(2):
-                start = par * 64 + q * SLOTS + k
+                start = par * 64 + k * 12 + q
                 col_ref[start:start + 1, :] = value[:, par * LANES:(par + 1) * LANES]
     for par in range(2):
-        col_ref[par * 64 + 45:par * 64 + 46, :] = filled[:, par * LANES:(par + 1) * LANES]
+        col_ref[par * 64 + 60:par * 64 + 61, :] = filled[:, par * LANES:(par + 1) * LANES]
     out_ref[...] = col_ref[...].T
 
 
-def force_kernel(face_ref, seg_ref, out_ref, row_ref, wide_ref):
+def force_kernel(face_ref, left_ref, seg_ref, out_ref, row_ref, right_ref, wide_ref):
     row_ref[...] = face_ref[...].T
     groups = seg_ref.shape[0] // 2
     for g in range(2 * groups):
         columns = seg_ref[g].T
-        for q in range(6):
-            wide_ref[g % 2, q, (g // 2) * LANES:(g // 2 + 1) * LANES, :] = jnp.broadcast_to(
-                columns[:, q:q + 1], (LANES, LANES))
+        for i in range(3):
+            wide_ref[g % 2, i, (g // 2) * LANES:(g // 2 + 1) * LANES, :] = jnp.broadcast_to(
+                columns[:, i:i + 1], (LANES, LANES))
     out_ref[...] = jnp.zeros(out_ref.shape, F32)
-    chunk = 64
+    half_log2e = 0.5 * 1.4426950408889634
+    number = lax.broadcasted_iota(jnp.int32, (16, LANES), 0)
     for par in range(2):
-        count = jnp.sum(row_ref[par * 64 + 45:par * 64 + 46, :], axis=1, keepdims=True)
-        stiff = jnp.broadcast_to(STIFFNESS * lax.rsqrt(jnp.maximum(count, 1.0)), (1, LANES))
+        count = jnp.sum(row_ref[par * 64 + 60:par * 64 + 61, :], axis=1, keepdims=True)
+        stiff = pieces(jnp.broadcast_to(STIFFNESS * lax.rsqrt(jnp.maximum(count, 1.0)), (1, LANES)))
         for k in range(SLOTS):
-            geo = [row_ref[par * 64 + q * SLOTS + k:par * 64 + q * SLOTS + k + 1, :] for q in range(9)]
-
-            def pairs(step, total, par=par, geo=geo, stiff=stiff):
-                at = pl.ds(pl.multiple_of(step * chunk, chunk), chunk)
-                seg = [wide_ref[par, q, at, :] for q in range(6)]
-                normal = seg[3:6]
-                off = [geo[i] - seg[i] for i in range(3)]
-                dist_sq = off[0] * off[0] + off[1] * off[1] + off[2] * off[2]
-                gap = off[0] * normal[0] + off[1] * normal[1] + off[2] * normal[2]
-                closing = geo[6] * normal[0] + geo[7] * normal[1] + geo[8] * normal[2]
-                projected = jnp.abs(geo[3] * normal[0] + geo[4] * normal[1] + geo[5] * normal[2])
-                weight = jnp.exp(-0.5 * dist_sq)
-                traction = weight * jnp.maximum(-gap, 0.0) * (stiff - DAMPING * closing) * projected
-                return tuple(
-                    total[i] + jnp.sum((traction * normal[i]).reshape(chunk // 8, 8, LANES), axis=0)
-                    for i in range(3))
-
-            zero = jnp.zeros((8, LANES), F32)
-            total = lax.fori_loop(0, wide_ref.shape[2] // chunk, pairs, (zero, zero, zero))
-            for i in range(3):
-                force = jnp.sum(total[i], axis=0, keepdims=True)
-                for x in range(out_ref.shape[0]):
-                    out_ref[x, i * 10 + par * SLOTS + k:i * 10 + par * SLOTS + k + 1, :] = force
+            start = par * 64 + k * 12
+            face = row_ref[start:start + 16, :]
+            center = [row_ref[start + i:start + i + 1, :] for i in range(3)]
+            square = pieces(half_log2e * (
+                center[0] * center[0] + center[1] * center[1] + center[2] * center[2]))
+            extra = jnp.where((number >= 6) & (number < 9), 1.0, 0.0)
+            for piece in range(3):
+                extra = jnp.where(number == piece, square[piece], extra)
+                extra = jnp.where(number == 3 + piece, stiff[piece], extra)
+            first, second, third = pieces(face)
+            blocks = (first, second, third, first, second, first, extra, jnp.zeros_like(extra))
+            for group, block in enumerate(blocks):
+                right_ref[par, group * 16:(group + 1) * 16, k * LANES:(k + 1) * LANES] = block.astype(BF16)
+    chunks = left_ref.shape[1]
+    for par in range(2):
+        for first in range(0, SLOTS, 2):
+            width = min(2, SLOTS - first)
+            right = right_ref[par, :, first * LANES:(first + width) * LANES]
+            total = [[jnp.zeros((8, LANES), F32) for _ in range(3)] for _ in range(width)]
+            for chunk in range(chunks):
+                found = jnp.dot(left_ref[par, chunk], right, preferred_element_type=F32)
+                normal = [wide_ref[par, i, chunk * 64:(chunk + 1) * 64, :] for i in range(3)]
+                for k in range(width):
+                    at = slice(k * LANES, (k + 1) * LANES)
+                    weight = jnp.exp2(found[0:64, at])
+                    traction = (weight * jnp.maximum(found[64:128, at], 0.0) * found[128:192, at]
+                                * jnp.abs(found[192:256, at]))
+                    for i in range(3):
+                        total[k][i] = total[k][i] + jnp.sum(
+                            (traction * normal[i]).reshape(8, 8, LANES), axis=0)
+            for k in range(width):
+                for i in range(3):
+                    force = jnp.sum(total[k][i], axis=0, keepdims=True)
+                    row = i * 10 + par * SLOTS + first + k
+                    for x in range(out_ref.shape[0]):
+                        out_ref[x, row:row + 1, :] = force
 
 
 def pick_kernel(force_ref, code_ref, out_ref, row_ref):
@@ -204,7 +254,7 @@
                 jnp.where(mine, found[i * 40:(i + 1) * 40], 0.0), axis=0, keepdims=True)
 
 
-def local(node_data, eroded, bucket_map, seg_point, seg_angle):
+def step(node_data, eroded, bucket_map, seg_point, seg_angle):
     owners = lax.axis_size("elem")
     groups = lax.axis_size("bucket")
     faces = node_data.shape[1]
@@ -212,13 +262,7 @@
     uncovered = 6 * eroded.shape[0]
     vmem = pl.BlockSpec(memory_space=pltpu.VMEM)
 
-    segs = pl.pallas_call(
-        segment_kernel,
-        out_shape=jax.ShapeDtypeStruct((seg_point.shape[0], 8, seg_point.shape[2]), F32),
-        in_specs=[vmem, vmem],
-        out_specs=vmem,
-        name="segments",
-    )(seg_point.transpose(1, 0, 2), seg_angle)
+    segs = jnp.concatenate([seg_point, seg_angle], axis=1)
     segs = lax.all_to_all(segs, "bucket", 0, 0, tiled=True)
 
     node_tiles = node_data.reshape(3, 8, blocks, LANES).transpose(0, 2, 1, 3).reshape(24 * blocks, LANES)
@@ -244,17 +288,30 @@
 
     arrived = lax.all_to_all(packed.reshape(owners, 1, LANES), "elem", 0, 0, tiled=True)
 
+    left, normal = pl.pallas_call(
+        coefficient_kernel,
+        out_shape=(
+            jax.ShapeDtypeStruct((2, 2 * groups, 256, LANES), BF16),
+            jax.ShapeDtypeStruct((2 * groups, 8, LANES), F32),
+        ),
+        in_specs=[vmem],
+        out_specs=(vmem, vmem),
+        scratch_shapes=[pltpu.VMEM((2 * groups, 4 * LANES, LANES), F32)],
+        name="coefficients",
+    )(segs)
+
     force = pl.pallas_call(
         force_kernel,
         out_shape=jax.ShapeDtypeStruct((groups, 32, LANES), F32),
-        in_specs=[vmem, vmem],
+        in_specs=[vmem, vmem, vmem],
         out_specs=vmem,
         scratch_shapes=[
             pltpu.VMEM((LANES, LANES), F32),
-            pltpu.VMEM((2, 6, groups * LANES, LANES), F32),
+            pltpu.VMEM((2, LANES, SLOTS * LANES), BF16),
+            pltpu.VMEM((2, 3, groups * LANES, LANES), F32),
         ],
         name="force",
-    )(arrived.reshape(owners, LANES), segs)
+    )(arrived.reshape(owners, LANES), left, normal)
 
     shared = lax.all_to_all(force, "bucket", 0, 0, tiled=True)
     outgoing = shared.reshape(groups * 32, owners).T
@@ -279,4 +336,4 @@
         P("elem", None, "bucket"),
     )
     out_specs = P(None, "elem")
-    return jax.shard_map(local, mesh=mesh, in_specs=in_specs, out_specs=out_specs, check_vma=False)
+    return jax.shard_map(step, mesh=mesh, in_specs=in_specs, out_specs=out_specs, check_vma=False)

time: 78.7 us -> 76.6 us (0.973)
  blocking collectives: 57.3 us -> 27.7 us
  starting transfers between devices: 4.83 us -> 22.9 us
  waiting for transfers between devices: 0.01 us -> 8.98 us
  Pallas kernels: 15.9 us -> 13.5 us
  local copies, waits for them, and re-layouts: 0.09 us -> 1.42 us
  other arithmetic: 0 us -> 1.32 us
    all_to_all x3 -> x2, blocking collectives: 57.3 us -> 27.7 us  [the longest x1 18.9 us: step(): lax.all_to_all(outgoing.reshape(owners, 1, LANES), 'elem', 0, 0, tiled=True)]
    all_to_all x1 -> x2, starting transfers between devices: 4.83 us -> 22.9 us  [the longest x1 18.1 us: step(): lax.all_to_all(packed.reshape(owners, 1, LANES), 'elem', 0, 0, tiled=True)]
    all_to_all x1 -> x2, waiting for transfers between devices: 0.01 us -> 8.98 us  [the longest x1 8.98 us: step(): lax.all_to_all(packed.reshape(owners, 1, LANES), 'elem', 0, 0, tiled=True)]
    pallas_call x4, Pallas kernels: 15.9 us -> 13.5 us  [the longest x1 5.21 us: step(): pl.pallas_call(pack_kernel, out_shape=(jax.ShapeDtypeStruct((owners, LANE...]
    unnamed x2 -> x5, local copies, waits for them, and re-layouts: 0.01 us -> 1.34 us
    concatenate x0 -> x1, other arithmetic: none -> 1.32 us  [step(): segs = jnp.concatenate([seg_point, seg_angle], axis=1)]
  transfers between devices with their start and end apart: 1 -> 2, of which waited for: 0 -> 1; matrix products, arithmetic and copies ran while one was open for 0% -> 0% of each run, Pallas kernels for 7% -> 10%
where the time goes in v3:
time: 76.6 us; the launch traced here: 75.9 us
  blocking collectives  27.7 us (36%)
  starting transfers between devices  22.9 us (30%)
  Pallas kernels  13.5 us (18%)
  waiting for transfers between devices  8.98 us (12%)
  local copies, waits for them, and re-layouts  1.42 us (2%)
  other arithmetic  1.32 us (2%)
    all_to_all x1, blocking collectives, step(): lax.all_to_all(outgoing.reshape(owners, 1, LANES), 'elem', 0, 0, tiled=True)  18.9 us
    all_to_all x1, starting transfers between devices, step(): lax.all_to_all(packed.reshape(owners, 1, LANES), 'elem', 0, 0, tiled=True)  18.1 us
    all_to_all x1, waiting for transfers between devices, step(): lax.all_to_all(packed.reshape(owners, 1, LANES), 'elem', 0, 0, tiled=True)  8.98 us
    all_to_all x1, blocking collectives, step(): shared = lax.all_to_all(force, 'bucket', 0, 0, tiled=True)  8.79 us
    pallas_call x1, Pallas kernels, step(): pl.pallas_call(pack_kernel, out_shape=(jax.ShapeDtypeStruct((owners, LANE...  5.21 us
    all_to_all x1, starting transfers between devices, step(): segs = lax.all_to_all(segs, 'bucket', 0, 0, tiled=True)  4.83 us
    pallas_call x1, Pallas kernels, step(): pl.pallas_call(force_kernel, out_shape=jax.ShapeDtypeStruct((groups, 32,...  3.78 us
    pallas_call x1, Pallas kernels, step(): pl.pallas_call(coefficient_kernel, out_shape=(jax.ShapeDtypeStruct((2, 2...  2.44 us
  transfers between devices with their start and end apart: 2, of which 1 were waited for; matrix products, arithmetic and copies ran while one was open for 0% of the time, Pallas kernels for 10%

profile of v3, /device:TPU:1, one launch (start us, length us, event | category | flops | bytes accessed | tf_op | source)
XLA Modules:
  0.0 75.9 jit_solution(10045174814799418331)
XLA Ops:
  0.0 0.7 copy.11
  0.7 1.3 %pad_maximum_fusion = f32[8,5,128]{2,1,0:T(8,128)} fusion(f32[8,2,128]{2,1,0:T(2,128)} %param.9, f32[8,3,128]{2,1,0:T(4,128)S(1)} %copy.11), kind=kLoop, calls=%fused_computation | loop fusion | flops 5120 | bytes 40960 | tf_op jit(solution)/shard_map/concatenate | solution.py:265
  2.0 4.8 %all-to-all-start.1 = ((f32[8,5,128]{2,1,0:T(8,128)}), f32[8,5,128]{2,1,0:T(8,128)S(1)}, u32[]{:S(2)}, u32[]{:S(2)}) async-start(f32[8,5,128]{2,1,0:T(8,128)} %pad_maximum_fusion), calls=%async_computation.1 | async-start | bytes 65536 | tf_op jit(solution)/shard_map/all_to_all | solution.py:266
  6.9 5.2 %pack.1 = (f32[128,128]{1,0:T(8,128)}, s32[2,3072]{1,0:T(2,128)}) custom-call(s32[4,128]{1,0:T(4,128)} %bitcast.23, s32[96,128]{1,0:T(8,128)} %bitcast.22, f32[2304,128]{1,0:T(8,128)} %bitcast.17), custom_call_target="tpu_custom_call" | custom-call | tf_op jit(solution)/shard_map/pack/pallas_call | solution.py:269
  12.1 0.0 all-to-all-done.1.seg_ref
  12.1 0.0 copy-start.1
  12.1 18.1 %all-to-all-start = ((f32[128,1,128]{2,1,0:T(1,128)}), f32[128,1,128]{2,1,0:T(1,128)S(1)}, u32[]{:S(2)}, u32[]{:S(2)}) async-start(f32[128,1,128]{2,1,0:T(1,128)} %bitcast.21), calls=%async_computation | async-start | bytes 131072 | tf_op jit(solution)/shard_map/all_to_all | solution.py:289
  30.2 0.0 copy-done.1
  30.2 2.4 %coefficients.1 = (bf16[2,8,256,128]{3,2,1,0:T(8,128)(2,1)}, f32[8,8,128]{2,1,0:T(8,128)}) custom-call(f32[8,5,128]{2,1,0:T(8,128)} %copy-done.1), custom_call_target="tpu_custom_call" | custom-call | tf_op jit(solution)/shard_map/coefficients/pallas_call | solution.py:291
  32.6 9.0 %all-to-all-done = f32[128,1,128]{2,1,0:T(1,128)S(1)} async-done(((f32[128,1,128]{2,1,0:T(1,128)}), f32[128,1,128]{2,1,0:T(1,128)S(1)}, u32[]{:S(2)}, u32[]{:S(2)}) %all-to-all-start) | async-done | bytes 65568 | tf_op jit(solution)/shard_map/all_to_all | solution.py:289
  41.6 0.0 copy-start
  41.6 0.6 copy-done
  42.2 3.8 %force.1 = f32[4,32,128]{2,1,0:T(8,128)} custom-call(f32[128,128]{1,0:T(8,128)} %bitcast.18, bf16[2,8,256,128]{3,2,1,0:T(8,128)(2,1)} %get-tuple-element.10.left_ref, f32[8,8,128]{2,1,0:T(8,128)} %get-tuple-element.11.seg_ref), custom_call_target="tpu_custom_call" | custom-call | tf_op jit(solution)/shard_map/force/pallas_call | solution.py:303
  46.0 8.8 %all_to_all.20 = f32[4,32,128]{2,1,0:T(8,128)S(1)} all-to-all(f32[4,32,128]{2,1,0:T(8,128)} %force.1), channel_id=1, replica_groups=mesh['elem'=128,'bucket'=4] {'bucket'}, dimensions={0} | all-to-all | bytes 131072 | tf_op jit(solution)/shard_map/all_to_all | solution.py:316
  54.8 0.1 copy.12
  54.9 18.9 %all_to_all.21 = f32[128,1,128]{2,1,0:T(1,128)} all-to-all(f32[128,1,128]{2,1,0:T(1,128)S(1)} %copy.12), channel_id=1, replica_groups=mesh['elem'=128,'bucket'=4] {'elem'}, dimensions={0} | all-to-all | bytes 131072 | tf_op jit(solution)/shard_map/all_to_all | solution.py:318
  73.8 2.1 %pick.1 = f32[3,3072]{1,0:T(4,128)} custom-call(f32[128,128]{1,0:T(8,128)} %bitcast.19, s32[2,3072]{1,0:T(2,128)} %get-tuple-element.12.code_ref), custom_call_target="tpu_custom_call" | custom-call | tf_op jit(solution)/shard_map/pick/pallas_call | solution.py:320
Async XLA Ops:
  2.0 10.1 %all-to-all-start.1 = ((f32[8,5,128]{2,1,0:T(8,128)}), f32[8,5,128]{2,1,0:T(8,128)S(1)}, u32[]{:S(2)}, u32[]{:S(2)}) async-start(f32[8,5,128]{2,1,0:T(8,128)} %pad_maximum_fusion), calls=%async_computation.1 | async-start | bytes 65536 | tf_op jit(solution)/shard_map/all_to_all | solution.py:266
  12.1 18.1 %copy-start.1 = (f32[8,5,128]{2,1,0:T(8,128)}, f32[8,5,128]{2,1,0:T(8,128)S(1)}, u32[]{:S(2)}) copy-start(f32[8,5,128]{2,1,0:T(8,128)S(1)} %all-to-all-done.1.seg_ref) | copy-start | bytes 61444
  12.1 29.5 %all-to-all-start = ((f32[128,1,128]{2,1,0:T(1,128)}), f32[128,1,128]{2,1,0:T(1,128)S(1)}, u32[]{:S(2)}, u32[]{:S(2)}) async-start(f32[128,1,128]{2,1,0:T(1,128)} %bitcast.21), calls=%async_computation | async-start | bytes 131072 | tf_op jit(solution)/shard_map/all_to_all | solution.py:289
  41.6 0.6 copy-start

commit v4 on v3

--- a/solution.py
+++ b/solution.py
@@ -14,9 +14,20 @@
 NT = (((1,), (1,)), ((), ()))
 
 
+def near(value):
+    return pltpu.with_memory_space_constraint(value, pltpu.VMEM)
+
+
 def one_hot(row, size):
     numbers = lax.broadcasted_iota(jnp.int32, (size, row.shape[1]), 0)
     return jnp.where(numbers == row, 1.0, 0.0).astype(BF16)
+
+
+def join_kernel(point_ref, angle_ref, out_ref):
+    for i in range(3):
+        out_ref[:, i, :] = point_ref[i]
+    for i in range(2):
+        out_ref[:, 3 + i, :] = angle_ref[:, i, :]
 
 
 def pieces(value):
@@ -262,15 +273,21 @@
     uncovered = 6 * eroded.shape[0]
     vmem = pl.BlockSpec(memory_space=pltpu.VMEM)
 
-    segs = jnp.concatenate([seg_point, seg_angle], axis=1)
+    segs = pl.pallas_call(
+        join_kernel,
+        out_shape=pltpu.VMEM((seg_point.shape[0], 5, seg_point.shape[2]), F32),
+        in_specs=[vmem, vmem],
+        out_specs=vmem,
+        name="join",
+    )(seg_point.transpose(1, 0, 2), seg_angle)
     segs = lax.all_to_all(segs, "bucket", 0, 0, tiled=True)
 
     node_tiles = node_data.reshape(3, 8, blocks, LANES).transpose(0, 2, 1, 3).reshape(24 * blocks, LANES)
     packed, code = pl.pallas_call(
         pack_kernel,
         out_shape=(
-            jax.ShapeDtypeStruct((owners, LANES), F32),
-            jax.ShapeDtypeStruct((2, uncovered), jnp.int32),
+            pltpu.VMEM((owners, LANES), F32),
+            pltpu.VMEM((2, uncovered), jnp.int32),
         ),
         in_specs=[vmem, vmem, pl.BlockSpec(memory_space=pl.ANY)],
         out_specs=(vmem, vmem),
@@ -291,18 +308,18 @@
     left, normal = pl.pallas_call(
         coefficient_kernel,
         out_shape=(
-            jax.ShapeDtypeStruct((2, 2 * groups, 256, LANES), BF16),
-            jax.ShapeDtypeStruct((2 * groups, 8, LANES), F32),
+            pltpu.VMEM((2, 2 * groups, 256, LANES), BF16),
+            pltpu.VMEM((2 * groups, 8, LANES), F32),
         ),
         in_specs=[vmem],
         out_specs=(vmem, vmem),
         scratch_shapes=[pltpu.VMEM((2 * groups, 4 * LANES, LANES), F32)],
         name="coefficients",
-    )(segs)
+    )(near(segs))
 
     force = pl.pallas_call(
         force_kernel,
-        out_shape=jax.ShapeDtypeStruct((groups, 32, LANES), F32),
+        out_shape=pltpu.VMEM((groups, 32, LANES), F32),
         in_specs=[vmem, vmem, vmem],
         out_specs=vmem,
         scratch_shapes=[
@@ -311,7 +328,7 @@
             pltpu.VMEM((2, 3, groups * LANES, LANES), F32),
         ],
         name="force",
-    )(arrived.reshape(owners, LANES), left, normal)
+    )(near(arrived.reshape(owners, LANES)), near(left), near(normal))
 
     shared = lax.all_to_all(force, "bucket", 0, 0, tiled=True)
     outgoing = shared.reshape(groups * 32, owners).T
@@ -324,7 +341,7 @@
         out_specs=vmem,
         scratch_shapes=[pltpu.VMEM((120, LANES), F32)],
         name="pick",
-    )(returned.reshape(owners, LANES), code)
+    )(near(returned.reshape(owners, LANES)), near(code))
 
 
 def solution(mesh):

time: 76.6 us -> 72.2 us (0.943)
  Pallas kernels: 13.5 us -> 11.2 us
  waiting for transfers between devices: 8.98 us -> 10.8 us
  local copies, waits for them, and re-layouts: 1.42 us -> 0.09 us
  other arithmetic: 1.32 us -> 0 us
  blocking collectives: 27.7 us -> 26.9 us
    all_to_all x1, waiting for transfers between devices: 8.98 us -> 10.8 us  [step(): lax.all_to_all(packed.reshape(owners, 1, LANES), 'elem', 0, 0, tiled=True)]
    pallas_call x3 -> x4, Pallas kernels: 11.4 us -> 9.94 us  [the longest x1 5.96 us: step(): pl.pallas_call(pack_kernel, out_shape=(pltpu.VMEM((owners, LANES), F32),...]
    unnamed x5 -> x0, local copies, waits for them, and re-layouts: 1.34 us -> none
    concatenate x1 -> x0, other arithmetic: 1.32 us -> none  [step(): segs = jnp.concatenate([seg_point, seg_angle], axis=1)]
    pallas_call x1, Pallas kernels: 2.1 us -> 1.26 us  [step(): pl.pallas_call(pick_kernel, out_shape=jax.ShapeDtypeStruct((3, uncovered)...]
    all_to_all x1, blocking collectives: 18.9 us -> 18.1 us  [step(): lax.all_to_all(outgoing.reshape(owners, 1, LANES), 'elem', 0, 0, tiled=True)]
  transfers between devices with their start and end apart: 2 -> 2, of which waited for: 1 -> 1; matrix products, arithmetic and copies ran while one was open for 0% -> 0% of each run, Pallas kernels for 10% -> 9%
where the time goes in v4:
time: 72.2 us; the launch traced here: 71.7 us
  blocking collectives  26.9 us (37%)
  starting transfers between devices  22.7 us (31%)
  Pallas kernels  11.2 us (16%)
  waiting for transfers between devices  10.8 us (15%)
    all_to_all x1, blocking collectives, step(): lax.all_to_all(outgoing.reshape(owners, 1, LANES), 'elem', 0, 0, tiled=True)  18.1 us
    all_to_all x1, starting transfers between devices, step(): lax.all_to_all(packed.reshape(owners, 1, LANES), 'elem', 0, 0, tiled=True)  17.9 us
    all_to_all x1, waiting for transfers between devices, step(): lax.all_to_all(packed.reshape(owners, 1, LANES), 'elem', 0, 0, tiled=True)  10.8 us
    all_to_all x1, blocking collectives, step(): shared = lax.all_to_all(force, 'bucket', 0, 0, tiled=True)  8.79 us
    pallas_call x1, Pallas kernels, step(): pl.pallas_call(pack_kernel, out_shape=(pltpu.VMEM((owners, LANES), F32),...  5.96 us
    all_to_all x1, starting transfers between devices, step(): segs = lax.all_to_all(segs, 'bucket', 0, 0, tiled=True)  4.83 us
    pallas_call x1, Pallas kernels, step(): pl.pallas_call(force_kernel, out_shape=pltpu.VMEM((groups, 32, LANES), F3...  1.94 us
  transfers between devices with their start and end apart: 2, of which 1 were waited for; matrix products, arithmetic and copies ran while one was open for 0% of the time, Pallas kernels for 9%

profile of v4, /device:TPU:1, one launch (start us, length us, event | category | flops | bytes accessed | tf_op | source)
XLA Modules:
  0.0 71.7 jit_solution(9242521124240103931)
XLA Ops:
  0.0 1.3 %join.1 = f32[8,5,128]{2,1,0:T(8,128)} custom-call(f32[3,8,128]{2,1,0:T(8,128)} %bitcast.23, f32[8,2,128]{2,1,0:T(2,128)} %angle_ref.1), custom_call_target="tpu_custom_call" | custom-call | tf_op jit(solution)/shard_map/join/pallas_call | solution.py:276
  1.3 4.8 %all-to-all-start.1 = ((f32[8,5,128]{2,1,0:T(8,128)}), f32[8,5,128]{2,1,0:T(8,128)S(1)}, u32[]{:S(2)}, u32[]{:S(2)}) async-start(f32[8,5,128]{2,1,0:T(8,128)} %join.1), calls=%async_computation.1 | async-start | bytes 65536 | tf_op jit(solution)/shard_map/all_to_all | solution.py:283
  6.2 6.0 %pack.1 = (f32[128,128]{1,0:T(8,128)}, s32[2,3072]{1,0:T(2,128)S(1)}) custom-call(s32[4,128]{1,0:T(4,128)} %bitcast.24, s32[96,128]{1,0:T(8,128)} %bitcast.22, f32[2304,128]{1,0:T(8,128)} %bitcast.20), custom_call_target="tpu_custom_call" | custom-call | tf_op jit(solution)/shard_map/pack/pallas_call | solution.py:286
  12.1 0.0 all-to-all-done.1.seg_ref
  12.1 17.9 %all-to-all-start = ((f32[128,1,128]{2,1,0:T(1,128)}), f32[128,1,128]{2,1,0:T(1,128)S(1)}, u32[]{:S(2)}, u32[]{:S(2)}) async-start(f32[128,1,128]{2,1,0:T(1,128)} %bitcast.6), calls=%async_computation | async-start | bytes 131072 | tf_op jit(solution)/shard_map/all_to_all | solution.py:306
  30.0 0.7 coefficients.1
  30.8 10.8 %all-to-all-done = f32[128,1,128]{2,1,0:T(1,128)S(1)} async-done(((f32[128,1,128]{2,1,0:T(1,128)}), f32[128,1,128]{2,1,0:T(1,128)S(1)}, u32[]{:S(2)}, u32[]{:S(2)}) %all-to-all-start) | async-done | bytes 65568 | tf_op jit(solution)/shard_map/all_to_all | solution.py:306
  41.5 1.9 %force.1 = f32[4,32,128]{2,1,0:T(8,128)S(1)} custom-call(f32[128,128]{1,0:T(8,128)S(1)} %bitcast.18, bf16[2,8,256,128]{3,2,1,0:T(8,128)(2,1)S(1)} %get-tuple-element.10.left_ref, f32[8,8,128]{2,1,0:T(8,128)S(1)} %get-tuple-element.11.seg_ref), custom_call_target="tpu_custom_call" | custom-call | tf_op jit(solution)/shard_map/force/pallas_call | solution.py:320
  43.5 8.8 %all_to_all.20 = f32[4,32,128]{2,1,0:T(8,128)S(1)} all-to-all(f32[4,32,128]{2,1,0:T(8,128)S(1)} %force.1), channel_id=1, replica_groups=mesh['elem'=128,'bucket'=4] {'bucket'}, dimensions={0} | all-to-all | bytes 131072 | tf_op jit(solution)/shard_map/all_to_all | solution.py:333
  52.3 0.1 copy.9
  52.3 18.1 %all_to_all.21 = f32[128,1,128]{2,1,0:T(1,128)S(1)} all-to-all(f32[128,1,128]{2,1,0:T(1,128)S(1)} %copy.9), channel_id=1, replica_groups=mesh['elem'=128,'bucket'=4] {'elem'}, dimensions={0} | all-to-all | bytes 131072 | tf_op jit(solution)/shard_map/all_to_all | solution.py:335
  70.5 1.3 %pick.1 = f32[3,3072]{1,0:T(4,128)} custom-call(f32[128,128]{1,0:T(8,128)S(1)} %bitcast.19, s32[2,3072]{1,0:T(2,128)S(1)} %get-tuple-element.12.code_ref), custom_call_target="tpu_custom_call" | custom-call | tf_op jit(solution)/shard_map/pick/pallas_call | solution.py:337
Async XLA Ops:
  1.3 10.8 %all-to-all-start.1 = ((f32[8,5,128]{2,1,0:T(8,128)}), f32[8,5,128]{2,1,0:T(8,128)S(1)}, u32[]{:S(2)}, u32[]{:S(2)}) async-start(f32[8,5,128]{2,1,0:T(8,128)} %join.1), calls=%async_computation.1 | async-start | bytes 65536 | tf_op jit(solution)/shard_map/all_to_all | solution.py:283
  12.1 29.4 %all-to-all-start = ((f32[128,1,128]{2,1,0:T(1,128)}), f32[128,1,128]{2,1,0:T(1,128)S(1)}, u32[]{:S(2)}, u32[]{:S(2)}) async-start(f32[128,1,128]{2,1,0:T(1,128)} %bitcast.6), calls=%async_computation | async-start | bytes 131072 | tf_op jit(solution)/shard_map/all_to_all | solution.py:306

commit v5 on v4

--- a/solution.py
+++ b/solution.py
@@ -23,7 +23,9 @@
     return jnp.where(numbers == row, 1.0, 0.0).astype(BF16)
 
 
-def join_kernel(point_ref, angle_ref, out_ref):
+def join_kernel(point_ref, angle_ref, eroded_ref, map_ref, out_ref, near_eroded_ref, near_map_ref):
+    near_eroded_ref[...] = eroded_ref[...]
+    near_map_ref[...] = map_ref[...]
     for i in range(3):
         out_ref[:, i, :] = point_ref[i]
     for i in range(2):
@@ -78,8 +80,8 @@
                 left_ref[g % 2, (g // 2) * 2 + half, term * 64:(term + 1) * 64, :] = turned[half * 64:(half + 1) * 64]
 
 
-def pack_kernel(eroded_ref, map_ref, node_hbm, out_ref, code_ref, node_ref, row_ref, col_ref, rank_ref, owner_hot,
-                geo_ref, sem):
+def pack_kernel(eroded_ref, map_ref, node_hbm, out_ref, code_ref, node_ref, row_ref, col_ref, other_ref, rank_ref,
+                owner_hot, geo_ref, sem):
     copy = pltpu.make_async_copy(node_hbm, node_ref, sem)
     copy.start()
     group = lax.axis_index("bucket")
@@ -118,6 +120,7 @@
         at = slice(t * LANES, (t + 1) * LANES)
         mine = rank_ref[0:1, at]
         other = jnp.broadcast_to(mine, (LANES, LANES)).T
+        other_ref[at, :] = other
         hit = jnp.where((other == mine) & earlier, 1.0, 0.0)
         rank_ref[1:2, at] = jnp.sum(hit, axis=0, keepdims=True)
         bucket = mine.astype(jnp.int32)
@@ -140,15 +143,20 @@
     inner = bucket & 7
     code_ref[0:1, :] = owner
     code_ref[1:2, :] = inner * SLOTS + rank
-    column = jnp.where((inner >> 1) == group, (inner & 1) * LANES + owner, -1)
-    source = jnp.zeros((16, 256), F32)
-    for c in range(count // step):
-        at = slice(c * step, (c + 1) * step)
+    lane = lax.broadcasted_iota(jnp.int32, (1, LANES), 1)
+    wanted = [(lane * 8 + group * 2 + par).astype(F32) for par in range(2)]
+    pair = 2 * LANES
+    sources = [jnp.zeros((16, 256), F32), jnp.zeros((16, 256), F32)]
+    numbers = lax.broadcasted_iota(jnp.int32, (16, pair), 0)
+    for c in range(count // pair):
+        at = slice(c * pair, (c + 1) * pair)
         face = row_ref[0:1, at]
-        numbers = lax.broadcasted_iota(jnp.int32, (16, step), 0)
         parts = jnp.where(numbers < 8, (face >> 7) + 1, face & (LANES - 1))
         left = jnp.where((numbers & 7) == rank[:, at], parts, 0).astype(F32).astype(BF16)
-        source = source + lax.dot_general(left, one_hot(column[:, at], 256), NT, preferred_element_type=F32)
+        other = other_ref[at, :]
+        right = jnp.concatenate([jnp.where(other == want, 1.0, 0.0).astype(BF16) for want in wanted], axis=1)
+        sources[c % 2] = sources[c % 2] + jnp.dot(left, right, preferred_element_type=F32)
+    source = sources[0] + sources[1]
 
     copy.wait()
     for g in range(blocks // 16):
@@ -171,20 +179,22 @@
             geo_ref[at, LANES:] = (value - first.astype(F32)).astype(BF16)
 
     col_ref[...] = jnp.zeros(col_ref.shape, F32)
-    geometry = geo_ref[...]
     filled = jnp.zeros((1, 256), F32)
     for k in range(SLOTS):
         high = source[k:k + 1, :].astype(jnp.int32) - 1
         low = source[8 + k:9 + k, :].astype(jnp.int32)
         filled = filled + jnp.where(high >= 0, 1.0, 0.0)
         hot = one_hot(low, LANES)
-        found = jnp.dot(geometry, jnp.concatenate([hot, hot], axis=0), preferred_element_type=F32)
+        hot = jnp.concatenate([hot, hot], axis=0)
         mine = lax.broadcasted_iota(jnp.int32, (blocks, 256), 0) == high
-        for q in range(9):
-            value = jnp.sum(jnp.where(mine, found[q * blocks:(q + 1) * blocks], 0.0), axis=0, keepdims=True)
-            for par in range(2):
-                start = par * 64 + k * 12 + q
-                col_ref[start:start + 1, :] = value[:, par * LANES:(par + 1) * LANES]
+        for start, end in ((0, 5), (5, 9)):
+            found = jnp.dot(geo_ref[start * blocks:end * blocks, :], hot, preferred_element_type=F32)
+            for q in range(start, end):
+                at = (q - start) * blocks
+                value = jnp.sum(jnp.where(mine, found[at:at + blocks], 0.0), axis=0, keepdims=True)
+                for par in range(2):
+                    row = par * 64 + k * 12 + q
+                    col_ref[row:row + 1, :] = value[:, par * LANES:(par + 1) * LANES]
     for par in range(2):
         col_ref[par * 64 + 60:par * 64 + 61, :] = filled[:, par * LANES:(par + 1) * LANES]
     out_ref[...] = col_ref[...].T
@@ -223,7 +233,7 @@
         for first in range(0, SLOTS, 2):
             width = min(2, SLOTS - first)
             right = right_ref[par, :, first * LANES:(first + width) * LANES]
-            total = [[jnp.zeros((8, LANES), F32) for _ in range(3)] for _ in range(width)]
+            total = [[jnp.zeros((8, LANES), F32) for i in range(3)] for k in range(width)]
             for chunk in range(chunks):
                 found = jnp.dot(left_ref[par, chunk], right, preferred_element_type=F32)
                 normal = [wide_ref[par, i, chunk * 64:(chunk + 1) * 64, :] for i in range(3)]
@@ -250,22 +260,19 @@
             row_ref[i * 40 + x * 10:i * 40 + x * 10 + 10, :] = turned[x * 32 + i * 10:x * 32 + i * 10 + 10, :]
     value = row_ref[...]
     first = value.astype(BF16)
-    second = (value - first.astype(F32)).astype(BF16)
-    left = jnp.concatenate([first.astype(F32), second.astype(F32)], axis=0).astype(BF16)
-    rows = value.shape[0]
+    left = jnp.concatenate([first, (value - first.astype(F32)).astype(BF16)], axis=1)
     step = 512
     for c in range(out_ref.shape[1] // step):
         at = slice(c * step, (c + 1) * step)
         hot = one_hot(code_ref[0:1, at], LANES)
-        both = jnp.dot(left, hot, preferred_element_type=F32)
-        found = both[:rows] + both[rows:]
+        found = jnp.dot(left, jnp.concatenate([hot, hot], axis=0), preferred_element_type=F32)
         mine = lax.broadcasted_iota(jnp.int32, (40, step), 0) == code_ref[1:2, at]
         for i in range(3):
             out_ref[i:i + 1, at] = jnp.sum(
                 jnp.where(mine, found[i * 40:(i + 1) * 40], 0.0), axis=0, keepdims=True)
 
 
-def step(node_data, eroded, bucket_map, seg_point, seg_angle):
+def local(node_data, eroded, bucket_map, seg_point, seg_angle):
     owners = lax.axis_size("elem")
     groups = lax.axis_size("bucket")
     faces = node_data.shape[1]
@@ -273,13 +280,17 @@
     uncovered = 6 * eroded.shape[0]
     vmem = pl.BlockSpec(memory_space=pltpu.VMEM)
 
-    segs = pl.pallas_call(
+    segs, near_eroded, near_map = pl.pallas_call(
         join_kernel,
-        out_shape=pltpu.VMEM((seg_point.shape[0], 5, seg_point.shape[2]), F32),
-        in_specs=[vmem, vmem],
-        out_specs=vmem,
+        out_shape=(
+            pltpu.VMEM((seg_point.shape[0], 5, seg_point.shape[2]), F32),
+            pltpu.VMEM((uncovered // 6 // LANES, LANES), jnp.int32),
+            pltpu.VMEM((blocks, LANES), jnp.int32),
+        ),
+        in_specs=[vmem, vmem, vmem, vmem],
+        out_specs=(vmem, vmem, vmem),
         name="join",
-    )(seg_point.transpose(1, 0, 2), seg_angle)
+    )(seg_point.transpose(1, 0, 2), seg_angle, eroded.reshape(-1, LANES), bucket_map.reshape(blocks, LANES))
     segs = lax.all_to_all(segs, "bucket", 0, 0, tiled=True)
 
     node_tiles = node_data.reshape(3, 8, blocks, LANES).transpose(0, 2, 1, 3).reshape(24 * blocks, LANES)
@@ -295,27 +306,30 @@
             pltpu.VMEM((24 * blocks, LANES), F32),
             pltpu.VMEM((1, uncovered), jnp.int32),
             pltpu.VMEM((LANES, LANES), F32),
+            pltpu.VMEM((uncovered, LANES), F32),
             pltpu.VMEM((2, uncovered), F32),
             pltpu.VMEM((LANES, uncovered), BF16),
             pltpu.VMEM((9 * blocks, 2 * LANES), BF16),
             pltpu.SemaphoreType.DMA,
         ],
         name="pack",
-    )(eroded.reshape(-1, LANES), bucket_map.reshape(blocks, LANES), node_tiles)
-
-    arrived = lax.all_to_all(packed.reshape(owners, 1, LANES), "elem", 0, 0, tiled=True)
-
-    left, normal = pl.pallas_call(
-        coefficient_kernel,
-        out_shape=(
-            pltpu.VMEM((2, 2 * groups, 256, LANES), BF16),
-            pltpu.VMEM((2 * groups, 8, LANES), F32),
-        ),
-        in_specs=[vmem],
-        out_specs=(vmem, vmem),
-        scratch_shapes=[pltpu.VMEM((2 * groups, 4 * LANES, LANES), F32)],
-        name="coefficients",
-    )(near(segs))
+    )(near(near_eroded), near(near_map), node_tiles)
+
+    with jax.named_scope("dispatch"):
+        arrived = lax.all_to_all(packed.reshape(owners, 1, LANES), "elem", 0, 0, tiled=True)
+
+    with jax.named_scope("coefficients"):
+        left, normal = pl.pallas_call(
+            coefficient_kernel,
+            out_shape=(
+                pltpu.VMEM((2, 2 * groups, 256, LANES), BF16),
+                pltpu.VMEM((2 * groups, 8, LANES), F32),
+            ),
+            in_specs=[vmem],
+            out_specs=(vmem, vmem),
+            scratch_shapes=[pltpu.VMEM((2 * groups, 4 * LANES, LANES), F32)],
+            name="coefficients",
+        )(near(segs))
 
     force = pl.pallas_call(
         force_kernel,
@@ -353,4 +367,4 @@
         P("elem", None, "bucket"),
     )
     out_specs = P(None, "elem")
-    return jax.shard_map(step, mesh=mesh, in_specs=in_specs, out_specs=out_specs, check_vma=False)
+    return jax.shard_map(local, mesh=mesh, in_specs=in_specs, out_specs=out_specs, check_vma=False)

time: 72.2 us -> 70.9 us (0.982)
  Pallas kernels: 11.2 us -> 9.99 us
  starting transfers between devices: 22.7 us -> 23.5 us
    pallas_call x5, Pallas kernels: 11.2 us -> 9.99 us  [the longest x1 4.66 us: local(): pl.pallas_call(pack_kernel, out_shape=(pltpu.VMEM((owners, LANES), F32),...]
    all_to_all x2, starting transfers between devices: 22.7 us -> 23.5 us  [the longest x1 18.6 us: local(): lax.all_to_all(packed.reshape(owners, 1, LANES), 'elem', 0, 0, tiled=True)]
    all_to_all x2, blocking collectives: 26.9 us -> 26.2 us  [the longest x1 18.1 us: local(): lax.all_to_all(outgoing.reshape(owners, 1, LANES), 'elem', 0, 0, tiled=True)]
  transfers between devices with their start and end apart: 2 -> 2, of which waited for: 1 -> 1; matrix products, arithmetic and copies ran while one was open for 0% -> 0% of each run, Pallas kernels for 9% -> 8%
where the time goes in v5:
time: 70.9 us; the launch traced here: 70.5 us
  blocking collectives  26.2 us (37%)
  starting transfers between devices  23.5 us (33%)
  waiting for transfers between devices  10.8 us (15%)
  Pallas kernels  9.99 us (14%)
    all_to_all x1, starting transfers between devices, local(): lax.all_to_all(packed.reshape(owners, 1, LANES), 'elem', 0, 0, tiled=True)  18.6 us
    all_to_all x1, blocking collectives, local(): lax.all_to_all(outgoing.reshape(owners, 1, LANES), 'elem', 0, 0, tiled=True)  18.1 us
    all_to_all x1, waiting for transfers between devices, local(): lax.all_to_all(packed.reshape(owners, 1, LANES), 'elem', 0, 0, tiled=True)  10.8 us
    all_to_all x1, blocking collectives, local(): shared = lax.all_to_all(force, 'bucket', 0, 0, tiled=True)  8.03 us
    all_to_all x1, starting transfers between devices, local(): segs = lax.all_to_all(segs, 'bucket', 0, 0, tiled=True)  4.83 us
    pallas_call x1, Pallas kernels, local(): pl.pallas_call(pack_kernel, out_shape=(pltpu.VMEM((owners, LANES), F32),...  4.66 us
    pallas_call x1, Pallas kernels, local(): pl.pallas_call(force_kernel, out_shape=pltpu.VMEM((groups, 32, LANES), F3...  1.94 us
    pallas_call x1, Pallas kernels, local(): pl.pallas_call(join_kernel, out_shape=(pltpu.VMEM((seg_point.shape[0], 5,...  1.48 us
  transfers between devices with their start and end apart: 2, of which 1 were waited for; matrix products, arithmetic and copies ran while one was open for 0% of the time, Pallas kernels for 8%

profile of v5, /device:TPU:1, one launch (start us, length us, event | category | flops | bytes accessed | tf_op | source)
XLA Modules:
  0.0 70.5 jit_solution(13921978875146073401)
XLA Ops:
  0.0 1.5 %join.1 = (f32[8,5,128]{2,1,0:T(8,128)}, s32[4,128]{1,0:T(4,128)S(1)}, s32[96,128]{1,0:T(8,128)S(1)}) custom-call(f32[3,8,128]{2,1,0:T(8,128)} %bitcast.23, f32[8,2,128]{2,1,0:T(2,128)} %angle_ref.1, s32[4,128]{1,0:T(4,128)} %bitcast.24, s32[96,128]{1,0:T(8,128)} %bitcast.22), custom_call_target="tpu_custom_call" | custom-call | tf_op jit(solution)/shard_map/join/pallas_call | solution.py:283
  1.5 4.8 %all-to-all-start.1 = ((f32[8,5,128]{2,1,0:T(8,128)}), f32[8,5,128]{2,1,0:T(8,128)S(1)}, u32[]{:S(2)}, u32[]{:S(2)}) async-start(f32[8,5,128]{2,1,0:T(8,128)} %get-tuple-element.15), calls=%async_computation.1 | async-start | bytes 65536 | tf_op jit(solution)/shard_map/all_to_all | solution.py:294
  6.3 4.7 %pack.1 = (f32[128,128]{1,0:T(8,128)}, s32[2,3072]{1,0:T(2,128)S(1)}) custom-call(s32[4,128]{1,0:T(4,128)S(1)} %get-tuple-element.12.eroded_ref, s32[96,128]{1,0:T(8,128)S(1)} %get-tuple-element.13.map_ref, f32[2304,128]{1,0:T(8,128)} %bitcast.20), custom_call_target="tpu_custom_call" | custom-call | tf_op jit(solution)/shard_map/pack/pallas_call | solution.py:297
  11.0 0.0 all-to-all-done.1.seg_ref
  11.0 18.6 %all-to-all-start = ((f32[128,1,128]{2,1,0:T(1,128)}), f32[128,1,128]{2,1,0:T(1,128)S(1)}, u32[]{:S(2)}, u32[]{:S(2)}) async-start(f32[128,1,128]{2,1,0:T(1,128)} %bitcast.7), calls=%async_computation | async-start | bytes 131072 | tf_op jit(solution)/shard_map/dispatch/all_to_all | solution.py:319
  29.6 0.7 %coefficients.1 = (bf16[2,8,256,128]{3,2,1,0:T(8,128)(2,1)S(1)}, f32[8,8,128]{2,1,0:T(8,128)S(1)}) custom-call(f32[8,5,128]{2,1,0:T(8,128)S(1)} %all-to-all-done.1.seg_ref), custom_call_target="tpu_custom_call" | custom-call | tf_op jit(solution)/shard_map/coefficients/coefficients/pallas_call | solution.py:322
  30.4 10.8 %all-to-all-done = f32[128,1,128]{2,1,0:T(1,128)S(1)} async-done(((f32[128,1,128]{2,1,0:T(1,128)}), f32[128,1,128]{2,1,0:T(1,128)S(1)}, u32[]{:S(2)}, u32[]{:S(2)}) %all-to-all-start) | async-done | bytes 65568 | tf_op jit(solution)/shard_map/dispatch/all_to_all | solution.py:319
  41.1 1.9 %force.1 = f32[4,32,128]{2,1,0:T(8,128)S(1)} custom-call(f32[128,128]{1,0:T(8,128)S(1)} %bitcast.18, bf16[2,8,256,128]{3,2,1,0:T(8,128)(2,1)S(1)} %get-tuple-element.16.left_ref, f32[8,8,128]{2,1,0:T(8,128)S(1)} %get-tuple-element.17.seg_ref), custom_call_target="tpu_custom_call" | custom-call | tf_op jit(solution)/shard_map/force/pallas_call | solution.py:334
  43.0 8.0 %all_to_all.20 = f32[4,32,128]{2,1,0:T(8,128)S(1)} all-to-all(f32[4,32,128]{2,1,0:T(8,128)S(1)} %force.1), channel_id=1, replica_groups=mesh['elem'=128,'bucket'=4] {'bucket'}, dimensions={0} | all-to-all | bytes 131072 | tf_op jit(solution)/shard_map/all_to_all | solution.py:347
  51.1 0.1 copy.9
  51.2 18.1 %all_to_all.21 = f32[128,1,128]{2,1,0:T(1,128)S(1)} all-to-all(f32[128,1,128]{2,1,0:T(1,128)S(1)} %copy.9), channel_id=1, replica_groups=mesh['elem'=128,'bucket'=4] {'elem'}, dimensions={0} | all-to-all | bytes 131072 | tf_op jit(solution)/shard_map/all_to_all | solution.py:349
  69.3 1.2 %pick.1 = f32[3,3072]{1,0:T(4,128)} custom-call(f32[128,128]{1,0:T(8,128)S(1)} %bitcast.19, s32[2,3072]{1,0:T(2,128)S(1)} %get-tuple-element.18.code_ref), custom_call_target="tpu_custom_call" | custom-call | tf_op jit(solution)/shard_map/pick/pallas_call | solution.py:351
Async XLA Ops:
  1.5 9.5 %all-to-all-start.1 = ((f32[8,5,128]{2,1,0:T(8,128)}), f32[8,5,128]{2,1,0:T(8,128)S(1)}, u32[]{:S(2)}, u32[]{:S(2)}) async-start(f32[8,5,128]{2,1,0:T(8,128)} %get-tuple-element.15), calls=%async_computation.1 | async-start | bytes 65536 | tf_op jit(solution)/shard_map/all_to_all | solution.py:294
  11.0 30.1 %all-to-all-start = ((f32[128,1,128]{2,1,0:T(1,128)}), f32[128,1,128]{2,1,0:T(1,128)S(1)}, u32[]{:S(2)}, u32[]{:S(2)}) async-start(f32[128,1,128]{2,1,0:T(1,128)} %bitcast.7), calls=%async_computation | async-start | bytes 131072 | tf_op jit(solution)/shard_map/dispatch/all_to_all | solution.py:319

commit v6 on v5

--- a/solution.py
+++ b/solution.py
@@ -3,7 +3,7 @@
 from jax import lax
 from jax.experimental import pallas as pl
 from jax.experimental.pallas import tpu as pltpu
-from jax.sharding import PartitionSpec as P
+from jax.sharding import Mesh, PartitionSpec as P
 
 STIFFNESS = 20.0
 DAMPING = 0.5
@@ -141,8 +141,8 @@
     rank = rank_ref[1:2, :].astype(jnp.int32)
     owner = bucket >> 3
     inner = bucket & 7
-    code_ref[0:1, :] = owner
-    code_ref[1:2, :] = inner * SLOTS + rank
+    code_ref[0:1, :] = (owner & (LANES - 2)) + (inner & 1)
+    code_ref[1:2, :] = ((owner & 1) * 4 + (inner >> 1)) * SLOTS + rank
     lane = lax.broadcasted_iota(jnp.int32, (1, LANES), 1)
     wanted = [(lane * 8 + group * 2 + par).astype(F32) for par in range(2)]
     pair = 2 * LANES
@@ -201,14 +201,14 @@
 
 
 def force_kernel(face_ref, left_ref, seg_ref, out_ref, row_ref, right_ref, wide_ref):
-    row_ref[...] = face_ref[...].T
+    half = LANES // 2
+    row_ref[...] = jnp.concatenate([face_ref[pl.ds(core, half, stride=2), :] for core in range(2)], axis=0).T
     groups = seg_ref.shape[0] // 2
     for g in range(2 * groups):
         columns = seg_ref[g].T
         for i in range(3):
             wide_ref[g % 2, i, (g // 2) * LANES:(g // 2 + 1) * LANES, :] = jnp.broadcast_to(
                 columns[:, i:i + 1], (LANES, LANES))
-    out_ref[...] = jnp.zeros(out_ref.shape, F32)
     half_log2e = 0.5 * 1.4426950408889634
     number = lax.broadcasted_iota(jnp.int32, (16, LANES), 0)
     for par in range(2):
@@ -247,17 +247,22 @@
                             (traction * normal[i]).reshape(8, 8, LANES), axis=0)
             for k in range(width):
                 for i in range(3):
-                    force = jnp.sum(total[k][i], axis=0, keepdims=True)
-                    row = i * 10 + par * SLOTS + first + k
-                    for x in range(out_ref.shape[0]):
-                        out_ref[x, row:row + 1, :] = force
+                    row = par * 16 + i * SLOTS + first + k
+                    row_ref[row:row + 1, :] = jnp.sum(total[k][i], axis=0, keepdims=True)
+        row_ref[par * 16 + 15:par * 16 + 16, :] = jnp.zeros((1, LANES), F32)
+    for core in range(2):
+        at = slice(core * half, (core + 1) * half)
+        both = jnp.concatenate([row_ref[0:16, at], row_ref[16:32, at]], axis=1)
+        for x in range(4):
+            out_ref[core * 4 + x] = both
 
 
 def pick_kernel(force_ref, code_ref, out_ref, row_ref):
     turned = force_ref[...].T
-    for x in range(4):
+    for g in range(8):
         for i in range(3):
-            row_ref[i * 40 + x * 10:i * 40 + x * 10 + 10, :] = turned[x * 32 + i * 10:x * 32 + i * 10 + 10, :]
+            to, start = i * 40 + g * SLOTS, g * 16 + i * SLOTS
+            row_ref[to:to + SLOTS, :] = turned[start:start + SLOTS, :]
     value = row_ref[...]
     first = value.astype(BF16)
     left = jnp.concatenate([first, (value - first.astype(F32)).astype(BF16)], axis=1)
@@ -273,7 +278,7 @@
 
 
 def local(node_data, eroded, bucket_map, seg_point, seg_angle):
-    owners = lax.axis_size("elem")
+    owners = lax.axis_size(("chip", "core"))
     groups = lax.axis_size("bucket")
     faces = node_data.shape[1]
     blocks = faces // LANES
@@ -316,7 +321,7 @@
     )(near(near_eroded), near(near_map), node_tiles)
 
     with jax.named_scope("dispatch"):
-        arrived = lax.all_to_all(packed.reshape(owners, 1, LANES), "elem", 0, 0, tiled=True)
+        arrived = lax.all_to_all(packed.reshape(owners, 1, LANES), ("chip", "core"), 0, 0, tiled=True)
 
     with jax.named_scope("coefficients"):
         left, normal = pl.pallas_call(
@@ -333,7 +338,7 @@
 
     force = pl.pallas_call(
         force_kernel,
-        out_shape=pltpu.VMEM((groups, 32, LANES), F32),
+        out_shape=pltpu.VMEM((2 * groups, 16, LANES), F32),
         in_specs=[vmem, vmem, vmem],
         out_specs=vmem,
         scratch_shapes=[
@@ -344,9 +349,9 @@
         name="force",
     )(near(arrived.reshape(owners, LANES)), near(left), near(normal))
 
-    shared = lax.all_to_all(force, "bucket", 0, 0, tiled=True)
-    outgoing = shared.reshape(groups * 32, owners).T
-    returned = lax.all_to_all(outgoing.reshape(owners, 1, LANES), "elem", 0, 0, tiled=True)
+    shared = lax.all_to_all(force, ("core", "bucket"), 0, 0, tiled=True)
+    outgoing = shared.reshape(groups * 32, 2, owners // 2).transpose(2, 1, 0)
+    returned = lax.all_to_all(outgoing, "chip", 0, 0, tiled=True)
 
     return pl.pallas_call(
         pick_kernel,
@@ -359,12 +364,7 @@
 
 
 def solution(mesh):
-    in_specs = (
-        P(None, "elem"),
-        P("elem"),
-        P("elem"),
-        P("elem", None, "bucket"),
-        P("elem", None, "bucket"),
-    )
-    out_specs = P(None, "elem")
-    return jax.shard_map(local, mesh=mesh, in_specs=in_specs, out_specs=out_specs, check_vma=False)
+    split = Mesh(mesh.devices.reshape(-1, 2, mesh.shape["bucket"]), ("chip", "core", "bucket"))
+    elem = ("chip", "core")
+    in_specs = (P(None, elem), P(elem), P(elem), P(elem, None, "bucket"), P(elem, None, "bucket"))
+    return jax.shard_map(local, mesh=split, in_specs=in_specs, out_specs=P(None, elem), check_vma=False)

time: 70.9 us -> 69.2 us (0.976)
  blocking collectives: 26.2 us -> 24.3 us
    all_to_all x2, blocking collectives: 26.2 us -> 24.3 us  [the longest x1 14.9 us: local(): returned = lax.all_to_all(outgoing, 'chip', 0, 0, tiled=True)]
where the time goes in v6:
time: 69.2 us; the launch traced here: 68.8 us
  blocking collectives  24.3 us (35%)
  starting transfers between devices  23.5 us (34%)
  waiting for transfers between devices  10.8 us (16%)
  Pallas kernels  10 us (14%)
    all_to_all x1, starting transfers between devices, local(): lax.all_to_all(packed.reshape(owners, 1, LANES), ('chip', 'core'), 0, 0,...  18.6 us
    all_to_all x1, blocking collectives, local(): returned = lax.all_to_all(outgoing, 'chip', 0, 0, tiled=True)  14.9 us
    all_to_all x1, waiting for transfers between devices, local(): lax.all_to_all(packed.reshape(owners, 1, LANES), ('chip', 'core'), 0, 0,...  10.8 us
    all_to_all x1, blocking collectives, local(): shared = lax.all_to_all(force, ('core', 'bucket'), 0, 0, tiled=True)  9.4 us
    all_to_all x1, starting transfers between devices, local(): segs = lax.all_to_all(segs, 'bucket', 0, 0, tiled=True)  4.83 us
    pallas_call x1, Pallas kernels, local(): pl.pallas_call(pack_kernel, out_shape=(pltpu.VMEM((owners, LANES), F32),...  4.66 us
    pallas_call x1, Pallas kernels, local(): pl.pallas_call(force_kernel, out_shape=pltpu.VMEM((2 * groups, 16, LANES)...  1.98 us
    pallas_call x1, Pallas kernels, local(): pl.pallas_call(join_kernel, out_shape=(pltpu.VMEM((seg_point.shape[0], 5,...  1.48 us
  transfers between devices with their start and end apart: 2, of which 1 were waited for; matrix products, arithmetic and copies ran while one was open for 0% of the time, Pallas kernels for 8%

profile of v6, /device:TPU:1, one launch (start us, length us, event | category | flops | bytes accessed | tf_op | source)
XLA Modules:
  0.0 68.8 jit_solution(14412463242942176169)
XLA Ops:
  0.0 1.5 %join.1 = (f32[8,5,128]{2,1,0:T(8,128)}, s32[4,128]{1,0:T(4,128)S(1)}, s32[96,128]{1,0:T(8,128)S(1)}) custom-call(f32[3,8,128]{2,1,0:T(8,128)} %bitcast.19, f32[8,2,128]{2,1,0:T(2,128)} %angle_ref.1, s32[4,128]{1,0:T(4,128)} %bitcast.20, s32[96,128]{1,0:T(8,128)} %bitcast.18), custom_call_target="tpu_custom_call" | custom-call | tf_op jit(solution)/shard_map/join/pallas_call | solution.py:288
  1.5 4.8 %all-to-all-start.1 = ((f32[8,5,128]{2,1,0:T(8,128)}), f32[8,5,128]{2,1,0:T(8,128)S(1)}, u32[]{:S(2)}, u32[]{:S(2)}) async-start(f32[8,5,128]{2,1,0:T(8,128)} %get-tuple-element.15), calls=%async_computation.1 | async-start | bytes 65536 | tf_op jit(solution)/shard_map/all_to_all | solution.py:299
  6.3 4.7 %pack.1 = (f32[128,128]{1,0:T(8,128)}, s32[2,3072]{1,0:T(2,128)S(1)}) custom-call(s32[4,128]{1,0:T(4,128)S(1)} %get-tuple-element.12.eroded_ref, s32[96,128]{1,0:T(8,128)S(1)} %get-tuple-element.13.map_ref, f32[2304,128]{1,0:T(8,128)} %bitcast.16), custom_call_target="tpu_custom_call" | custom-call | tf_op jit(solution)/shard_map/pack/pallas_call | solution.py:302
  11.0 0.0 all-to-all-done.1.seg_ref
  11.0 18.6 %all-to-all-start = ((f32[128,1,128]{2,1,0:T(1,128)}), f32[128,1,128]{2,1,0:T(1,128)S(1)}, u32[]{:S(2)}, u32[]{:S(2)}) async-start(f32[128,1,128]{2,1,0:T(1,128)} %bitcast.7), calls=%async_computation | async-start | bytes 131072 | tf_op jit(solution)/shard_map/dispatch/all_to_all | solution.py:324
  29.6 0.7 %coefficients.1 = (bf16[2,8,256,128]{3,2,1,0:T(8,128)(2,1)S(1)}, f32[8,8,128]{2,1,0:T(8,128)S(1)}) custom-call(f32[8,5,128]{2,1,0:T(8,128)S(1)} %all-to-all-done.1.seg_ref), custom_call_target="tpu_custom_call" | custom-call | tf_op jit(solution)/shard_map/coefficients/coefficients/pallas_call | solution.py:327
  30.4 10.8 %all-to-all-done = f32[128,1,128]{2,1,0:T(1,128)S(1)} async-done(((f32[128,1,128]{2,1,0:T(1,128)}), f32[128,1,128]{2,1,0:T(1,128)S(1)}, u32[]{:S(2)}, u32[]{:S(2)}) %all-to-all-start) | async-done | bytes 65568 | tf_op jit(solution)/shard_map/dispatch/all_to_all | solution.py:324
  41.1 2.0 %force.1 = f32[8,16,128]{2,1,0:T(8,128)S(1)} custom-call(f32[128,128]{1,0:T(8,128)S(1)} %bitcast.14, bf16[2,8,256,128]{3,2,1,0:T(8,128)(2,1)S(1)} %get-tuple-element.16.left_ref, f32[8,8,128]{2,1,0:T(8,128)S(1)} %get-tuple-element.17.seg_ref), custom_call_target="tpu_custom_call" | custom-call | tf_op jit(solution)/shard_map/force/pallas_call | solution.py:339
  43.1 9.4 %all_to_all.20 = f32[8,16,128]{2,1,0:T(8,128)S(1)} all-to-all(f32[8,16,128]{2,1,0:T(8,128)S(1)} %force.1), channel_id=1, replica_groups=mesh['chip'=64,'core'=2,'bucket'=4] {'core','bucket'}, dimensions={0} | all-to-all | bytes 131072 | tf_op jit(solution)/shard_map/all_to_all | solution.py:352
  52.5 0.1 reshape.30
  52.6 0.1 copy.9
  52.7 14.9 %all_to_all.21 = f32[64,2,128]{2,1,0:T(2,128)S(1)} all-to-all(f32[64,2,128]{2,1,0:T(2,128)S(1)} %copy.9), channel_id=1, replica_groups=mesh['chip'=64,'core'=2,'bucket'=4] {'chip'}, dimensions={0} | all-to-all | bytes 131072 | tf_op jit(solution)/shard_map/all_to_all | solution.py:354
  67.6 1.2 %pick.1 = f32[3,3072]{1,0:T(4,128)} custom-call(f32[128,128]{1,0:T(8,128)S(1)} %bitcast.15, s32[2,3072]{1,0:T(2,128)S(1)} %get-tuple-element.18.code_ref), custom_call_target="tpu_custom_call" | custom-call | tf_op jit(solution)/shard_map/pick/pallas_call | solution.py:356
Async XLA Ops:
  1.5 9.5 %all-to-all-start.1 = ((f32[8,5,128]{2,1,0:T(8,128)}), f32[8,5,128]{2,1,0:T(8,128)S(1)}, u32[]{:S(2)}, u32[]{:S(2)}) async-start(f32[8,5,128]{2,1,0:T(8,128)} %get-tuple-element.15), calls=%async_computation.1 | async-start | bytes 65536 | tf_op jit(solution)/shard_map/all_to_all | solution.py:299
  11.0 30.1 %all-to-all-start = ((f32[128,1,128]{2,1,0:T(1,128)}), f32[128,1,128]{2,1,0:T(1,128)S(1)}, u32[]{:S(2)}, u32[]{:S(2)}) async-start(f32[128,1,128]{2,1,0:T(1,128)} %bitcast.7), calls=%async_computation | async-start | bytes 131072 | tf_op jit(solution)/shard_map/dispatch/all_to_all | solution.py:324

commit v7 on v6

--- a/solution.py
+++ b/solution.py
@@ -1,3 +1,5 @@
+import functools
+
 import jax
 import jax.numpy as jnp
 from jax import lax
@@ -23,13 +25,27 @@
     return jnp.where(numbers == row, 1.0, 0.0).astype(BF16)
 
 
-def join_kernel(point_ref, angle_ref, eroded_ref, map_ref, out_ref, near_eroded_ref, near_map_ref):
-    near_eroded_ref[...] = eroded_ref[...]
-    near_map_ref[...] = map_ref[...]
+def join_kernel(point_hbm, angle_hbm, eroded_hbm, map_hbm, node_hbm, out_hbm, near_eroded_ref, near_map_ref,
+                near_node_ref, point_ref, angle_ref, out_ref, sem):
+    part = near_node_ref.shape[0] // 3
+    pairs = [(point_hbm, point_ref), (angle_hbm, angle_ref), (eroded_hbm, near_eroded_ref), (map_hbm, near_map_ref)]
+    for i in range(3):
+        at = pl.ds(i * part, part)
+        pairs.append((node_hbm.at[at, :], near_node_ref.at[at, :]))
+    copies = [pltpu.make_async_copy(source, target, sem.at[i]) for i, (source, target) in enumerate(pairs)]
+    for copy in copies:
+        copy.start()
+    for copy in copies[:2]:
+        copy.wait()
     for i in range(3):
         out_ref[:, i, :] = point_ref[i]
     for i in range(2):
         out_ref[:, 3 + i, :] = angle_ref[:, i, :]
+    away = pltpu.make_async_copy(out_ref, out_hbm, sem.at[7])
+    away.start()
+    for copy in copies[2:]:
+        copy.wait()
+    away.wait()
 
 
 def pieces(value):
@@ -80,10 +96,8 @@
                 left_ref[g % 2, (g // 2) * 2 + half, term * 64:(term + 1) * 64, :] = turned[half * 64:(half + 1) * 64]
 
 
-def pack_kernel(eroded_ref, map_ref, node_hbm, out_ref, code_ref, node_ref, row_ref, col_ref, other_ref, rank_ref,
-                owner_hot, geo_ref, sem):
-    copy = pltpu.make_async_copy(node_hbm, node_ref, sem)
-    copy.start()
+def pack_kernel(eroded_ref, map_ref, node_ref, out_ref, code_ref, row_ref, col_ref, other_ref, rank_ref, owner_hot,
+                geo_ref):
     group = lax.axis_index("bucket")
     blocks = map_ref.shape[0]
     count = row_ref.shape[1]
@@ -146,7 +160,7 @@
     lane = lax.broadcasted_iota(jnp.int32, (1, LANES), 1)
     wanted = [(lane * 8 + group * 2 + par).astype(F32) for par in range(2)]
     pair = 2 * LANES
-    sources = [jnp.zeros((16, 256), F32), jnp.zeros((16, 256), F32)]
+    sources = []
     numbers = lax.broadcasted_iota(jnp.int32, (16, pair), 0)
     for c in range(count // pair):
         at = slice(c * pair, (c + 1) * pair)
@@ -155,10 +169,9 @@
         left = jnp.where((numbers & 7) == rank[:, at], parts, 0).astype(F32).astype(BF16)
         other = other_ref[at, :]
         right = jnp.concatenate([jnp.where(other == want, 1.0, 0.0).astype(BF16) for want in wanted], axis=1)
-        sources[c % 2] = sources[c % 2] + jnp.dot(left, right, preferred_element_type=F32)
-    source = sources[0] + sources[1]
-
-    copy.wait()
+        sources.append(jnp.dot(left, right, preferred_element_type=F32))
+    source = functools.reduce(jnp.add, sources)
+
     for g in range(blocks // 16):
         row = [node_ref[pl.ds((r // 8) * blocks * 8 + r % 8 + g * 128, 16, stride=8), :] for r in range(24)]
         corner = [row[3 * m:3 * m + 3] for m in range(4)]
@@ -186,14 +199,18 @@
         filled = filled + jnp.where(high >= 0, 1.0, 0.0)
         hot = one_hot(low, LANES)
         hot = jnp.concatenate([hot, hot], axis=0)
-        mine = lax.broadcasted_iota(jnp.int32, (blocks, 256), 0) == high
+        numbers = lax.broadcasted_iota(jnp.int32, (8, 256), 0)
         for start, end in ((0, 5), (5, 9)):
             found = jnp.dot(geo_ref[start * blocks:end * blocks, :], hot, preferred_element_type=F32)
-            for q in range(start, end):
-                at = (q - start) * blocks
-                value = jnp.sum(jnp.where(mine, found[at:at + blocks], 0.0), axis=0, keepdims=True)
+            values = [jnp.zeros((8, 256), F32)] * (end - start)
+            for h in range(0, blocks, 8):
+                mine = numbers == high - h
+                for i in range(end - start):
+                    values[i] = jnp.where(mine, found[i * blocks + h:i * blocks + h + 8], values[i])
+            for i in range(end - start):
+                value = jnp.sum(values[i], axis=0, keepdims=True)
                 for par in range(2):
-                    row = par * 64 + k * 12 + q
+                    row = par * 64 + k * 12 + start + i
                     col_ref[row:row + 1, :] = value[:, par * LANES:(par + 1) * LANES]
     for par in range(2):
         col_ref[par * 64 + 60:par * 64 + 61, :] = filled[:, par * LANES:(par + 1) * LANES]
@@ -284,41 +301,47 @@
     blocks = faces // LANES
     uncovered = 6 * eroded.shape[0]
     vmem = pl.BlockSpec(memory_space=pltpu.VMEM)
-
-    segs, near_eroded, near_map = pl.pallas_call(
+    anywhere = pl.BlockSpec(memory_space=pl.ANY)
+
+    node_tiles = node_data.reshape(3, 8, blocks, LANES).transpose(0, 2, 1, 3).reshape(24 * blocks, LANES)
+    segs, near_eroded, near_map, near_node = pl.pallas_call(
         join_kernel,
         out_shape=(
-            pltpu.VMEM((seg_point.shape[0], 5, seg_point.shape[2]), F32),
+            jax.ShapeDtypeStruct((seg_point.shape[0], 5, seg_point.shape[2]), F32),
             pltpu.VMEM((uncovered // 6 // LANES, LANES), jnp.int32),
             pltpu.VMEM((blocks, LANES), jnp.int32),
+            pltpu.VMEM((24 * blocks, LANES), F32),
         ),
-        in_specs=[vmem, vmem, vmem, vmem],
-        out_specs=(vmem, vmem, vmem),
+        in_specs=[anywhere] * 5,
+        out_specs=(anywhere, vmem, vmem, vmem),
+        scratch_shapes=[
+            pltpu.VMEM((3, seg_point.shape[0], seg_point.shape[2]), F32),
+            pltpu.VMEM(seg_angle.shape, F32),
+            pltpu.VMEM((seg_point.shape[0], 5, seg_point.shape[2]), F32),
+            pltpu.SemaphoreType.DMA((8,)),
+        ],
         name="join",
-    )(seg_point.transpose(1, 0, 2), seg_angle, eroded.reshape(-1, LANES), bucket_map.reshape(blocks, LANES))
+    )(seg_point.transpose(1, 0, 2), seg_angle, eroded.reshape(-1, LANES), bucket_map.reshape(blocks, LANES), node_tiles)
     segs = lax.all_to_all(segs, "bucket", 0, 0, tiled=True)
 
-    node_tiles = node_data.reshape(3, 8, blocks, LANES).transpose(0, 2, 1, 3).reshape(24 * blocks, LANES)
     packed, code = pl.pallas_call(
         pack_kernel,
         out_shape=(
             pltpu.VMEM((owners, LANES), F32),
             pltpu.VMEM((2, uncovered), jnp.int32),
         ),
-        in_specs=[vmem, vmem, pl.BlockSpec(memory_space=pl.ANY)],
+        in_specs=[vmem, vmem, vmem],
         out_specs=(vmem, vmem),
         scratch_shapes=[
-            pltpu.VMEM((24 * blocks, LANES), F32),
             pltpu.VMEM((1, uncovered), jnp.int32),
             pltpu.VMEM((LANES, LANES), F32),
             pltpu.VMEM((uncovered, LANES), F32),
             pltpu.VMEM((2, uncovered), F32),
             pltpu.VMEM((LANES, uncovered), BF16),
             pltpu.VMEM((9 * blocks, 2 * LANES), BF16),
-            pltpu.SemaphoreType.DMA,
         ],
         name="pack",
-    )(near(near_eroded), near(near_map), node_tiles)
+    )(near(near_eroded), near(near_map), near(near_node))
 
     with jax.named_scope("dispatch"):
         arrived = lax.all_to_all(packed.reshape(owners, 1, LANES), ("chip", "core"), 0, 0, tiled=True)

time: 69.2 us -> 68.3 us (0.987)
  blocking collectives: 24.3 us -> 23.5 us
  Pallas kernels: 10 us -> 9.23 us
    all_to_all x1, blocking collectives: 9.4 us -> 8.58 us  [local(): shared = lax.all_to_all(force, ('core', 'bucket'), 0, 0, tiled=True)]
    pallas_call x1, Pallas kernels: 4.66 us -> 3.87 us  [local(): pl.pallas_call(pack_kernel, out_shape=(pltpu.VMEM((owners, LANES), F32),...]
  transfers between devices with their start and end apart: 2 -> 2, of which waited for: 1 -> 2; matrix products, arithmetic and copies ran while one was open for 0% -> 0% of each run, Pallas kernels for 8% -> 7%
where the time goes in v7:
time: 68.3 us; the launch traced here: 68 us
  starting transfers between devices  23.9 us (35%)
  blocking collectives  23.5 us (34%)
  waiting for transfers between devices  11.2 us (16%)
  Pallas kernels  9.23 us (14%)
    all_to_all x1, starting transfers between devices, local(): lax.all_to_all(packed.reshape(owners, 1, LANES), ('chip', 'core'), 0, 0,...  19 us
    all_to_all x1, blocking collectives, local(): returned = lax.all_to_all(outgoing, 'chip', 0, 0, tiled=True)  14.9 us
    all_to_all x1, waiting for transfers between devices, local(): lax.all_to_all(packed.reshape(owners, 1, LANES), ('chip', 'core'), 0, 0,...  10.8 us
    all_to_all x1, blocking collectives, local(): shared = lax.all_to_all(force, ('core', 'bucket'), 0, 0, tiled=True)  8.58 us
    all_to_all x1, starting transfers between devices, local(): segs = lax.all_to_all(segs, 'bucket', 0, 0, tiled=True)  4.84 us
    pallas_call x1, Pallas kernels, local(): pl.pallas_call(pack_kernel, out_shape=(pltpu.VMEM((owners, LANES), F32),...  3.87 us
    pallas_call x1, Pallas kernels, local(): pl.pallas_call(force_kernel, out_shape=pltpu.VMEM((2 * groups, 16, LANES)...  2.05 us
    pallas_call x1, Pallas kernels, local(): pl.pallas_call(join_kernel, out_shape=(jax.ShapeDtypeStruct((seg_point.sh...  1.4 us
  transfers between devices with their start and end apart: 2, of which 2 were waited for; matrix products, arithmetic and copies ran while one was open for 0% of the time, Pallas kernels for 7%

profile of v7, /device:TPU:1, one launch (start us, length us, event | category | flops | bytes accessed | tf_op | source)
XLA Modules:
  0.0 68.0 jit_solution(14956915818425294329)
XLA Ops:
  0.0 1.4 %join.1 = (f32[8,5,128]{2,1,0:T(8,128)}, s32[4,128]{1,0:T(4,128)S(1)}, s32[96,128]{1,0:T(8,128)S(1)}, f32[2304,128]{1,0:T(8,128)S(1)}) custom-call(f32[3,8,128]{2,1,0:T(8,128)} %bitcast.19, f32[8,2,128]{2,1,0:T(2,128)} %angle_hbm.1, s32[4,128]{1,0:T(4,128)} %bitcast.20, s32[96,128]{1,0:T(8,128)} %bitcast.18, f32[2304,128]{1,0:T(8,128)} %bitcast.16), custom_call_target="tpu_custom_call" | custom-call | tf_op jit(solution)/shard_map/join/pallas_call | solution.py:307
  1.4 4.8 %all-to-all-start.1 = ((f32[8,5,128]{2,1,0:T(8,128)}), f32[8,5,128]{2,1,0:T(8,128)S(1)}, u32[]{:S(2)}, u32[]{:S(2)}) async-start(f32[8,5,128]{2,1,0:T(8,128)} %get-tuple-element.17), calls=%async_computation.1 | async-start | bytes 65536 | tf_op jit(solution)/shard_map/all_to_all | solution.py:325
  6.2 3.9 %pack.1 = (f32[128,128]{1,0:T(8,128)}, s32[2,3072]{1,0:T(2,128)S(1)}) custom-call(s32[4,128]{1,0:T(4,128)S(1)} %get-tuple-element.13.eroded_ref, s32[96,128]{1,0:T(8,128)S(1)} %get-tuple-element.14.map_ref, f32[2304,128]{1,0:T(8,128)S(1)} %get-tuple-element.15.node_ref), custom_call_target="tpu_custom_call" | custom-call | tf_op jit(solution)/shard_map/pack/pallas_call | solution.py:327
  10.1 0.4 all-to-all-done.1.seg_ref
  10.6 19.0 %all-to-all-start = ((f32[128,1,128]{2,1,0:T(1,128)}), f32[128,1,128]{2,1,0:T(1,128)S(1)}, u32[]{:S(2)}, u32[]{:S(2)}) async-start(f32[128,1,128]{2,1,0:T(1,128)} %bitcast.7), calls=%async_computation | async-start | bytes 131072 | tf_op jit(solution)/shard_map/dispatch/all_to_all | solution.py:347
  29.6 0.7 %coefficients.1 = (bf16[2,8,256,128]{3,2,1,0:T(8,128)(2,1)S(1)}, f32[8,8,128]{2,1,0:T(8,128)S(1)}) custom-call(f32[8,5,128]{2,1,0:T(8,128)S(1)} %all-to-all-done.1.seg_ref), custom_call_target="tpu_custom_call" | custom-call | tf_op jit(solution)/shard_map/coefficients/coefficients/pallas_call | solution.py:350
  30.3 10.8 %all-to-all-done = f32[128,1,128]{2,1,0:T(1,128)S(1)} async-done(((f32[128,1,128]{2,1,0:T(1,128)}), f32[128,1,128]{2,1,0:T(1,128)S(1)}, u32[]{:S(2)}, u32[]{:S(2)}) %all-to-all-start) | async-done | bytes 65568 | tf_op jit(solution)/shard_map/dispatch/all_to_all | solution.py:347
  41.0 2.1 %force.1 = f32[8,16,128]{2,1,0:T(8,128)S(1)} custom-call(f32[128,128]{1,0:T(8,128)S(1)} %bitcast.14, bf16[2,8,256,128]{3,2,1,0:T(8,128)(2,1)S(1)} %get-tuple-element.18.left_ref, f32[8,8,128]{2,1,0:T(8,128)S(1)} %get-tuple-element.19.seg_ref), custom_call_target="tpu_custom_call" | custom-call | tf_op jit(solution)/shard_map/force/pallas_call | solution.py:362
  43.1 8.6 %all_to_all.20 = f32[8,16,128]{2,1,0:T(8,128)S(1)} all-to-all(f32[8,16,128]{2,1,0:T(8,128)S(1)} %force.1), channel_id=1, replica_groups=mesh['chip'=64,'core'=2,'bucket'=4] {'core','bucket'}, dimensions={0} | all-to-all | bytes 131072 | tf_op jit(solution)/shard_map/all_to_all | solution.py:375
  51.7 0.1 reshape.30
  51.8 0.1 copy.9
  51.9 14.9 %all_to_all.21 = f32[64,2,128]{2,1,0:T(2,128)S(1)} all-to-all(f32[64,2,128]{2,1,0:T(2,128)S(1)} %copy.9), channel_id=1, replica_groups=mesh['chip'=64,'core'=2,'bucket'=4] {'chip'}, dimensions={0} | all-to-all | bytes 131072 | tf_op jit(solution)/shard_map/all_to_all | solution.py:377
  66.8 1.2 %pick.1 = f32[3,3072]{1,0:T(4,128)} custom-call(f32[128,128]{1,0:T(8,128)S(1)} %bitcast.15, s32[2,3072]{1,0:T(2,128)S(1)} %get-tuple-element.20.code_ref), custom_call_target="tpu_custom_call" | custom-call | tf_op jit(solution)/shard_map/pick/pallas_call | solution.py:379
Async XLA Ops:
  1.4 9.1 %all-to-all-start.1 = ((f32[8,5,128]{2,1,0:T(8,128)}), f32[8,5,128]{2,1,0:T(8,128)S(1)}, u32[]{:S(2)}, u32[]{:S(2)}) async-start(f32[8,5,128]{2,1,0:T(8,128)} %get-tuple-element.17), calls=%async_computation.1 | async-start | bytes 65536 | tf_op jit(solution)/shard_map/all_to_all | solution.py:325
  10.6 30.5 %all-to-all-start = ((f32[128,1,128]{2,1,0:T(1,128)}), f32[128,1,128]{2,1,0:T(1,128)S(1)}, u32[]{:S(2)}, u32[]{:S(2)}) async-start(f32[128,1,128]{2,1,0:T(1,128)} %bitcast.7), calls=%async_computation | async-start | bytes 131072 | tf_op jit(solution)/shard_map/dispatch/all_to_all | solution.py:347

commit v8 on v7

--- a/solution.py
+++ b/solution.py
@@ -25,25 +25,66 @@
     return jnp.where(numbers == row, 1.0, 0.0).astype(BF16)
 
 
-def join_kernel(point_hbm, angle_hbm, eroded_hbm, map_hbm, node_hbm, out_hbm, near_eroded_ref, near_map_ref,
-                near_node_ref, point_ref, angle_ref, out_ref, sem):
-    part = near_node_ref.shape[0] // 3
-    pairs = [(point_hbm, point_ref), (angle_hbm, angle_ref), (eroded_hbm, near_eroded_ref), (map_hbm, near_map_ref)]
+def start_kernel(point_hbm, angle_hbm, eroded_hbm, map_hbm, node_hbm, out_hbm, node_ref, row_ref, bucket_ref, hot_ref,
+                 count_ref, point_ref, angle_ref, eroded_ref, map_ref, out_ref, sem):
+    part = node_ref.shape[0] // 3
+    pairs = [(eroded_hbm, eroded_ref), (map_hbm, map_ref), (point_hbm, point_ref), (angle_hbm, angle_ref)]
     for i in range(3):
         at = pl.ds(i * part, part)
-        pairs.append((node_hbm.at[at, :], near_node_ref.at[at, :]))
+        pairs.append((node_hbm.at[at, :], node_ref.at[at, :]))
     copies = [pltpu.make_async_copy(source, target, sem.at[i]) for i, (source, target) in enumerate(pairs)]
     for copy in copies:
         copy.start()
-    for copy in copies[:2]:
-        copy.wait()
-    for i in range(3):
-        out_ref[:, i, :] = point_ref[i]
-    for i in range(2):
-        out_ref[:, 3 + i, :] = angle_ref[:, i, :]
+    blocks = map_ref.shape[0]
+    count = row_ref.shape[1]
+    rows4 = eroded_ref.shape[0]
+    span = count // rows4
+    copies[0].wait()
+
+    eroded = eroded_ref[...]
+    lane = lax.broadcasted_iota(jnp.int32, (LANES, span), 1)
+    six = 6 * lax.broadcasted_iota(jnp.int32, (LANES, span), 0)
+    spread = jnp.where((lane >= six) & (lane < six + 6), 1.0, 0.0).astype(BF16)
+    high = jnp.dot((eroded >> 3).astype(F32).astype(BF16), spread, preferred_element_type=F32)
+    low = jnp.dot((eroded & 7).astype(F32).astype(BF16), spread, preferred_element_type=F32)
+    number = lax.broadcasted_iota(jnp.int32, (rows4, span), 1)
+    faces4 = 6 * (high * 8.0 + low).astype(jnp.int32) + number % 6
+    for a in range(rows4):
+        row_ref[0:1, a * span:(a + 1) * span] = faces4[a:a + 1, :]
+    copies[1].wait()
+    buckets = map_ref[...]
+    digits = jnp.concatenate([(buckets & 1016).astype(F32), (buckets & 7).astype(F32)], axis=1).astype(BF16)
+    step = 512
+    for c in range(count // step):
+        at = slice(c * step, (c + 1) * step)
+        face = row_ref[0:1, at]
+        hot = one_hot(face & (LANES - 1), LANES)
+        value = jnp.dot(digits, jnp.concatenate([hot, hot], axis=0), preferred_element_type=F32)
+        numbers = lax.broadcasted_iota(jnp.int32, (blocks, step), 0)
+        bucket_ref[0:1, at] = jnp.sum(jnp.where(numbers == (face >> 7), value, 0.0), axis=0, keepdims=True)
+    total = jnp.zeros((16, LANES), F32)
+    for t in range(count // LANES):
+        at = slice(t * LANES, (t + 1) * LANES)
+        bucket = bucket_ref[0:1, at].astype(jnp.int32)
+        hot = one_hot(bucket >> 3, LANES)
+        hot_ref[:, at] = hot
+        inner = one_hot(bucket & 7, 16)
+        found = lax.dot_general(inner, hot, NT, preferred_element_type=F32)
+        count_ref[t * 16:(t + 1) * 16, :] = found
+        total = total + found
+
+    copies[2].wait()
+    copies[3].wait()
+    for core in range(2):
+        at = slice(core * 8, core * 8 + 8)
+        for i in range(3):
+            out_ref[at, i, :] = point_ref[i]
+        for i in range(2):
+            out_ref[at, 3 + i, :] = angle_ref[:, i, :]
+        out_ref[at, 5, :] = total[0:8]
     away = pltpu.make_async_copy(out_ref, out_hbm, sem.at[7])
     away.start()
-    for copy in copies[2:]:
+    for copy in copies[4:]:
         copy.wait()
     away.wait()
 
@@ -90,73 +131,41 @@
     for i in range(3, 8):
         normal_ref[:, i, :] = jnp.zeros_like(ring)
     for g in range(seg_ref.shape[0]):
+        inner = slice(g // 8 * LANES, (g // 8 + 1) * LANES)
         for term in range(4):
             turned = rows_ref[g, term * LANES:(term + 1) * LANES, :].T.astype(BF16)
             for half in range(2):
-                left_ref[g % 2, (g // 2) * 2 + half, term * 64:(term + 1) * 64, :] = turned[half * 64:(half + 1) * 64]
-
-
-def pack_kernel(eroded_ref, map_ref, node_ref, out_ref, code_ref, row_ref, col_ref, other_ref, rank_ref, owner_hot,
-                geo_ref):
+                left_ref[g % 2, (g % 8) // 2 * 2 + half, term * 64:(term + 1) * 64, inner] = (
+                    turned[half * 64:(half + 1) * 64])
+
+
+def pack_kernel(row_ref, bucket_ref, hot_ref, count_ref, node_ref, col_ref, code_ref, other_ref, rank_ref, geo_ref):
     group = lax.axis_index("bucket")
-    blocks = map_ref.shape[0]
     count = row_ref.shape[1]
     tiles = count // LANES
-    rows4 = eroded_ref.shape[0]
-    span = count // rows4
-
-    eroded = eroded_ref[...]
-    lane = lax.broadcasted_iota(jnp.int32, (LANES, span), 1)
-    six = 6 * lax.broadcasted_iota(jnp.int32, (LANES, span), 0)
-    spread = jnp.where((lane >= six) & (lane < six + 6), 1.0, 0.0).astype(BF16)
-    high = jnp.dot((eroded >> 3).astype(F32).astype(BF16), spread, preferred_element_type=F32)
-    low = jnp.dot((eroded & 7).astype(F32).astype(BF16), spread, preferred_element_type=F32)
-    number = lax.broadcasted_iota(jnp.int32, (rows4, span), 1)
-    faces4 = 6 * (high * 8.0 + low).astype(jnp.int32) + number % 6
-    for a in range(rows4):
-        row_ref[0:1, a * span:(a + 1) * span] = faces4[a:a + 1, :]
-
-    buckets = map_ref[...]
-    digits = jnp.concatenate([(buckets & 1016).astype(F32), (buckets & 7).astype(F32)], axis=1).astype(BF16)
-    step = 512
-    for c in range(count // step):
-        at = slice(c * step, (c + 1) * step)
-        face = row_ref[0:1, at]
-        hot = one_hot(face & (LANES - 1), LANES)
-        value = jnp.dot(digits, jnp.concatenate([hot, hot], axis=0), preferred_element_type=F32)
-        numbers = lax.broadcasted_iota(jnp.int32, (blocks, step), 0)
-        rank_ref[0:1, at] = jnp.sum(jnp.where(numbers == (face >> 7), value, 0.0), axis=0, keepdims=True)
+    blocks = geo_ref.shape[0] // 9
 
     earlier = (lax.broadcasted_iota(jnp.int32, (LANES, LANES), 0)
                < lax.broadcasted_iota(jnp.int32, (LANES, LANES), 1))
-    counts, picks = [], []
+    before = jnp.zeros((16, LANES), F32)
     for t in range(tiles):
         at = slice(t * LANES, (t + 1) * LANES)
-        mine = rank_ref[0:1, at]
+        mine = bucket_ref[0:1, at]
         other = jnp.broadcast_to(mine, (LANES, LANES)).T
         other_ref[at, :] = other
         hit = jnp.where((other == mine) & earlier, 1.0, 0.0)
-        rank_ref[1:2, at] = jnp.sum(hit, axis=0, keepdims=True)
-        bucket = mine.astype(jnp.int32)
-        hot = one_hot(bucket >> 3, LANES)
-        owner_hot[:, at] = hot
-        picks.append(lax.broadcasted_iota(jnp.int32, (16, LANES), 0) == (bucket & 7))
-        inner = jnp.where(picks[t], 1.0, 0.0).astype(BF16)
-        counts.append(lax.dot_general(inner, hot, NT, preferred_element_type=F32))
-    before = jnp.zeros((16, LANES), F32)
-    for t in range(tiles):
-        at = slice(t * LANES, (t + 1) * LANES)
+        rank = jnp.sum(hit, axis=0, keepdims=True)
         if t:
-            before = before + counts[t - 1]
-            seen = jnp.dot(before.astype(BF16), owner_hot[:, at], preferred_element_type=F32)
-            rank_ref[1:2, at] += jnp.sum(jnp.where(picks[t], seen, 0.0), axis=0, keepdims=True)
-
-    bucket = rank_ref[0:1, :].astype(jnp.int32)
-    rank = rank_ref[1:2, :].astype(jnp.int32)
-    owner = bucket >> 3
-    inner = bucket & 7
-    code_ref[0:1, :] = (owner & (LANES - 2)) + (inner & 1)
-    code_ref[1:2, :] = ((owner & 1) * 4 + (inner >> 1)) * SLOTS + rank
+            before = before + count_ref[(t - 1) * 16:t * 16, :]
+            seen = jnp.dot(before.astype(BF16), hot_ref[:, at], preferred_element_type=F32)
+            picked = lax.broadcasted_iota(jnp.int32, (16, LANES), 0) == (mine.astype(jnp.int32) & 7)
+            rank = rank + jnp.sum(jnp.where(picked, seen, 0.0), axis=0, keepdims=True)
+        rank_ref[0:1, at] = rank
+
+    bucket = bucket_ref[0:1, :].astype(jnp.int32)
+    rank = rank_ref[0:1, :].astype(jnp.int32)
+    code_ref[0:1, :] = bucket >> 3
+    code_ref[1:2, :] = (bucket & 7) * SLOTS + rank
     lane = lax.broadcasted_iota(jnp.int32, (1, LANES), 1)
     wanted = [(lane * 8 + group * 2 + par).astype(F32) for par in range(2)]
     pair = 2 * LANES
@@ -214,23 +223,37 @@
                     col_ref[row:row + 1, :] = value[:, par * LANES:(par + 1) * LANES]
     for par in range(2):
         col_ref[par * 64 + 60:par * 64 + 61, :] = filled[:, par * LANES:(par + 1) * LANES]
-    out_ref[...] = col_ref[...].T
+
+
+def send_kernel(col_ref, seg_ref, out_ref, all_ref):
+    all_ref[...] = col_ref[...]
+    peer = (1 - lax.axis_index("core")) * 8 + lax.axis_index("bucket") * 2
+    for par in range(2):
+        all_ref[par * 64 + 61:par * 64 + 62, :] = seg_ref[peer + par, 5:6, :]
+    out_ref[...] = all_ref[...].T
 
 
 def force_kernel(face_ref, left_ref, seg_ref, out_ref, row_ref, right_ref, wide_ref):
     half = LANES // 2
     row_ref[...] = jnp.concatenate([face_ref[pl.ds(core, half, stride=2), :] for core in range(2)], axis=0).T
-    groups = seg_ref.shape[0] // 2
-    for g in range(2 * groups):
-        columns = seg_ref[g].T
-        for i in range(3):
-            wide_ref[g % 2, i, (g // 2) * LANES:(g // 2 + 1) * LANES, :] = jnp.broadcast_to(
-                columns[:, i:i + 1], (LANES, LANES))
+    lane = lax.broadcasted_iota(jnp.int32, (LANES, LANES), 1)
+    lower = lane < half
+    columns = seg_ref[...].reshape(LANES, LANES).T
+    for par in range(2):
+        for x in range(4):
+            for i in range(3):
+                pair = [columns[:, g * 8 + i:g * 8 + i + 1] for g in (x * 2 + par, 8 + x * 2 + par)]
+                wide = [jnp.broadcast_to(value, (LANES, LANES)) for value in pair]
+                wide_ref[par, i, x * LANES:(x + 1) * LANES, :] = jnp.where(lower, wide[0], wide[1])
+    first_core = lower[0:1, :]
     half_log2e = 0.5 * 1.4426950408889634
     number = lax.broadcasted_iota(jnp.int32, (16, LANES), 0)
+    number_lane = lax.broadcasted_iota(jnp.int32, (16, LANES), 1)
     for par in range(2):
-        count = jnp.sum(row_ref[par * 64 + 60:par * 64 + 61, :], axis=1, keepdims=True)
-        stiff = pieces(jnp.broadcast_to(STIFFNESS * lax.rsqrt(jnp.maximum(count, 1.0)), (1, LANES)))
+        count = row_ref[par * 64 + 60:par * 64 + 61, :] + row_ref[par * 64 + 61:par * 64 + 62, :]
+        sums = [jnp.sum(jnp.where(mine, count, 0.0), axis=1, keepdims=True) for mine in (first_core, ~first_core)]
+        count = jnp.where(first_core, sums[0], sums[1])
+        stiff = pieces(STIFFNESS * lax.rsqrt(jnp.maximum(count, 1.0)))
         for k in range(SLOTS):
             start = par * 64 + k * 12
             face = row_ref[start:start + 16, :]
@@ -244,7 +267,9 @@
             first, second, third = pieces(face)
             blocks = (first, second, third, first, second, first, extra, jnp.zeros_like(extra))
             for group, block in enumerate(blocks):
-                right_ref[par, group * 16:(group + 1) * 16, k * LANES:(k + 1) * LANES] = block.astype(BF16)
+                for core, mine in enumerate((number_lane < half, number_lane >= half)):
+                    at = core * LANES + group * 16
+                    right_ref[par, at:at + 16, k * LANES:(k + 1) * LANES] = jnp.where(mine, block, 0.0).astype(BF16)
     chunks = left_ref.shape[1]
     for par in range(2):
         for first in range(0, SLOTS, 2):
@@ -267,11 +292,8 @@
                     row = par * 16 + i * SLOTS + first + k
                     row_ref[row:row + 1, :] = jnp.sum(total[k][i], axis=0, keepdims=True)
         row_ref[par * 16 + 15:par * 16 + 16, :] = jnp.zeros((1, LANES), F32)
-    for core in range(2):
-        at = slice(core * half, (core + 1) * half)
-        both = jnp.concatenate([row_ref[0:16, at], row_ref[16:32, at]], axis=1)
-        for x in range(4):
-            out_ref[core * 4 + x] = both
+    for x in range(4):
+        out_ref[x] = row_ref[0:32, :]
 
 
 def pick_kernel(force_ref, code_ref, out_ref, row_ref):
@@ -304,75 +326,81 @@
     anywhere = pl.BlockSpec(memory_space=pl.ANY)
 
     node_tiles = node_data.reshape(3, 8, blocks, LANES).transpose(0, 2, 1, 3).reshape(24 * blocks, LANES)
-    segs, near_eroded, near_map, near_node = pl.pallas_call(
-        join_kernel,
+    local_buckets, width = seg_point.shape[0], seg_point.shape[2]
+    segs, node, row, bucket, hot, counts = pl.pallas_call(
+        start_kernel,
         out_shape=(
-            jax.ShapeDtypeStruct((seg_point.shape[0], 5, seg_point.shape[2]), F32),
+            jax.ShapeDtypeStruct((2 * local_buckets, 6, width), F32),
+            pltpu.VMEM((24 * blocks, LANES), F32),
+            pltpu.VMEM((1, uncovered), jnp.int32),
+            pltpu.VMEM((1, uncovered), F32),
+            pltpu.VMEM((LANES, uncovered), BF16),
+            pltpu.VMEM((uncovered // 8, LANES), F32),
+        ),
+        in_specs=[anywhere] * 5,
+        out_specs=(anywhere, vmem, vmem, vmem, vmem, vmem),
+        scratch_shapes=[
+            pltpu.VMEM((3, local_buckets, width), F32),
+            pltpu.VMEM(seg_angle.shape, F32),
             pltpu.VMEM((uncovered // 6 // LANES, LANES), jnp.int32),
             pltpu.VMEM((blocks, LANES), jnp.int32),
-            pltpu.VMEM((24 * blocks, LANES), F32),
-        ),
-        in_specs=[anywhere] * 5,
-        out_specs=(anywhere, vmem, vmem, vmem),
-        scratch_shapes=[
-            pltpu.VMEM((3, seg_point.shape[0], seg_point.shape[2]), F32),
-            pltpu.VMEM(seg_angle.shape, F32),
-            pltpu.VMEM((seg_point.shape[0], 5, seg_point.shape[2]), F32),
+            pltpu.VMEM((2 * local_buckets, 6, width), F32),
             pltpu.SemaphoreType.DMA((8,)),
         ],
-        name="join",
+        name="start",
     )(seg_point.transpose(1, 0, 2), seg_angle, eroded.reshape(-1, LANES), bucket_map.reshape(blocks, LANES), node_tiles)
-    segs = lax.all_to_all(segs, "bucket", 0, 0, tiled=True)
-
-    packed, code = pl.pallas_call(
+    segs = lax.all_to_all(segs, ("core", "bucket"), 0, 0, tiled=True)
+
+    columns, code = pl.pallas_call(
         pack_kernel,
-        out_shape=(
-            pltpu.VMEM((owners, LANES), F32),
-            pltpu.VMEM((2, uncovered), jnp.int32),
-        ),
-        in_specs=[vmem, vmem, vmem],
+        out_shape=(pltpu.VMEM((LANES, owners), F32), pltpu.VMEM((2, uncovered), jnp.int32)),
+        in_specs=[vmem] * 5,
         out_specs=(vmem, vmem),
         scratch_shapes=[
-            pltpu.VMEM((1, uncovered), jnp.int32),
-            pltpu.VMEM((LANES, LANES), F32),
             pltpu.VMEM((uncovered, LANES), F32),
-            pltpu.VMEM((2, uncovered), F32),
-            pltpu.VMEM((LANES, uncovered), BF16),
+            pltpu.VMEM((1, uncovered), F32),
             pltpu.VMEM((9 * blocks, 2 * LANES), BF16),
         ],
         name="pack",
-    )(near(near_eroded), near(near_map), near(near_node))
-
-    with jax.named_scope("dispatch"):
-        arrived = lax.all_to_all(packed.reshape(owners, 1, LANES), ("chip", "core"), 0, 0, tiled=True)
+    )(near(row), near(bucket), near(hot), near(counts), near(node))
+
+    packed = pl.pallas_call(
+        send_kernel,
+        out_shape=jax.ShapeDtypeStruct((owners, LANES), F32),
+        in_specs=[vmem, vmem],
+        out_specs=vmem,
+        scratch_shapes=[pltpu.VMEM((LANES, owners), F32)],
+        name="send",
+    )(near(columns), near(segs))
+    arrived = lax.all_to_all(packed.reshape(owners // 2, 2, LANES), "chip", 0, 0, tiled=True)
 
     with jax.named_scope("coefficients"):
         left, normal = pl.pallas_call(
             coefficient_kernel,
             out_shape=(
-                pltpu.VMEM((2, 2 * groups, 256, LANES), BF16),
-                pltpu.VMEM((2 * groups, 8, LANES), F32),
+                pltpu.VMEM((2, 2 * groups, 256, 2 * LANES), BF16),
+                pltpu.VMEM((4 * groups, 8, LANES), F32),
             ),
             in_specs=[vmem],
             out_specs=(vmem, vmem),
-            scratch_shapes=[pltpu.VMEM((2 * groups, 4 * LANES, LANES), F32)],
+            scratch_shapes=[pltpu.VMEM((4 * groups, 4 * LANES, LANES), F32)],
             name="coefficients",
         )(near(segs))
 
     force = pl.pallas_call(
         force_kernel,
-        out_shape=pltpu.VMEM((2 * groups, 16, LANES), F32),
+        out_shape=pltpu.VMEM((groups, 32, LANES), F32),
         in_specs=[vmem, vmem, vmem],
         out_specs=vmem,
         scratch_shapes=[
             pltpu.VMEM((LANES, LANES), F32),
-            pltpu.VMEM((2, LANES, SLOTS * LANES), BF16),
+            pltpu.VMEM((2, 2 * LANES, SLOTS * LANES), BF16),
             pltpu.VMEM((2, 3, groups * LANES, LANES), F32),
         ],
         name="force",
     )(near(arrived.reshape(owners, LANES)), near(left), near(normal))
 
-    shared = lax.all_to_all(force, ("core", "bucket"), 0, 0, tiled=True)
+    shared = lax.all_to_all(force, "bucket", 0, 0, tiled=True)
     outgoing = shared.reshape(groups * 32, 2, owners // 2).transpose(2, 1, 0)
     returned = lax.all_to_all(outgoing, "chip", 0, 0, tiled=True)
 

time: 68.3 us -> 71.2 us (1.042)
  the two profiles are of different devices: /device:TPU:1 before, /device:TPU:8 now
where the time goes in v8:
time: 71.2 us; the launch traced here: 70.8 us
  blocking collectives  24.2 us (34%)
  starting transfers between devices  20.9 us (29%)
  waiting for transfers between devices  11.9 us (17%)
  Pallas kernels  10.6 us (15%)
  local copies, waits for them, and re-layouts  3.15 us (4%)
    all_to_all x1, starting transfers between devices, local(): lax.all_to_all(packed.reshape(owners // 2, 2, LANES), 'chip', 0, 0, tiled...  16.6 us
    all_to_all x1, blocking collectives, local(): returned = lax.all_to_all(outgoing, 'chip', 0, 0, tiled=True)  16 us
    all_to_all x1, waiting for transfers between devices, local(): lax.all_to_all(packed.reshape(owners // 2, 2, LANES), 'chip', 0, 0, tiled...  8.51 us
    all_to_all x1, blocking collectives, local(): shared = lax.all_to_all(force, 'bucket', 0, 0, tiled=True)  8.2 us
    all_to_all x1, starting transfers between devices, local(): segs = lax.all_to_all(segs, ('core', 'bucket'), 0, 0, tiled=True)  4.31 us
    all_to_all x1, waiting for transfers between devices, local(): segs = lax.all_to_all(segs, ('core', 'bucket'), 0, 0, tiled=True)  3.4 us
    unnamed x4, local copies, waits for them, and re-layouts  2.93 us
    pallas_call x1, Pallas kernels, local(): pl.pallas_call(start_kernel, out_shape=(jax.ShapeDtypeStruct((2 * local_b...  2.76 us
  transfers between devices with their start and end apart: 2, of which 2 were waited for; matrix products, arithmetic and copies ran while one was open for 0% of the time, Pallas kernels for 5%

profile of v8, /device:TPU:8, one launch (start us, length us, event | category | flops | bytes accessed | tf_op | source)
XLA Modules:
  0.0 70.8 jit_solution(9804780829027992813)
XLA Ops:
  0.0 2.8 %start.1 = (f32[16,6,128]{2,1,0:T(8,128)}, f32[2304,128]{1,0:T(8,128)S(1)}, s32[1,3072]{1,0:T(1,128)S(1)}, f32[1,3072]{1,0:T(1,128)S(1)}, bf16[128,3072]{1,0:T(8,128)(2,1)S(1)}, /*index=5*/f32[384,128]{1,0:T(8,128)S(1)}) custom-call(f32[3,8,128]{2,1,0:T(8,128)} %bitcast.18, f32[8,2,128]{2,1,0:T(2,128)} %angle_hbm.1, s32[4,128]{1,0:T(4,128)} %bitcast.19, ...), custom_call_target="tpu_custom_call" | custom-call | tf_op jit(solution)/shard_map/start/pallas_call | solution.py:330
  2.8 4.3 %all-to-all-start = ((f32[16,6,128]{2,1,0:T(8,128)}), f32[16,6,128]{2,1,0:T(8,128)S(1)}, u32[]{:S(2)}, u32[]{:S(2)}) async-start(f32[16,6,128]{2,1,0:T(8,128)} %get-tuple-element.21), calls=%async_computation | async-start | bytes 131072 | tf_op jit(solution)/shard_map/all_to_all | solution.py:352
  7.1 1.9 %pack.1 = (f32[128,128]{1,0:T(8,128)S(1)}, s32[2,3072]{1,0:T(2,128)S(1)}) custom-call(s32[1,3072]{1,0:T(1,128)S(1)} %get-tuple-element.15.row_ref, f32[1,3072]{1,0:T(1,128)S(1)} %get-tuple-element.16.bucket_ref, bf16[128,3072]{1,0:T(8,128)(2,1)S(1)} %get-tuple-element.17.hot_ref, f32[384,128]{1,0:T(8,128)S(1)} %get-tuple-element.18.count_ref, ...), custom_call_target="tpu_custom_call" | custom-call | tf_op jit(solution)/shard_map/pack/pallas_call | solution.py:354
  9.0 3.4 %all-to-all-done.seg_ref = f32[16,6,128]{2,1,0:T(8,128)S(1)} async-done(((f32[16,6,128]{2,1,0:T(8,128)}), f32[16,6,128]{2,1,0:T(8,128)S(1)}, u32[]{:S(2)}, u32[]{:S(2)}) %all-to-all-start) | async-done | bytes 49184 | tf_op jit(solution)/shard_map/all_to_all | solution.py:352
  12.4 0.7 %send.1 = f32[128,128]{1,0:T(8,128)} custom-call(f32[128,128]{1,0:T(8,128)S(1)} %get-tuple-element.20.col_ref, f32[16,6,128]{2,1,0:T(8,128)S(1)} %all-to-all-done.seg_ref), custom_call_target="tpu_custom_call" | custom-call | tf_op jit(solution)/shard_map/send/pallas_call | solution.py:367
  13.2 16.6 %all-to-all-start.1 = ((f32[64,2,128]{2,1,0:T(2,128)}), f32[64,2,128]{2,1,0:T(2,128)S(1)}, u32[]{:S(2)}, u32[]{:S(2)}) async-start(f32[64,2,128]{2,1,0:T(2,128)} %bitcast.16), calls=%async_computation.1 | async-start | bytes 131072 | tf_op jit(solution)/shard_map/all_to_all | solution.py:375
  29.8 1.5 %coefficients.1 = (bf16[2,8,256,256]{3,2,1,0:T(8,128)(2,1)S(1)}, f32[16,8,128]{2,1,0:T(8,128)S(1)}) custom-call(f32[16,6,128]{2,1,0:T(8,128)S(1)} %all-to-all-done.seg_ref), custom_call_target="tpu_custom_call" | custom-call | tf_op jit(solution)/shard_map/coefficients/coefficients/pallas_call | solution.py:378
  31.2 0.0 copy-start
  31.2 1.3 %copy-done = bf16[2,8,256,256]{3,2,1,0:T(8,128)(2,1)} copy-done((bf16[2,8,256,256]{3,2,1,0:T(8,128)(2,1)}, bf16[2,8,256,256]{3,2,1,0:T(8,128)(2,1)S(1)}, u32[]{:S(2)}) %copy-start) | copy-done | bytes 2097176
  32.6 8.5 %all-to-all-done.1 = f32[64,2,128]{2,1,0:T(2,128)S(1)} async-done(((f32[64,2,128]{2,1,0:T(2,128)}), f32[64,2,128]{2,1,0:T(2,128)S(1)}, u32[]{:S(2)}, u32[]{:S(2)}) %all-to-all-start.1) | async-done | bytes 65568 | tf_op jit(solution)/shard_map/all_to_all | solution.py:375
  41.1 0.0 copy-start.1
  41.1 1.6 %copy-done.1 = bf16[2,8,256,256]{3,2,1,0:T(8,128)(2,1)S(1)} copy-done((bf16[2,8,256,256]{3,2,1,0:T(8,128)(2,1)S(1)}, bf16[2,8,256,256]{3,2,1,0:T(8,128)(2,1)}, u32[]{:S(2)}) %copy-start.1) | copy-done | bytes 2097176
  42.7 2.5 %force.1 = f32[4,32,128]{2,1,0:T(8,128)S(1)} custom-call(f32[128,128]{1,0:T(8,128)S(1)} %bitcast.12, bf16[2,8,256,256]{3,2,1,0:T(8,128)(2,1)S(1)} %copy-done.1, f32[16,8,128]{2,1,0:T(8,128)S(1)} %get-tuple-element.23.seg_ref), custom_call_target="tpu_custom_call" | custom-call | tf_op jit(solution)/shard_map/force/pallas_call | solution.py:390
  45.1 8.2 %all_to_all.20 = f32[4,32,128]{2,1,0:T(8,128)S(1)} all-to-all(f32[4,32,128]{2,1,0:T(8,128)S(1)} %force.1), channel_id=1, replica_groups=mesh['chip'=64,'core'=2,'bucket'=4] {'bucket'}, dimensions={0} | all-to-all | bytes 131072 | tf_op jit(solution)/shard_map/all_to_all | solution.py:403
  53.3 0.1 reshape.30
  53.5 0.1 copy.8
  53.6 16.0 %all_to_all.21 = f32[64,2,128]{2,1,0:T(2,128)S(1)} all-to-all(f32[64,2,128]{2,1,0:T(2,128)S(1)} %copy.8), channel_id=1, replica_groups=mesh['chip'=64,'core'=2,'bucket'=4] {'chip'}, dimensions={0} | all-to-all | bytes 131072 | tf_op jit(solution)/shard_map/all_to_all | solution.py:405
  69.6 1.2 %pick.1 = f32[3,3072]{1,0:T(4,128)} custom-call(f32[128,128]{1,0:T(8,128)S(1)} %bitcast.13, s32[2,3072]{1,0:T(2,128)S(1)} %get-tuple-element.24.code_ref), custom_call_target="tpu_custom_call" | custom-call | tf_op jit(solution)/shard_map/pick/pallas_call | solution.py:407
Async XLA Ops:
  2.8 9.7 %all-to-all-start = ((f32[16,6,128]{2,1,0:T(8,128)}), f32[16,6,128]{2,1,0:T(8,128)S(1)}, u32[]{:S(2)}, u32[]{:S(2)}) async-start(f32[16,6,128]{2,1,0:T(8,128)} %get-tuple-element.21), calls=%async_computation | async-start | bytes 131072 | tf_op jit(solution)/shard_map/all_to_all | solution.py:352
  13.2 27.9 %all-to-all-start.1 = ((f32[64,2,128]{2,1,0:T(2,128)}), f32[64,2,128]{2,1,0:T(2,128)S(1)}, u32[]{:S(2)}, u32[]{:S(2)}) async-start(f32[64,2,128]{2,1,0:T(2,128)} %bitcast.16), calls=%async_computation.1 | async-start | bytes 131072 | tf_op jit(solution)/shard_map/all_to_all | solution.py:375
  31.2 1.3 %copy-start = (bf16[2,8,256,256]{3,2,1,0:T(8,128)(2,1)}, bf16[2,8,256,256]{3,2,1,0:T(8,128)(2,1)S(1)}, u32[]{:S(2)}) copy-start(bf16[2,8,256,256]{3,2,1,0:T(8,128)(2,1)S(1)} %get-tuple-element.22.left_ref) | copy-start | bytes 6291460
  41.1 1.6 %copy-start.1 = (bf16[2,8,256,256]{3,2,1,0:T(8,128)(2,1)S(1)}, bf16[2,8,256,256]{3,2,1,0:T(8,128)(2,1)}, u32[]{:S(2)}) copy-start(bf16[2,8,256,256]{3,2,1,0:T(8,128)(2,1)} %copy-done) | copy-start | bytes 6291460

commit v9 on v7

--- a/solution.py
+++ b/solution.py
@@ -25,25 +25,53 @@
     return jnp.where(numbers == row, 1.0, 0.0).astype(BF16)
 
 
-def join_kernel(point_hbm, angle_hbm, eroded_hbm, map_hbm, node_hbm, out_hbm, near_eroded_ref, near_map_ref,
-                near_node_ref, point_ref, angle_ref, out_ref, sem):
-    part = near_node_ref.shape[0] // 3
-    pairs = [(point_hbm, point_ref), (angle_hbm, angle_ref), (eroded_hbm, near_eroded_ref), (map_hbm, near_map_ref)]
+def start_kernel(point_hbm, angle_hbm, eroded_hbm, map_hbm, node_hbm, out_hbm, node_ref, row_ref, bucket_ref, point_ref,
+                 angle_ref, eroded_ref, map_ref, out_ref, sem):
+    part = node_ref.shape[0] // 3
+    pairs = [(eroded_hbm, eroded_ref), (map_hbm, map_ref), (point_hbm, point_ref), (angle_hbm, angle_ref)]
     for i in range(3):
         at = pl.ds(i * part, part)
-        pairs.append((node_hbm.at[at, :], near_node_ref.at[at, :]))
+        pairs.append((node_hbm.at[at, :], node_ref.at[at, :]))
     copies = [pltpu.make_async_copy(source, target, sem.at[i]) for i, (source, target) in enumerate(pairs)]
     for copy in copies:
         copy.start()
-    for copy in copies[:2]:
-        copy.wait()
+
+    copies[2].wait()
+    copies[3].wait()
     for i in range(3):
         out_ref[:, i, :] = point_ref[i]
     for i in range(2):
         out_ref[:, 3 + i, :] = angle_ref[:, i, :]
     away = pltpu.make_async_copy(out_ref, out_hbm, sem.at[7])
     away.start()
-    for copy in copies[2:]:
+    blocks = map_ref.shape[0]
+    count = row_ref.shape[1]
+    rows4 = eroded_ref.shape[0]
+    span = count // rows4
+    copies[0].wait()
+
+    eroded = eroded_ref[...]
+    lane = lax.broadcasted_iota(jnp.int32, (LANES, span), 1)
+    six = 6 * lax.broadcasted_iota(jnp.int32, (LANES, span), 0)
+    spread = jnp.where((lane >= six) & (lane < six + 6), 1.0, 0.0).astype(BF16)
+    high = jnp.dot((eroded >> 3).astype(F32).astype(BF16), spread, preferred_element_type=F32)
+    low = jnp.dot((eroded & 7).astype(F32).astype(BF16), spread, preferred_element_type=F32)
+    number = lax.broadcasted_iota(jnp.int32, (rows4, span), 1)
+    faces4 = 6 * (high * 8.0 + low).astype(jnp.int32) + number % 6
+    for a in range(rows4):
+        row_ref[0:1, a * span:(a + 1) * span] = faces4[a:a + 1, :]
+    copies[1].wait()
+    buckets = map_ref[...]
+    digits = jnp.concatenate([(buckets & 1016).astype(F32), (buckets & 7).astype(F32)], axis=1).astype(BF16)
+    step = 512
+    for c in range(count // step):
+        at = slice(c * step, (c + 1) * step)
+        face = row_ref[0:1, at]
+        hot = one_hot(face & (LANES - 1), LANES)
+        value = jnp.dot(digits, jnp.concatenate([hot, hot], axis=0), preferred_element_type=F32)
+        numbers = lax.broadcasted_iota(jnp.int32, (blocks, step), 0)
+        bucket_ref[0:1, at] = jnp.sum(jnp.where(numbers == (face >> 7), value, 0.0), axis=0, keepdims=True)
+    for copy in copies[4:]:
         copy.wait()
     away.wait()
 
@@ -96,47 +124,22 @@
                 left_ref[g % 2, (g // 2) * 2 + half, term * 64:(term + 1) * 64, :] = turned[half * 64:(half + 1) * 64]
 
 
-def pack_kernel(eroded_ref, map_ref, node_ref, out_ref, code_ref, row_ref, col_ref, other_ref, rank_ref, owner_hot,
-                geo_ref):
+def pack_kernel(row_ref, bucket_ref, node_ref, out_ref, code_ref, col_ref, other_ref, rank_ref, owner_hot, geo_ref):
     group = lax.axis_index("bucket")
-    blocks = map_ref.shape[0]
     count = row_ref.shape[1]
     tiles = count // LANES
-    rows4 = eroded_ref.shape[0]
-    span = count // rows4
-
-    eroded = eroded_ref[...]
-    lane = lax.broadcasted_iota(jnp.int32, (LANES, span), 1)
-    six = 6 * lax.broadcasted_iota(jnp.int32, (LANES, span), 0)
-    spread = jnp.where((lane >= six) & (lane < six + 6), 1.0, 0.0).astype(BF16)
-    high = jnp.dot((eroded >> 3).astype(F32).astype(BF16), spread, preferred_element_type=F32)
-    low = jnp.dot((eroded & 7).astype(F32).astype(BF16), spread, preferred_element_type=F32)
-    number = lax.broadcasted_iota(jnp.int32, (rows4, span), 1)
-    faces4 = 6 * (high * 8.0 + low).astype(jnp.int32) + number % 6
-    for a in range(rows4):
-        row_ref[0:1, a * span:(a + 1) * span] = faces4[a:a + 1, :]
-
-    buckets = map_ref[...]
-    digits = jnp.concatenate([(buckets & 1016).astype(F32), (buckets & 7).astype(F32)], axis=1).astype(BF16)
-    step = 512
-    for c in range(count // step):
-        at = slice(c * step, (c + 1) * step)
-        face = row_ref[0:1, at]
-        hot = one_hot(face & (LANES - 1), LANES)
-        value = jnp.dot(digits, jnp.concatenate([hot, hot], axis=0), preferred_element_type=F32)
-        numbers = lax.broadcasted_iota(jnp.int32, (blocks, step), 0)
-        rank_ref[0:1, at] = jnp.sum(jnp.where(numbers == (face >> 7), value, 0.0), axis=0, keepdims=True)
+    blocks = geo_ref.shape[0] // 9
 
     earlier = (lax.broadcasted_iota(jnp.int32, (LANES, LANES), 0)
                < lax.broadcasted_iota(jnp.int32, (LANES, LANES), 1))
     counts, picks = [], []
     for t in range(tiles):
         at = slice(t * LANES, (t + 1) * LANES)
-        mine = rank_ref[0:1, at]
+        mine = bucket_ref[0:1, at]
         other = jnp.broadcast_to(mine, (LANES, LANES)).T
         other_ref[at, :] = other
         hit = jnp.where((other == mine) & earlier, 1.0, 0.0)
-        rank_ref[1:2, at] = jnp.sum(hit, axis=0, keepdims=True)
+        rank_ref[0:1, at] = jnp.sum(hit, axis=0, keepdims=True)
         bucket = mine.astype(jnp.int32)
         hot = one_hot(bucket >> 3, LANES)
         owner_hot[:, at] = hot
@@ -149,10 +152,10 @@
         if t:
             before = before + counts[t - 1]
             seen = jnp.dot(before.astype(BF16), owner_hot[:, at], preferred_element_type=F32)
-            rank_ref[1:2, at] += jnp.sum(jnp.where(picks[t], seen, 0.0), axis=0, keepdims=True)
-
-    bucket = rank_ref[0:1, :].astype(jnp.int32)
-    rank = rank_ref[1:2, :].astype(jnp.int32)
+            rank_ref[0:1, at] += jnp.sum(jnp.where(picks[t], seen, 0.0), axis=0, keepdims=True)
+
+    bucket = bucket_ref[0:1, :].astype(jnp.int32)
+    rank = rank_ref[0:1, :].astype(jnp.int32)
     owner = bucket >> 3
     inner = bucket & 7
     code_ref[0:1, :] = (owner & (LANES - 2)) + (inner & 1)
@@ -304,44 +307,43 @@
     anywhere = pl.BlockSpec(memory_space=pl.ANY)
 
     node_tiles = node_data.reshape(3, 8, blocks, LANES).transpose(0, 2, 1, 3).reshape(24 * blocks, LANES)
-    segs, near_eroded, near_map, near_node = pl.pallas_call(
-        join_kernel,
+    buckets, width = seg_point.shape[0], seg_point.shape[2]
+    segs, node, row, bucket = pl.pallas_call(
+        start_kernel,
         out_shape=(
-            jax.ShapeDtypeStruct((seg_point.shape[0], 5, seg_point.shape[2]), F32),
-            pltpu.VMEM((uncovered // 6 // LANES, LANES), jnp.int32),
-            pltpu.VMEM((blocks, LANES), jnp.int32),
+            jax.ShapeDtypeStruct((buckets, 5, width), F32),
             pltpu.VMEM((24 * blocks, LANES), F32),
+            pltpu.VMEM((1, uncovered), jnp.int32),
+            pltpu.VMEM((1, uncovered), F32),
         ),
         in_specs=[anywhere] * 5,
         out_specs=(anywhere, vmem, vmem, vmem),
         scratch_shapes=[
-            pltpu.VMEM((3, seg_point.shape[0], seg_point.shape[2]), F32),
+            pltpu.VMEM((3, buckets, width), F32),
             pltpu.VMEM(seg_angle.shape, F32),
-            pltpu.VMEM((seg_point.shape[0], 5, seg_point.shape[2]), F32),
+            pltpu.VMEM((uncovered // 6 // LANES, LANES), jnp.int32),
+            pltpu.VMEM((blocks, LANES), jnp.int32),
+            pltpu.VMEM((buckets, 5, width), F32),
             pltpu.SemaphoreType.DMA((8,)),
         ],
-        name="join",
+        name="start",
     )(seg_point.transpose(1, 0, 2), seg_angle, eroded.reshape(-1, LANES), bucket_map.reshape(blocks, LANES), node_tiles)
     segs = lax.all_to_all(segs, "bucket", 0, 0, tiled=True)
 
     packed, code = pl.pallas_call(
         pack_kernel,
-        out_shape=(
-            pltpu.VMEM((owners, LANES), F32),
-            pltpu.VMEM((2, uncovered), jnp.int32),
-        ),
-        in_specs=[vmem, vmem, vmem],
+        out_shape=(jax.ShapeDtypeStruct((owners, LANES), F32), pltpu.VMEM((2, uncovered), jnp.int32)),
+        in_specs=[vmem] * 3,
         out_specs=(vmem, vmem),
         scratch_shapes=[
-            pltpu.VMEM((1, uncovered), jnp.int32),
-            pltpu.VMEM((LANES, LANES), F32),
+            pltpu.VMEM((LANES, owners), F32),
             pltpu.VMEM((uncovered, LANES), F32),
-            pltpu.VMEM((2, uncovered), F32),
+            pltpu.VMEM((1, uncovered), F32),
             pltpu.VMEM((LANES, uncovered), BF16),
             pltpu.VMEM((9 * blocks, 2 * LANES), BF16),
         ],
         name="pack",
-    )(near(near_eroded), near(near_map), near(near_node))
+    )(near(row), near(bucket), near(node))
 
     with jax.named_scope("dispatch"):
         arrived = lax.all_to_all(packed.reshape(owners, 1, LANES), ("chip", "core"), 0, 0, tiled=True)

time: 68.3 us -> 67.8 us (level)
  waiting for transfers between devices: 11.2 us -> 11.9 us
  blocking collectives: 23.5 us -> 22.8 us
    all_to_all x1, waiting for transfers between devices: 0.43 us -> 1.17 us  [local(): segs = lax.all_to_all(segs, 'bucket', 0, 0, tiled=True)]
  transfers between devices with their start and end apart: 2 -> 2, of which waited for: 2 -> 2; matrix products, arithmetic and copies ran while one was open for 0% -> 0% of each run, Pallas kernels for 7% -> 6%
where the time goes in v9:
time: 67.8 us; the launch traced here: 67.6 us
  starting transfers between devices  23.9 us (35%)
  blocking collectives  22.8 us (34%)
  waiting for transfers between devices  11.9 us (18%)
  Pallas kernels  8.7 us (13%)
    all_to_all x1, starting transfers between devices, local(): lax.all_to_all(packed.reshape(owners, 1, LANES), ('chip', 'core'), 0, 0,...  19 us
    all_to_all x1, blocking collectives, local(): returned = lax.all_to_all(outgoing, 'chip', 0, 0, tiled=True)  14.9 us
    all_to_all x1, waiting for transfers between devices, local(): lax.all_to_all(packed.reshape(owners, 1, LANES), ('chip', 'core'), 0, 0,...  10.8 us
    all_to_all x1, blocking collectives, local(): shared = lax.all_to_all(force, ('core', 'bucket'), 0, 0, tiled=True)  7.92 us
    all_to_all x1, starting transfers between devices, local(): segs = lax.all_to_all(segs, 'bucket', 0, 0, tiled=True)  4.84 us
    pallas_call x1, Pallas kernels, local(): pl.pallas_call(pack_kernel, out_shape=(jax.ShapeDtypeStruct((owners, LANE...  3.13 us
    pallas_call x1, Pallas kernels, local(): pl.pallas_call(force_kernel, out_shape=pltpu.VMEM((2 * groups, 16, LANES)...  2.06 us
    pallas_call x1, Pallas kernels, local(): pl.pallas_call(start_kernel, out_shape=(jax.ShapeDtypeStruct((buckets, 5,...  1.61 us
  transfers between devices with their start and end apart: 2, of which 2 were waited for; matrix products, arithmetic and copies ran while one was open for 0% of the time, Pallas kernels for 6%

profile of v9, /device:TPU:1, one launch (start us, length us, event | category | flops | bytes accessed | tf_op | source)
XLA Modules:
  0.0 67.6 jit_solution(17341326623091951657)
XLA Ops:
  0.0 1.6 %start.1 = (f32[8,5,128]{2,1,0:T(8,128)}, f32[2304,128]{1,0:T(8,128)S(1)}, s32[1,3072]{1,0:T(1,128)S(1)}, f32[1,3072]{1,0:T(1,128)S(1)}) custom-call(f32[3,8,128]{2,1,0:T(8,128)} %bitcast.20, f32[8,2,128]{2,1,0:T(2,128)} %angle_hbm.1, s32[4,128]{1,0:T(4,128)} %bitcast.21, s32[96,128]{1,0:T(8,128)} %bitcast.19, f32[2304,128]{1,0:T(8,128)} %bitcast.16), custom_call_target="tpu_custom_call" | custom-call | tf_op jit(solution)/shard_map/start/pallas_call | solution.py:311
  1.6 4.8 %all-to-all-start.1 = ((f32[8,5,128]{2,1,0:T(8,128)}), f32[8,5,128]{2,1,0:T(8,128)S(1)}, u32[]{:S(2)}, u32[]{:S(2)}) async-start(f32[8,5,128]{2,1,0:T(8,128)} %get-tuple-element.17), calls=%async_computation.1 | async-start | bytes 65536 | tf_op jit(solution)/shard_map/all_to_all | solution.py:331
  6.5 3.1 %pack.1 = (f32[128,128]{1,0:T(8,128)}, s32[2,3072]{1,0:T(2,128)S(1)}) custom-call(s32[1,3072]{1,0:T(1,128)S(1)} %get-tuple-element.13.row_ref, f32[1,3072]{1,0:T(1,128)S(1)} %get-tuple-element.14.bucket_ref, f32[2304,128]{1,0:T(8,128)S(1)} %get-tuple-element.15.node_ref), custom_call_target="tpu_custom_call" | custom-call | tf_op jit(solution)/shard_map/pack/pallas_call | solution.py:333
  9.6 1.2 %all-to-all-done.1.seg_ref = f32[8,5,128]{2,1,0:T(8,128)S(1)} async-done(((f32[8,5,128]{2,1,0:T(8,128)}), f32[8,5,128]{2,1,0:T(8,128)S(1)}, u32[]{:S(2)}, u32[]{:S(2)}) %all-to-all-start.1) | async-done | bytes 20512 | tf_op jit(solution)/shard_map/all_to_all | solution.py:331
  10.8 19.0 %all-to-all-start = ((f32[128,1,128]{2,1,0:T(1,128)}), f32[128,1,128]{2,1,0:T(1,128)S(1)}, u32[]{:S(2)}, u32[]{:S(2)}) async-start(f32[128,1,128]{2,1,0:T(1,128)} %bitcast.18), calls=%async_computation | async-start | bytes 131072 | tf_op jit(solution)/shard_map/dispatch/all_to_all | solution.py:349
  29.8 0.7 %coefficients.1 = (bf16[2,8,256,128]{3,2,1,0:T(8,128)(2,1)S(1)}, f32[8,8,128]{2,1,0:T(8,128)S(1)}) custom-call(f32[8,5,128]{2,1,0:T(8,128)S(1)} %all-to-all-done.1.seg_ref), custom_call_target="tpu_custom_call" | custom-call | tf_op jit(solution)/shard_map/coefficients/coefficients/pallas_call | solution.py:352
  30.5 10.8 %all-to-all-done = f32[128,1,128]{2,1,0:T(1,128)S(1)} async-done(((f32[128,1,128]{2,1,0:T(1,128)}), f32[128,1,128]{2,1,0:T(1,128)S(1)}, u32[]{:S(2)}, u32[]{:S(2)}) %all-to-all-start) | async-done | bytes 65568 | tf_op jit(solution)/shard_map/dispatch/all_to_all | solution.py:349
  41.3 2.1 %force.1 = f32[8,16,128]{2,1,0:T(8,128)S(1)} custom-call(f32[128,128]{1,0:T(8,128)S(1)} %bitcast.14, bf16[2,8,256,128]{3,2,1,0:T(8,128)(2,1)S(1)} %get-tuple-element.18.left_ref, f32[8,8,128]{2,1,0:T(8,128)S(1)} %get-tuple-element.19.seg_ref), custom_call_target="tpu_custom_call" | custom-call | tf_op jit(solution)/shard_map/force/pallas_call | solution.py:364
  43.3 7.9 %all_to_all.20 = f32[8,16,128]{2,1,0:T(8,128)S(1)} all-to-all(f32[8,16,128]{2,1,0:T(8,128)S(1)} %force.1), channel_id=1, replica_groups=mesh['chip'=64,'core'=2,'bucket'=4] {'core','bucket'}, dimensions={0} | all-to-all | bytes 131072 | tf_op jit(solution)/shard_map/all_to_all | solution.py:377
  51.2 0.1 reshape.30
  51.4 0.1 copy.9
  51.5 14.9 %all_to_all.21 = f32[64,2,128]{2,1,0:T(2,128)S(1)} all-to-all(f32[64,2,128]{2,1,0:T(2,128)S(1)} %copy.9), channel_id=1, replica_groups=mesh['chip'=64,'core'=2,'bucket'=4] {'chip'}, dimensions={0} | all-to-all | bytes 131072 | tf_op jit(solution)/shard_map/all_to_all | solution.py:379
  66.4 1.2 %pick.1 = f32[3,3072]{1,0:T(4,128)} custom-call(f32[128,128]{1,0:T(8,128)S(1)} %bitcast.15, s32[2,3072]{1,0:T(2,128)S(1)} %get-tuple-element.20.code_ref), custom_call_target="tpu_custom_call" | custom-call | tf_op jit(solution)/shard_map/pick/pallas_call | solution.py:381
Async XLA Ops:
  1.6 9.1 %all-to-all-start.1 = ((f32[8,5,128]{2,1,0:T(8,128)}), f32[8,5,128]{2,1,0:T(8,128)S(1)}, u32[]{:S(2)}, u32[]{:S(2)}) async-start(f32[8,5,128]{2,1,0:T(8,128)} %get-tuple-element.17), calls=%async_computation.1 | async-start | bytes 65536 | tf_op jit(solution)/shard_map/all_to_all | solution.py:331
  10.8 30.5 %all-to-all-start = ((f32[128,1,128]{2,1,0:T(1,128)}), f32[128,1,128]{2,1,0:T(1,128)S(1)}, u32[]{:S(2)}, u32[]{:S(2)}) async-start(f32[128,1,128]{2,1,0:T(1,128)} %bitcast.18), calls=%async_computation | async-start | bytes 131072 | tf_op jit(solution)/shard_map/dispatch/all_to_all | solution.py:349

commit v10 on v9

--- a/solution.py
+++ b/solution.py
@@ -223,12 +223,6 @@
 def force_kernel(face_ref, left_ref, seg_ref, out_ref, row_ref, right_ref, wide_ref):
     half = LANES // 2
     row_ref[...] = jnp.concatenate([face_ref[pl.ds(core, half, stride=2), :] for core in range(2)], axis=0).T
-    groups = seg_ref.shape[0] // 2
-    for g in range(2 * groups):
-        columns = seg_ref[g].T
-        for i in range(3):
-            wide_ref[g % 2, i, (g // 2) * LANES:(g // 2 + 1) * LANES, :] = jnp.broadcast_to(
-                columns[:, i:i + 1], (LANES, LANES))
     half_log2e = 0.5 * 1.4426950408889634
     number = lax.broadcasted_iota(jnp.int32, (16, LANES), 0)
     for par in range(2):
@@ -255,6 +249,11 @@
             right = right_ref[par, :, first * LANES:(first + width) * LANES]
             total = [[jnp.zeros((8, LANES), F32) for i in range(3)] for k in range(width)]
             for chunk in range(chunks):
+                if first == 0 and chunk % 2 == 0:
+                    columns = seg_ref[chunk + par].T
+                    for i in range(3):
+                        wide_ref[par, i, chunk * 64:chunk * 64 + LANES, :] = jnp.broadcast_to(
+                            columns[:, i:i + 1], (LANES, LANES))
                 found = jnp.dot(left_ref[par, chunk], right, preferred_element_type=F32)
                 normal = [wide_ref[par, i, chunk * 64:(chunk + 1) * 64, :] for i in range(3)]
                 for k in range(width):

time: 67.8 us -> 67.8 us (level)
  no operation moved by 1% of the time
where the time goes in v10:
time: 67.8 us; the launch traced here: 67.5 us
  starting transfers between devices  23.9 us (35%)
  blocking collectives  22.8 us (34%)
  waiting for transfers between devices  11.9 us (18%)
  Pallas kernels  8.66 us (13%)
    all_to_all x1, starting transfers between devices, local(): lax.all_to_all(packed.reshape(owners, 1, LANES), ('chip', 'core'), 0, 0,...  19 us
    all_to_all x1, blocking collectives, local(): returned = lax.all_to_all(outgoing, 'chip', 0, 0, tiled=True)  14.9 us
    all_to_all x1, waiting for transfers between devices, local(): lax.all_to_all(packed.reshape(owners, 1, LANES), ('chip', 'core'), 0, 0,...  10.8 us
    all_to_all x1, blocking collectives, local(): shared = lax.all_to_all(force, ('core', 'bucket'), 0, 0, tiled=True)  7.92 us
    all_to_all x1, starting transfers between devices, local(): segs = lax.all_to_all(segs, 'bucket', 0, 0, tiled=True)  4.84 us
    pallas_call x1, Pallas kernels, local(): pl.pallas_call(pack_kernel, out_shape=(jax.ShapeDtypeStruct((owners, LANE...  3.13 us
    pallas_call x1, Pallas kernels, local(): pl.pallas_call(force_kernel, out_shape=pltpu.VMEM((2 * groups, 16, LANES)...  2.01 us
    pallas_call x1, Pallas kernels, local(): pl.pallas_call(start_kernel, out_shape=(jax.ShapeDtypeStruct((buckets, 5,...  1.61 us
  transfers between devices with their start and end apart: 2, of which 2 were waited for; matrix products, arithmetic and copies ran while one was open for 0% of the time, Pallas kernels for 6%

profile of v10, /device:TPU:1, one launch (start us, length us, event | category | flops | bytes accessed | tf_op | source)
XLA Modules:
  0.0 67.5 jit_solution(4093948545809138290)
XLA Ops:
  0.0 1.6 %start.1 = (f32[8,5,128]{2,1,0:T(8,128)}, f32[2304,128]{1,0:T(8,128)S(1)}, s32[1,3072]{1,0:T(1,128)S(1)}, f32[1,3072]{1,0:T(1,128)S(1)}) custom-call(f32[3,8,128]{2,1,0:T(8,128)} %bitcast.20, f32[8,2,128]{2,1,0:T(2,128)} %angle_hbm.1, s32[4,128]{1,0:T(4,128)} %bitcast.21, s32[96,128]{1,0:T(8,128)} %bitcast.19, f32[2304,128]{1,0:T(8,128)} %bitcast.16), custom_call_target="tpu_custom_call" | custom-call | tf_op jit(solution)/shard_map/start/pallas_call | solution.py:310
  1.6 4.8 %all-to-all-start.1 = ((f32[8,5,128]{2,1,0:T(8,128)}), f32[8,5,128]{2,1,0:T(8,128)S(1)}, u32[]{:S(2)}, u32[]{:S(2)}) async-start(f32[8,5,128]{2,1,0:T(8,128)} %get-tuple-element.17), calls=%async_computation.1 | async-start | bytes 65536 | tf_op jit(solution)/shard_map/all_to_all | solution.py:330
  6.5 3.1 %pack.1 = (f32[128,128]{1,0:T(8,128)}, s32[2,3072]{1,0:T(2,128)S(1)}) custom-call(s32[1,3072]{1,0:T(1,128)S(1)} %get-tuple-element.13.row_ref, f32[1,3072]{1,0:T(1,128)S(1)} %get-tuple-element.14.bucket_ref, f32[2304,128]{1,0:T(8,128)S(1)} %get-tuple-element.15.node_ref), custom_call_target="tpu_custom_call" | custom-call | tf_op jit(solution)/shard_map/pack/pallas_call | solution.py:332
  9.6 1.2 %all-to-all-done.1.seg_ref = f32[8,5,128]{2,1,0:T(8,128)S(1)} async-done(((f32[8,5,128]{2,1,0:T(8,128)}), f32[8,5,128]{2,1,0:T(8,128)S(1)}, u32[]{:S(2)}, u32[]{:S(2)}) %all-to-all-start.1) | async-done | bytes 20512 | tf_op jit(solution)/shard_map/all_to_all | solution.py:330
  10.8 19.0 %all-to-all-start = ((f32[128,1,128]{2,1,0:T(1,128)}), f32[128,1,128]{2,1,0:T(1,128)S(1)}, u32[]{:S(2)}, u32[]{:S(2)}) async-start(f32[128,1,128]{2,1,0:T(1,128)} %bitcast.18), calls=%async_computation | async-start | bytes 131072 | tf_op jit(solution)/shard_map/dispatch/all_to_all | solution.py:348
  29.8 0.7 %coefficients.1 = (bf16[2,8,256,128]{3,2,1,0:T(8,128)(2,1)S(1)}, f32[8,8,128]{2,1,0:T(8,128)S(1)}) custom-call(f32[8,5,128]{2,1,0:T(8,128)S(1)} %all-to-all-done.1.seg_ref), custom_call_target="tpu_custom_call" | custom-call | tf_op jit(solution)/shard_map/coefficients/coefficients/pallas_call | solution.py:351
  30.5 10.8 %all-to-all-done = f32[128,1,128]{2,1,0:T(1,128)S(1)} async-done(((f32[128,1,128]{2,1,0:T(1,128)}), f32[128,1,128]{2,1,0:T(1,128)S(1)}, u32[]{:S(2)}, u32[]{:S(2)}) %all-to-all-start) | async-done | bytes 65568 | tf_op jit(solution)/shard_map/dispatch/all_to_all | solution.py:348
  41.3 2.0 %force.1 = f32[8,16,128]{2,1,0:T(8,128)S(1)} custom-call(f32[128,128]{1,0:T(8,128)S(1)} %bitcast.14, bf16[2,8,256,128]{3,2,1,0:T(8,128)(2,1)S(1)} %get-tuple-element.18.left_ref, f32[8,8,128]{2,1,0:T(8,128)S(1)} %get-tuple-element.19.seg_ref), custom_call_target="tpu_custom_call" | custom-call | tf_op jit(solution)/shard_map/force/pallas_call | solution.py:363
  43.3 7.9 %all_to_all.20 = f32[8,16,128]{2,1,0:T(8,128)S(1)} all-to-all(f32[8,16,128]{2,1,0:T(8,128)S(1)} %force.1), channel_id=1, replica_groups=mesh['chip'=64,'core'=2,'bucket'=4] {'core','bucket'}, dimensions={0} | all-to-all | bytes 131072 | tf_op jit(solution)/shard_map/all_to_all | solution.py:376
  51.2 0.1 reshape.30
  51.3 0.1 copy.9
  51.4 14.9 %all_to_all.21 = f32[64,2,128]{2,1,0:T(2,128)S(1)} all-to-all(f32[64,2,128]{2,1,0:T(2,128)S(1)} %copy.9), channel_id=1, replica_groups=mesh['chip'=64,'core'=2,'bucket'=4] {'chip'}, dimensions={0} | all-to-all | bytes 131072 | tf_op jit(solution)/shard_map/all_to_all | solution.py:378
  66.3 1.2 %pick.1 = f32[3,3072]{1,0:T(4,128)} custom-call(f32[128,128]{1,0:T(8,128)S(1)} %bitcast.15, s32[2,3072]{1,0:T(2,128)S(1)} %get-tuple-element.20.code_ref), custom_call_target="tpu_custom_call" | custom-call | tf_op jit(solution)/shard_map/pick/pallas_call | solution.py:380
Async XLA Ops:
  1.6 9.1 %all-to-all-start.1 = ((f32[8,5,128]{2,1,0:T(8,128)}), f32[8,5,128]{2,1,0:T(8,128)S(1)}, u32[]{:S(2)}, u32[]{:S(2)}) async-start(f32[8,5,128]{2,1,0:T(8,128)} %get-tuple-element.17), calls=%async_computation.1 | async-start | bytes 65536 | tf_op jit(solution)/shard_map/all_to_all | solution.py:330
  10.8 30.5 %all-to-all-start = ((f32[128,1,128]{2,1,0:T(1,128)}), f32[128,1,128]{2,1,0:T(1,128)S(1)}, u32[]{:S(2)}, u32[]{:S(2)}) async-start(f32[128,1,128]{2,1,0:T(1,128)} %bitcast.18), calls=%async_computation | async-start | bytes 131072 | tf_op jit(solution)/shard_map/dispatch/all_to_all | solution.py:348

commit v11 on v9

--- a/solution.py
+++ b/solution.py
@@ -332,7 +332,7 @@
 
     packed, code = pl.pallas_call(
         pack_kernel,
-        out_shape=(jax.ShapeDtypeStruct((owners, LANES), F32), pltpu.VMEM((2, uncovered), jnp.int32)),
+        out_shape=(pltpu.VMEM((owners, LANES), F32), pltpu.VMEM((2, uncovered), jnp.int32)),
         in_specs=[vmem] * 3,
         out_specs=(vmem, vmem),
         scratch_shapes=[
@@ -344,9 +344,6 @@
         ],
         name="pack",
     )(near(row), near(bucket), near(node))
-
-    with jax.named_scope("dispatch"):
-        arrived = lax.all_to_all(packed.reshape(owners, 1, LANES), ("chip", "core"), 0, 0, tiled=True)
 
     with jax.named_scope("coefficients"):
         left, normal = pl.pallas_call(
@@ -361,6 +358,10 @@
             name="coefficients",
         )(near(segs))
 
+    packed, left, normal = lax.optimization_barrier((packed, left, normal))
+    with jax.named_scope("dispatch"):
+        arrived = lax.all_to_all(packed.reshape(owners, 1, LANES), ("chip", "core"), 0, 0, tiled=True)
+
     force = pl.pallas_call(
         force_kernel,
         out_shape=pltpu.VMEM((2 * groups, 16, LANES), F32),

time: 67.8 us -> 68.3 us (level)
  blocking collectives: 22.8 us -> 53.1 us
  starting transfers between devices: 23.9 us -> 4.84 us
  waiting for transfers between devices: 11.9 us -> 1.8 us
    all_to_all x0 -> x1, blocking collectives: none -> 30.3 us  [local(): lax.all_to_all(packed.reshape(owners, 1, LANES), ('chip', 'core'), 0, 0,...]
    all_to_all x1 -> x0, starting transfers between devices: 19 us -> none  [local(): lax.all_to_all(packed.reshape(owners, 1, LANES), ('chip', 'core'), 0, 0,...]
    all_to_all x1 -> x0, waiting for transfers between devices: 10.8 us -> none  [local(): lax.all_to_all(packed.reshape(owners, 1, LANES), ('chip', 'core'), 0, 0,...]
  transfers between devices with their start and end apart: 2 -> 1, of which waited for: 2 -> 1; matrix products, arithmetic and copies ran while one was open for 0% -> 0% of each run, Pallas kernels for 6% -> 4%
where the time goes in v11:
time: 68.3 us; the launch traced here: 68.1 us
  blocking collectives  53.1 us (78%)
  Pallas kernels  8.06 us (12%)
  starting transfers between devices  4.84 us (7%)
  waiting for transfers between devices  1.8 us (3%)
    all_to_all x1, blocking collectives, local(): lax.all_to_all(packed.reshape(owners, 1, LANES), ('chip', 'core'), 0, 0,...  30.3 us
    all_to_all x1, blocking collectives, local(): returned = lax.all_to_all(outgoing, 'chip', 0, 0, tiled=True)  14.9 us
    all_to_all x1, blocking collectives, local(): shared = lax.all_to_all(force, ('core', 'bucket'), 0, 0, tiled=True)  7.89 us
    all_to_all x1, starting transfers between devices, local(): segs = lax.all_to_all(segs, 'bucket', 0, 0, tiled=True)  4.84 us
    pallas_call x1, Pallas kernels, local(): pl.pallas_call(pack_kernel, out_shape=(pltpu.VMEM((owners, LANES), F32),...  2.49 us
    pallas_call x1, Pallas kernels, local(): pl.pallas_call(force_kernel, out_shape=pltpu.VMEM((2 * groups, 16, LANES)...  2.06 us
    all_to_all x1, waiting for transfers between devices, local(): segs = lax.all_to_all(segs, 'bucket', 0, 0, tiled=True)  1.8 us
    pallas_call x1, Pallas kernels, local(): pl.pallas_call(start_kernel, out_shape=(jax.ShapeDtypeStruct((buckets, 5,...  1.61 us
  transfers between devices with their start and end apart: 1, of which 1 were waited for; matrix products, arithmetic and copies ran while one was open for 0% of the time, Pallas kernels for 4%

profile of v11, /device:TPU:1, one launch (start us, length us, event | category | flops | bytes accessed | tf_op | source)
XLA Modules:
  0.0 68.1 jit_solution(16290282058162353644)
XLA Ops:
  0.0 1.6 %start.1 = (f32[8,5,128]{2,1,0:T(8,128)}, f32[2304,128]{1,0:T(8,128)S(1)}, s32[1,3072]{1,0:T(1,128)S(1)}, f32[1,3072]{1,0:T(1,128)S(1)}) custom-call(f32[3,8,128]{2,1,0:T(8,128)} %bitcast.20, f32[8,2,128]{2,1,0:T(2,128)} %angle_hbm.1, s32[4,128]{1,0:T(4,128)} %bitcast.21, s32[96,128]{1,0:T(8,128)} %bitcast.19, f32[2304,128]{1,0:T(8,128)} %bitcast.17), custom_call_target="tpu_custom_call" | custom-call | tf_op jit(solution)/shard_map/start/pallas_call | solution.py:311
  1.6 4.8 %all-to-all-start = ((f32[8,5,128]{2,1,0:T(8,128)}), f32[8,5,128]{2,1,0:T(8,128)S(1)}, u32[]{:S(2)}, u32[]{:S(2)}) async-start(f32[8,5,128]{2,1,0:T(8,128)} %get-tuple-element.20), calls=%async_computation | async-start | bytes 65536 | tf_op jit(solution)/shard_map/all_to_all | solution.py:331
  6.5 2.5 %pack.1 = (f32[128,128]{1,0:T(8,128)S(1)}, s32[2,3072]{1,0:T(2,128)S(1)}) custom-call(s32[1,3072]{1,0:T(1,128)S(1)} %get-tuple-element.16.row_ref, f32[1,3072]{1,0:T(1,128)S(1)} %get-tuple-element.17.bucket_ref, f32[2304,128]{1,0:T(8,128)S(1)} %get-tuple-element.18.node_ref), custom_call_target="tpu_custom_call" | custom-call | tf_op jit(solution)/shard_map/pack/pallas_call | solution.py:333
  9.0 1.8 %all-to-all-done.seg_ref = f32[8,5,128]{2,1,0:T(8,128)S(1)} async-done(((f32[8,5,128]{2,1,0:T(8,128)}), f32[8,5,128]{2,1,0:T(8,128)S(1)}, u32[]{:S(2)}, u32[]{:S(2)}) %all-to-all-start) | async-done | bytes 20512 | tf_op jit(solution)/shard_map/all_to_all | solution.py:331
  10.8 0.7 %coefficients.1 = (bf16[2,8,256,128]{3,2,1,0:T(8,128)(2,1)S(1)}, f32[8,8,128]{2,1,0:T(8,128)S(1)}) custom-call(f32[8,5,128]{2,1,0:T(8,128)S(1)} %all-to-all-done.seg_ref), custom_call_target="tpu_custom_call" | custom-call | tf_op jit(solution)/shard_map/coefficients/coefficients/pallas_call | solution.py:349
  11.5 30.3 %all_to_all.20 = f32[128,1,128]{2,1,0:T(1,128)S(1)} all-to-all(f32[128,1,128]{2,1,0:T(1,128)S(1)} %bitcast.16), channel_id=1, replica_groups=mesh['chip'=64,'core'=2,'bucket'=4] {'chip','core'}, dimensions={0} | all-to-all | bytes 131072 | tf_op jit(solution)/shard_map/dispatch/all_to_all | solution.py:363
  41.8 2.1 %force.1 = f32[8,16,128]{2,1,0:T(8,128)S(1)} custom-call(f32[128,128]{1,0:T(8,128)S(1)} %bitcast.14, bf16[2,8,256,128]{3,2,1,0:T(8,128)(2,1)S(1)} %get-tuple-element.24.left_ref, f32[8,8,128]{2,1,0:T(8,128)S(1)} %get-tuple-element.25.seg_ref), custom_call_target="tpu_custom_call" | custom-call | tf_op jit(solution)/shard_map/force/pallas_call | solution.py:365
  43.9 7.9 %all_to_all.21 = f32[8,16,128]{2,1,0:T(8,128)S(1)} all-to-all(f32[8,16,128]{2,1,0:T(8,128)S(1)} %force.1), channel_id=1, replica_groups=mesh['chip'=64,'core'=2,'bucket'=4] {'core','bucket'}, dimensions={0} | all-to-all | bytes 131072 | tf_op jit(solution)/shard_map/all_to_all | solution.py:378
  51.7 0.1 reshape.30
  51.9 0.1 copy.9
  52.0 14.9 %all_to_all.22 = f32[64,2,128]{2,1,0:T(2,128)S(1)} all-to-all(f32[64,2,128]{2,1,0:T(2,128)S(1)} %copy.9), channel_id=1, replica_groups=mesh['chip'=64,'core'=2,'bucket'=4] {'chip'}, dimensions={0} | all-to-all | bytes 131072 | tf_op jit(solution)/shard_map/all_to_all | solution.py:380
  66.9 1.2 %pick.1 = f32[3,3072]{1,0:T(4,128)} custom-call(f32[128,128]{1,0:T(8,128)S(1)} %bitcast.15, s32[2,3072]{1,0:T(2,128)S(1)} %get-tuple-element.26.code_ref), custom_call_target="tpu_custom_call" | custom-call | tf_op jit(solution)/shard_map/pick/pallas_call | solution.py:382
Async XLA Ops:
  1.6 9.1 %all-to-all-start = ((f32[8,5,128]{2,1,0:T(8,128)}), f32[8,5,128]{2,1,0:T(8,128)S(1)}, u32[]{:S(2)}, u32[]{:S(2)}) async-start(f32[8,5,128]{2,1,0:T(8,128)} %get-tuple-element.20), calls=%async_computation | async-start | bytes 65536 | tf_op jit(solution)/shard_map/all_to_all | solution.py:331

commit v12 on v9

--- a/solution.py
+++ b/solution.py
@@ -28,7 +28,7 @@
 def start_kernel(point_hbm, angle_hbm, eroded_hbm, map_hbm, node_hbm, out_hbm, node_ref, row_ref, bucket_ref, point_ref,
                  angle_ref, eroded_ref, map_ref, out_ref, sem):
     part = node_ref.shape[0] // 3
-    pairs = [(eroded_hbm, eroded_ref), (map_hbm, map_ref), (point_hbm, point_ref), (angle_hbm, angle_ref)]
+    pairs = [(point_hbm, point_ref), (angle_hbm, angle_ref), (eroded_hbm, eroded_ref), (map_hbm, map_ref)]
     for i in range(3):
         at = pl.ds(i * part, part)
         pairs.append((node_hbm.at[at, :], node_ref.at[at, :]))
@@ -36,19 +36,19 @@
     for copy in copies:
         copy.start()
 
-    copies[2].wait()
-    copies[3].wait()
+    copies[0].wait()
+    copies[1].wait()
     for i in range(3):
         out_ref[:, i, :] = point_ref[i]
     for i in range(2):
         out_ref[:, 3 + i, :] = angle_ref[:, i, :]
     away = pltpu.make_async_copy(out_ref, out_hbm, sem.at[7])
     away.start()
+    copies[2].wait()
     blocks = map_ref.shape[0]
     count = row_ref.shape[1]
     rows4 = eroded_ref.shape[0]
     span = count // rows4
-    copies[0].wait()
 
     eroded = eroded_ref[...]
     lane = lax.broadcasted_iota(jnp.int32, (LANES, span), 1)
@@ -60,7 +60,7 @@
     faces4 = 6 * (high * 8.0 + low).astype(jnp.int32) + number % 6
     for a in range(rows4):
         row_ref[0:1, a * span:(a + 1) * span] = faces4[a:a + 1, :]
-    copies[1].wait()
+    copies[3].wait()
     buckets = map_ref[...]
     digits = jnp.concatenate([(buckets & 1016).astype(F32), (buckets & 7).astype(F32)], axis=1).astype(BF16)
     step = 512

time: 67.8 us -> 67.9 us (level)
  no operation moved by 1% of the time
where the time goes in v12:
time: 67.9 us; the launch traced here: 67.5 us
  starting transfers between devices  23.9 us (35%)
  blocking collectives  22.8 us (34%)
  waiting for transfers between devices  11.9 us (18%)
  Pallas kernels  8.66 us (13%)
    all_to_all x1, starting transfers between devices, local(): lax.all_to_all(packed.reshape(owners, 1, LANES), ('chip', 'core'), 0, 0,...  19 us
    all_to_all x1, blocking collectives, local(): returned = lax.all_to_all(outgoing, 'chip', 0, 0, tiled=True)  14.9 us
    all_to_all x1, waiting for transfers between devices, local(): lax.all_to_all(packed.reshape(owners, 1, LANES), ('chip', 'core'), 0, 0,...  10.8 us
    all_to_all x1, blocking collectives, local(): shared = lax.all_to_all(force, ('core', 'bucket'), 0, 0, tiled=True)  7.92 us
    all_to_all x1, starting transfers between devices, local(): segs = lax.all_to_all(segs, 'bucket', 0, 0, tiled=True)  4.84 us
    pallas_call x1, Pallas kernels, local(): pl.pallas_call(pack_kernel, out_shape=(jax.ShapeDtypeStruct((owners, LANE...  3.12 us
    pallas_call x1, Pallas kernels, local(): pl.pallas_call(force_kernel, out_shape=pltpu.VMEM((2 * groups, 16, LANES)...  2.05 us
    pallas_call x1, Pallas kernels, local(): pl.pallas_call(start_kernel, out_shape=(jax.ShapeDtypeStruct((buckets, 5,...  1.57 us
  transfers between devices with their start and end apart: 2, of which 2 were waited for; matrix products, arithmetic and copies ran while one was open for 0% of the time, Pallas kernels for 6%

profile of v12, /device:TPU:1, one launch (start us, length us, event | category | flops | bytes accessed | tf_op | source)
XLA Modules:
  0.0 67.5 jit_solution(18415918436645932330)
XLA Ops:
  0.0 1.6 %start.1 = (f32[8,5,128]{2,1,0:T(8,128)}, f32[2304,128]{1,0:T(8,128)S(1)}, s32[1,3072]{1,0:T(1,128)S(1)}, f32[1,3072]{1,0:T(1,128)S(1)}) custom-call(f32[3,8,128]{2,1,0:T(8,128)} %bitcast.20, f32[8,2,128]{2,1,0:T(2,128)} %angle_hbm.1, s32[4,128]{1,0:T(4,128)} %bitcast.21, s32[96,128]{1,0:T(8,128)} %bitcast.19, f32[2304,128]{1,0:T(8,128)} %bitcast.16), custom_call_target="tpu_custom_call" | custom-call | tf_op jit(solution)/shard_map/start/pallas_call | solution.py:311
  1.6 4.8 %all-to-all-start.1 = ((f32[8,5,128]{2,1,0:T(8,128)}), f32[8,5,128]{2,1,0:T(8,128)S(1)}, u32[]{:S(2)}, u32[]{:S(2)}) async-start(f32[8,5,128]{2,1,0:T(8,128)} %get-tuple-element.17), calls=%async_computation.1 | async-start | bytes 65536 | tf_op jit(solution)/shard_map/all_to_all | solution.py:331
  6.4 3.1 %pack.1 = (f32[128,128]{1,0:T(8,128)}, s32[2,3072]{1,0:T(2,128)S(1)}) custom-call(s32[1,3072]{1,0:T(1,128)S(1)} %get-tuple-element.13.row_ref, f32[1,3072]{1,0:T(1,128)S(1)} %get-tuple-element.14.bucket_ref, f32[2304,128]{1,0:T(8,128)S(1)} %get-tuple-element.15.node_ref), custom_call_target="tpu_custom_call" | custom-call | tf_op jit(solution)/shard_map/pack/pallas_call | solution.py:333
  9.5 1.2 %all-to-all-done.1.seg_ref = f32[8,5,128]{2,1,0:T(8,128)S(1)} async-done(((f32[8,5,128]{2,1,0:T(8,128)}), f32[8,5,128]{2,1,0:T(8,128)S(1)}, u32[]{:S(2)}, u32[]{:S(2)}) %all-to-all-start.1) | async-done | bytes 20512 | tf_op jit(solution)/shard_map/all_to_all | solution.py:331
  10.7 19.0 %all-to-all-start = ((f32[128,1,128]{2,1,0:T(1,128)}), f32[128,1,128]{2,1,0:T(1,128)S(1)}, u32[]{:S(2)}, u32[]{:S(2)}) async-start(f32[128,1,128]{2,1,0:T(1,128)} %bitcast.18), calls=%async_computation | async-start | bytes 131072 | tf_op jit(solution)/shard_map/dispatch/all_to_all | solution.py:349
  29.8 0.7 %coefficients.1 = (bf16[2,8,256,128]{3,2,1,0:T(8,128)(2,1)S(1)}, f32[8,8,128]{2,1,0:T(8,128)S(1)}) custom-call(f32[8,5,128]{2,1,0:T(8,128)S(1)} %all-to-all-done.1.seg_ref), custom_call_target="tpu_custom_call" | custom-call | tf_op jit(solution)/shard_map/coefficients/coefficients/pallas_call | solution.py:352
  30.5 10.8 %all-to-all-done = f32[128,1,128]{2,1,0:T(1,128)S(1)} async-done(((f32[128,1,128]{2,1,0:T(1,128)}), f32[128,1,128]{2,1,0:T(1,128)S(1)}, u32[]{:S(2)}, u32[]{:S(2)}) %all-to-all-start) | async-done | bytes 65568 | tf_op jit(solution)/shard_map/dispatch/all_to_all | solution.py:349
  41.2 2.1 %force.1 = f32[8,16,128]{2,1,0:T(8,128)S(1)} custom-call(f32[128,128]{1,0:T(8,128)S(1)} %bitcast.14, bf16[2,8,256,128]{3,2,1,0:T(8,128)(2,1)S(1)} %get-tuple-element.18.left_ref, f32[8,8,128]{2,1,0:T(8,128)S(1)} %get-tuple-element.19.seg_ref), custom_call_target="tpu_custom_call" | custom-call | tf_op jit(solution)/shard_map/force/pallas_call | solution.py:364
  43.3 7.9 %all_to_all.20 = f32[8,16,128]{2,1,0:T(8,128)S(1)} all-to-all(f32[8,16,128]{2,1,0:T(8,128)S(1)} %force.1), channel_id=1, replica_groups=mesh['chip'=64,'core'=2,'bucket'=4] {'core','bucket'}, dimensions={0} | all-to-all | bytes 131072 | tf_op jit(solution)/shard_map/all_to_all | solution.py:377
  51.2 0.1 reshape.30
  51.3 0.1 copy.9
  51.4 14.9 %all_to_all.21 = f32[64,2,128]{2,1,0:T(2,128)S(1)} all-to-all(f32[64,2,128]{2,1,0:T(2,128)S(1)} %copy.9), channel_id=1, replica_groups=mesh['chip'=64,'core'=2,'bucket'=4] {'chip'}, dimensions={0} | all-to-all | bytes 131072 | tf_op jit(solution)/shard_map/all_to_all | solution.py:379
  66.3 1.2 %pick.1 = f32[3,3072]{1,0:T(4,128)} custom-call(f32[128,128]{1,0:T(8,128)S(1)} %bitcast.15, s32[2,3072]{1,0:T(2,128)S(1)} %get-tuple-element.20.code_ref), custom_call_target="tpu_custom_call" | custom-call | tf_op jit(solution)/shard_map/pick/pallas_call | solution.py:381
Async XLA Ops:
  1.6 9.1 %all-to-all-start.1 = ((f32[8,5,128]{2,1,0:T(8,128)}), f32[8,5,128]{2,1,0:T(8,128)S(1)}, u32[]{:S(2)}, u32[]{:S(2)}) async-start(f32[8,5,128]{2,1,0:T(8,128)} %get-tuple-element.17), calls=%async_computation.1 | async-start | bytes 65536 | tf_op jit(solution)/shard_map/all_to_all | solution.py:331
  10.7 30.5 %all-to-all-start = ((f32[128,1,128]{2,1,0:T(1,128)}), f32[128,1,128]{2,1,0:T(1,128)S(1)}, u32[]{:S(2)}, u32[]{:S(2)}) async-start(f32[128,1,128]{2,1,0:T(1,128)} %bitcast.18), calls=%async_computation | async-start | bytes 131072 | tf_op jit(solution)/shard_map/dispatch/all_to_all | solution.py:349
